TPU v7x, 512 devices: a 8x2x16 block of a 8x8x16 slice. The times are simulated.
512 devices in a mesh: job: 2 (over y), chain: 16 (over z), pair: 8 (over x), pno: 2 (over core).
Axes of the slice: x: 8, y: 2, z: 16, core: 2. Of those that a mesh axis runs over, the one named last changes fastest.
The devices are a block of a 8x8x16 slice.
Arguments:
- amplitudes: bfloat16 [1536, 128, 128], P(('job', 'chain', 'pair'), 'pno'), parts along dimension 0, may hold values from -4 to 4
- integrals: bfloat16 [1536, 128, 128], P(('job', 'chain', 'pair'), 'pno'), parts along dimension 0, may hold values from -6 to 6
- intersections: bfloat16 [1536, 32, 128, 128], P(('job', 'chain', 'pair')), parts along dimension 0, may hold values from -0.5 to 0.5
- coupling: float32 [1536, 32], P(('job', 'chain', 'pair')), parts along dimension 0, may hold values from -4 to 4
- pno_energies: float32 [1536, 128], P(('job', 'chain', 'pair')), parts along dimension 0, may hold values from 0.3 to 3
- pair_shift: float32 [1536], P(('job', 'chain', 'pair')), parts along dimension 0, may hold values from -1.5 to -0.3
- ranks: int32 [1536], P(('job', 'chain', 'pair')), parts along dimension 0, may hold values from 24 to 128
- neighbours: int32 [1536, 32], P(('job', 'chain', 'pair')), parts along dimension 0, may hold values from 0 to 767, as said below
Outputs:
- final_amplitudes: bfloat16 [1536, 128, 128], P(('job', 'chain', 'pair'), 'pno'), parts along dimension 0
- residual_norms: float32 [6], P('job'), parts along dimension 0
There are 2 independent parts, one for each index of `job`. A program takes and returns all parts, laid end to end along the dimension named above; each array names one. Nothing has to cross between parts.
Inputs may be any that keep to these rules, and one draw needn't show every extreme that they name: `neighbours`: every coupled pair of pair g lies in the fragment of g (pairs k * 48 to (k + 1) * 48 - 1 for k = g // 48) or in one of the two fragments beside it.
All inputs are finite; a program needn't handle non-finite values.
Results may differ from a plain program's by a relative error of at most 0.015.
Values may be sent and summed in bfloat16 or wider, within the bound.
No kernel may reach another device: no remote copies, remote signals or barrier semaphores. Data moves between devices by JAX's collectives and lax.ppermute only.
A program may use at most 64 MiB of HBM per device.

v0:
```python
import jax
import jax.numpy as jnp
from jax import lax
from jax.sharding import PartitionSpec as P

ITERS = 3


def laid_out(tiles, dim):
    tiles = jnp.moveaxis(tiles, 0, dim)
    shape = tiles.shape
    return tiles.reshape(*shape[:dim], shape[dim] * shape[dim + 1], *shape[dim + 2 :])


def copy_for_each(value, axis):
    copies = jnp.broadcast_to(value, (lax.axis_size(axis), *value.shape))
    return lax.all_to_all(copies, axis, split_axis=0, concat_axis=0, tiled=True)


def gathered_copies(value, axis, dim):
    return laid_out(copy_for_each(value, axis), dim)


def padded(cells, sides, width):
    for axis, dim in sides:
        count = lax.axis_size(axis)
        ends = count - 1
        head = lax.slice_in_dim(cells, 0, width, axis=dim)
        tail = lax.slice_in_dim(cells, cells.shape[dim] - width, cells.shape[dim], axis=dim)
        cells = jnp.concatenate(
            [
                lax.ppermute(tail, axis, [(i, (i + 1) % count) for i in range(ends)]),
                cells,
                lax.ppermute(head, axis, [((i + 1) % count, i) for i in range(ends)]),
            ],
            axis=dim,
        )
    return cells


def over_axes(value, axes):
    for axis in axes:
        value = lax.psum(value, axis)
    return value


def spread_amps(piece):
    whole_rows = gathered_copies(piece, "pno", 1)
    beside = padded(whole_rows, (("chain", 0),), whole_rows.shape[0])
    return lax.all_gather(beside, "pair", axis=0, tiled=True)


def per_device(
    amplitudes, integrals, intersections, coupling, pno_energies, pair_shift, ranks, neighbours
):
    count = amplitudes.shape[0]
    half = amplitudes.shape[1]
    width = amplitudes.shape[2]
    chain_pos = lax.axis_index("chain")
    first_row = lax.axis_index("pno") * half
    frag = count * lax.axis_size("pair")
    cells = frag * lax.axis_size("chain") * width * width
    columns = jnp.arange(width, dtype=jnp.int32)
    rows_here = first_row + jnp.arange(half, dtype=jnp.int32)
    live_cols = columns[None, :] < ranks[:, None]
    live_rows = rows_here[None, :] < ranks[:, None]
    mask = (live_rows[:, :, None] & live_cols[:, None, :]).astype(jnp.float32)
    energy_rows = lax.dynamic_slice_in_dim(pno_energies, first_row, half, 1)
    denom = energy_rows[:, :, None] + pno_energies[:, None, :] - pair_shift[:, None, None]
    over_rows = lax.dynamic_slice_in_dim(intersections, first_row, half, 2)
    own = (amplitudes.astype(jnp.float32) * mask).astype(jnp.bfloat16)
    ints = integrals.astype(jnp.float32)
    offset = neighbours // frag - chain_pos + 1
    within = neighbours % frag
    slots = within // count * (3 * count) + offset * count + within % count
    window = spread_amps(own)
    norms = []
    for step_no in range(ITERS):
        blocks = jnp.take(window, slots, axis=0)
        proj = jnp.einsum(
            "pnab,pnbc->pnac", over_rows, blocks, preferred_element_type=jnp.float32
        ).astype(jnp.bfloat16)
        terms = jnp.einsum(
            "pnac,pnbc->pnab", proj, intersections, preferred_element_type=jnp.float32
        )
        coupled = jnp.einsum("pn,pnab->pab", coupling, terms)
        own32 = own.astype(jnp.float32)
        resid = mask * (ints + coupled - denom * own32)
        delta = resid / denom
        more = step_no + 1 < ITERS
        squares = over_axes(jnp.sum(resid * resid), ("chain", "pair", "pno"))
        rms = jnp.sqrt(squares / cells)
        factor = 1.0 / (1.0 + rms)
        norms.append(rms)
        own = (own32 + delta * factor).astype(jnp.bfloat16)
        if more:
            window = spread_amps(own)
    return (own, jnp.stack(norms))


def solution(mesh):
    in_specs = (
        P(("job", "chain", "pair"), "pno", None),
        P(("job", "chain", "pair"), "pno", None),
        P(("job", "chain", "pair"), None, None, None),
        P(("job", "chain", "pair"), None),
        P(("job", "chain", "pair"), None),
        P(("job", "chain", "pair")),
        P(("job", "chain", "pair")),
        P(("job", "chain", "pair"), None),
    )
    out_specs = (P(("job", "chain", "pair"), "pno", None), P("job"))
    return jax.shard_map(
        per_device, mesh=mesh, in_specs=in_specs, out_specs=out_specs, check_vma=False
    )
```

profile of v0, /device:TPU:80, one launch (start us, length us, event | category | flops | bytes accessed | tf_op | source)
XLA Modules:
  0.0 527.2 jit_solution(2827774392820882856)
XLA Ops:
  9.8 3.9 all_to_all.15
  13.7 1.3 collective-permute-start.1
  15.0 6.7 %collective-permute-start = (bf16[6,128,128]{2,1,0:T(8,128)(2,1)S(1)}, bf16[6,128,128]{2,1,0:T(8,128)(2,1)S(1)}, u32[]{:S(2)}, u32[]{:S(2)}) collective-permute-start(bf16[6,128,128]{2,1,0:T(8,128)(2,1)S(1)} %bitcast.32), channel_id=1, source_target_pairs={{0,16},{16,32},{32,48},{48,64},{64,80},{80,96},{96,112},{112,128},... | collective-permute-start | bytes 589832 | tf_op jit(solution)/shard_map/ppermute | solution.py:32
  21.7 3.2 collective-permute-done.1
  28.7 94.6 %all-gather.4.cloned.1.call-done = bf16[144,128,128]{2,1,0:T(8,128)(2,1)} async-done(((bf16[18,128,128]{2,1,0:T(8,128)(2,1)}), bf16[144,128,128]{2,1,0:T(8,128)(2,1)}) %all-gather.4.cloned.1.call-update) | async-done | bytes 4718608 | tf_op jit(solution)/shard_map/all_gather | solution.py:50
  123.4 10.4 %gather_fusion = bf16[192,128,128]{2,1,0:T(8,128)(2,1)} fusion(bf16[144,128,128]{2,1,0:T(8,128)(2,1)} %all-gather.4.cloned.1.call-done, s32[1024]{0:T(1024)S(1)} %pad_clamp_fusion), kind=kCustom, calls=%fused_computation.clone | custom fusion | bytes 12583680 | tf_op jit(solution)/shard_map/jit(_take)/gather | solution.py:79
  133.8 10.9 %fusion.22 = bf16[6,32,64,128]{3,2,1,0:T(8,128)(2,1)} fusion(bf16[6,32,128,128]{3,2,1,0:T(8,128)(2,1)} %param.12, bf16[6,32,128,128]{3,2,1,0:T(8,128)(2,1)} %bitcast.29, pred[6,32]{1,0:T(8,128)(4,1)S(1)} %get-tuple-element.3, s32[]{:T(128)S(6)} %select_n.29), kind=kOutput, calls=%fused_computation.25 | convolution fusion | flops 810024960 | bytes 18874564 | tf_op jit(solution)/shard_map/pnac,pnbc->pnab/dot_general | solution.py:83
  144.6 3.7 fusion.4
  149.2 32.8 %psum.63 = f32[]{:T(128)} all-reduce(f32[]{:T(128)} %multiply_reduce_fusion.2), channel_id=1, replica_groups=mesh['job'=2,'chain'=16,'pair'=8,'pno'=2] {'chain'}, use_global_device_ids=true, to_apply=%region_1.3 | all-reduce | flops 1 | bytes 8 | tf_op jit(solution)/shard_map/psum | solution.py:43
  181.9 16.2 %psum.64 = f32[]{:T(128)} all-reduce(f32[]{:T(128)} %psum.63), channel_id=1, replica_groups=mesh['job'=2,'chain'=16,'pair'=8,'pno'=2] {'pair'}, use_global_device_ids=true, to_apply=%region_2.4 | all-reduce | flops 1 | bytes 8 | tf_op jit(solution)/shard_map/psum | solution.py:43
  198.2 3.1 psum.65
  202.3 3.9 all_to_all.16
  206.2 1.3 collective-permute-start.3
  207.5 4.6 collective-permute-start.2
  212.1 3.0 collective-permute-done.3
  217.5 64.6 %all-gather.6.cloned.1.call-done = bf16[144,128,128]{2,1,0:T(8,128)(2,1)} async-done(((bf16[18,128,128]{2,1,0:T(8,128)(2,1)}), bf16[144,128,128]{2,1,0:T(8,128)(2,1)}) %all-gather.6.cloned.1.call-update) | async-done | bytes 4718608 | tf_op jit(solution)/shard_map/all_gather | solution.py:50
  282.1 10.4 %gather_fusion.1 = bf16[192,128,128]{2,1,0:T(8,128)(2,1)} fusion(bf16[144,128,128]{2,1,0:T(8,128)(2,1)} %all-gather.6.cloned.1.call-done, s32[1024]{0:T(1024)S(1)} %pad_clamp_fusion), kind=kCustom, calls=%fused_computation.1.clone | custom fusion | bytes 12583680 | tf_op jit(solution)/shard_map/jit(_take)/gather | solution.py:79
  292.5 10.8 %fusion.20 = bf16[6,32,64,128]{3,2,1,0:T(8,128)(2,1)} fusion(bf16[6,32,128,128]{3,2,1,0:T(8,128)(2,1)} %param.12, bf16[6,32,128,128]{3,2,1,0:T(8,128)(2,1)} %bitcast.30, pred[6,32]{1,0:T(8,128)(4,1)S(1)} %get-tuple-element.3, s32[]{:T(128)S(6)} %select_n.29), kind=kOutput, calls=%fused_computation.23 | convolution fusion | flops 810024960 | bytes 18874564 | tf_op jit(solution)/shard_map/pnac,pnbc->pnab/dot_general | solution.py:83
  303.3 3.7 fusion.2
  307.8 32.8 %psum.66 = f32[]{:T(128)} all-reduce(f32[]{:T(128)} %multiply_reduce_fusion.1), channel_id=1, replica_groups=mesh['job'=2,'chain'=16,'pair'=8,'pno'=2] {'chain'}, use_global_device_ids=true, to_apply=%region_5.7 | all-reduce | flops 1 | bytes 8 | tf_op jit(solution)/shard_map/psum | solution.py:43
  340.6 16.2 %psum.67 = f32[]{:T(128)} all-reduce(f32[]{:T(128)} %psum.66), channel_id=1, replica_groups=mesh['job'=2,'chain'=16,'pair'=8,'pno'=2] {'pair'}, use_global_device_ids=true, to_apply=%region_6.8 | all-reduce | flops 1 | bytes 8 | tf_op jit(solution)/shard_map/psum | solution.py:43
  356.8 3.1 psum.68
  360.9 3.9 all_to_all.17
  366.1 4.8 collective-permute-start.4
  371.0 2.7 collective-permute-done.5
  375.8 64.9 %all-gather.8.cloned.1.call-done = bf16[144,128,128]{2,1,0:T(8,128)(2,1)} async-done(((bf16[18,128,128]{2,1,0:T(8,128)(2,1)}), bf16[144,128,128]{2,1,0:T(8,128)(2,1)}) %all-gather.8.cloned.1.call-update) | async-done | bytes 4718608 | tf_op jit(solution)/shard_map/all_gather | solution.py:50
  440.7 10.4 %gather_fusion.2 = bf16[192,128,128]{2,1,0:T(8,128)(2,1)} fusion(bf16[144,128,128]{2,1,0:T(8,128)(2,1)} %all-gather.8.cloned.1.call-done, s32[1024]{0:T(1024)S(1)} %pad_clamp_fusion), kind=kCustom, calls=%fused_computation.2.clone | custom fusion | bytes 12583680 | tf_op jit(solution)/shard_map/jit(_take)/gather | solution.py:79
  451.1 10.8 %fusion.18 = bf16[6,32,64,128]{3,2,1,0:T(8,128)(2,1)} fusion(bf16[6,32,128,128]{3,2,1,0:T(8,128)(2,1)} %param.12, bf16[6,32,128,128]{3,2,1,0:T(8,128)(2,1)} %bitcast.28, pred[6,32]{1,0:T(8,128)(4,1)S(1)} %get-tuple-element.3, s32[]{:T(128)S(6)} %select_n.29), kind=kOutput, calls=%fused_computation.21 | convolution fusion | flops 810024960 | bytes 18874564 | tf_op jit(solution)/shard_map/pnac,pnbc->pnab/dot_general | solution.py:83
  461.9 3.7 fusion
  466.4 32.8 %psum.69 = f32[]{:T(128)} all-reduce(f32[]{:T(128)} %multiply_reduce_fusion), channel_id=1, replica_groups=mesh['job'=2,'chain'=16,'pair'=8,'pno'=2] {'chain'}, use_global_device_ids=true, to_apply=%region_9.11 | all-reduce | flops 1 | bytes 8 | tf_op jit(solution)/shard_map/psum | solution.py:43
  499.2 16.2 %psum.70 = f32[]{:T(128)} all-reduce(f32[]{:T(128)} %psum.69), channel_id=1, replica_groups=mesh['job'=2,'chain'=16,'pair'=8,'pno'=2] {'pair'}, use_global_device_ids=true, to_apply=%region_10.12 | all-reduce | flops 1 | bytes 8 | tf_op jit(solution)/shard_map/psum | solution.py:43
  515.4 3.1 psum.71
  (44 shorter events, 16.4 us)
Async XLA Ops:
  7.2 137.5 %copy-start = (f32[6,32]{1,0:T(8,128)S(1)}, f32[6,32]{1,0:T(8,128)}, u32[]{:S(2)}) copy-start(f32[6,32]{1,0:T(8,128)} %param.13) | copy-start | bytes 2308
  7.2 116.2 %all-gather.4.cloned.1.call-start = ((), (), s32[]{:S(2)}) async-start(), calls=%async_computation.3 | async-start | bytes 5308416 | tf_op jit(solution)/shard_map/all_gather | solution.py:50
  13.7 11.2 %collective-permute-start.1 = (bf16[6,128,128]{2,1,0:T(8,128)(2,1)S(1)}, bf16[6,128,128]{2,1,0:T(8,128)(2,1)S(1)}, u32[]{:S(2)}, u32[]{:S(2)}) collective-permute-start(bf16[6,128,128]{2,1,0:T(8,128)(2,1)S(1)} %bitcast.31), channel_id=1, source_target_pairs={{16,0},{32,16},{48,32},{64,48},{80,64},{96,80},{112,96},{128,112},... | collective-permute-start | bytes 589832 | tf_op jit(solution)/shard_map/ppermute | solution.py:34
  15.0 11.1 %collective-permute-start = (bf16[6,128,128]{2,1,0:T(8,128)(2,1)S(1)}, bf16[6,128,128]{2,1,0:T(8,128)(2,1)S(1)}, u32[]{:S(2)}, u32[]{:S(2)}) collective-permute-start(bf16[6,128,128]{2,1,0:T(8,128)(2,1)S(1)} %bitcast.32), channel_id=1, source_target_pairs={{0,16},{16,32},{32,48},{48,64},{64,80},{80,96},{96,112},{112,128},... | collective-permute-start | bytes 589832 | tf_op jit(solution)/shard_map/ppermute | solution.py:32
  27.1 255.0 %all-gather.6.cloned.1.call-start = ((), (), s32[]{:S(2)}) async-start(), calls=%async_computation.4 | async-start | bytes 5308416 | tf_op jit(solution)/shard_map/all_gather | solution.py:50
  133.8 14.6 %copy-start.1 = (bf16[6,64,128]{2,1,0:T(8,128)(2,1)S(1)}, bf16[6,64,128]{2,1,0:T(8,128)(2,1)}, u32[]{:S(2)}) copy-start(bf16[6,64,128]{2,1,0:T(8,128)(2,1)} %param.11) | copy-start | bytes 294916
  133.8 14.6 %copy-start.2 = (bf16[6,64,128]{2,1,0:T(8,128)(2,1)S(1)}, bf16[6,64,128]{2,1,0:T(8,128)(2,1)}, u32[]{:S(2)}) copy-start(bf16[6,64,128]{2,1,0:T(8,128)(2,1)} %param.10) | copy-start | bytes 294916
  133.8 14.6 %copy-start.3 = (f32[6,128]{1,0:T(8,128)S(1)}, f32[6,128]{1,0:T(8,128)}, u32[]{:S(2)}) copy-start(f32[6,128]{1,0:T(8,128)} %param.14) | copy-start | bytes 9220
  133.8 14.6 %copy-start.4 = (f32[6]{0:T(128)S(1)}, f32[6]{0:T(128)}, u32[]{:S(2)}) copy-start(f32[6]{0:T(128)} %param.15) | copy-start | bytes 76
  206.2 8.9 %collective-permute-start.3 = (bf16[6,128,128]{2,1,0:T(8,128)(2,1)S(1)}, bf16[6,128,128]{2,1,0:T(8,128)(2,1)S(1)}, u32[]{:S(2)}, u32[]{:S(2)}) collective-permute-start(bf16[6,128,128]{2,1,0:T(8,128)(2,1)S(1)} %bitcast.34), channel_id=1, source_target_pairs={{16,0},{32,16},{48,32},{64,48},{80,64},{96,80},{112,96},{128,112},... | collective-permute-start | bytes 589832 | tf_op jit(solution)/shard_map/ppermute | solution.py:34
  207.5 8.8 %collective-permute-start.2 = (bf16[6,128,128]{2,1,0:T(8,128)(2,1)S(1)}, bf16[6,128,128]{2,1,0:T(8,128)(2,1)S(1)}, u32[]{:S(2)}, u32[]{:S(2)}) collective-permute-start(bf16[6,128,128]{2,1,0:T(8,128)(2,1)S(1)} %bitcast.35), channel_id=1, source_target_pairs={{0,16},{16,32},{32,48},{48,64},{64,80},{80,96},{96,112},{112,128},... | collective-permute-start | bytes 589832 | tf_op jit(solution)/shard_map/ppermute | solution.py:32
  217.2 223.5 %all-gather.8.cloned.1.call-start = ((), (), s32[]{:S(2)}) async-start(), calls=%async_computation.5 | async-start | bytes 5308416 | tf_op jit(solution)/shard_map/all_gather | solution.py:50
  364.8 8.9 %collective-permute-start.5 = (bf16[6,128,128]{2,1,0:T(8,128)(2,1)S(1)}, bf16[6,128,128]{2,1,0:T(8,128)(2,1)S(1)}, u32[]{:S(2)}, u32[]{:S(2)}) collective-permute-start(bf16[6,128,128]{2,1,0:T(8,128)(2,1)S(1)} %bitcast.37), channel_id=1, source_target_pairs={{16,0},{32,16},{48,32},{64,48},{80,64},{96,80},{112,96},{128,112},... | collective-permute-start | bytes 589832 | tf_op jit(solution)/shard_map/ppermute | solution.py:34
  366.1 8.8 %collective-permute-start.4 = (bf16[6,128,128]{2,1,0:T(8,128)(2,1)S(1)}, bf16[6,128,128]{2,1,0:T(8,128)(2,1)S(1)}, u32[]{:S(2)}, u32[]{:S(2)}) collective-permute-start(bf16[6,128,128]{2,1,0:T(8,128)(2,1)S(1)} %bitcast.38), channel_id=1, source_target_pairs={{0,16},{16,32},{32,48},{48,64},{64,80},{80,96},{96,112},{112,128},... | collective-permute-start | bytes 589832 | tf_op jit(solution)/shard_map/ppermute | solution.py:32
Sparse Core Ops, SparseCore 0:
  27.2 96.1 all-gather.3
  217.3 64.7 all-gather.5
  376.0 64.7 all-gather.7
where the time goes:
time: 530 us; the launch traced here: 527 us
  waiting for transfers between devices  237 us (45%)
  blocking collectives  168 us (32%)
  matrix products  43.6 us (8%)
  local copies, waits for them, and re-layouts  32.1 us (6%)
  starting transfers between devices  20.4 us (4%)
  between operations  16.1 us (3%)
  other arithmetic  9.94 us (2%)
    all_gather x3, waiting for transfers between devices, spread_amps(): return lax.all_gather(beside, 'pair', axis=0, tiled=True)  224 us
    psum x9, blocking collectives, over_axes(): value = lax.psum(value, axis)  156 us
    dot_general x3, matrix products, per_device(): jnp.einsum('pnac,pnbc->pnab', proj, intersections, preferred_element_type...  32.5 us
    gather x3, local copies, waits for them, and re-layouts, per_device(): blocks = jnp.take(window, slots, axis=0)  31.2 us
    ppermute x3, starting transfers between devices, padded(): lax.ppermute(tail, axis, [(i, (i + 1) % count) for i in range(ends)])  16.1 us
    all_to_all x3, blocking collectives, copy_for_each(): return lax.all_to_all(copies, axis, split_axis=0, concat_axis=0, tiled=True)  11.7 us
    dot_general x3, matrix products, per_device(): coupled = jnp.einsum('pn,pnab->pab', coupling, terms)  11.2 us
  transfers between devices with their start and end apart: 9, of which 9 were waited for; matrix products, arithmetic and copies ran while one was open for 0% of the time, Pallas kernels for 0%

commit v1 on v0

v1 whole, which is shorter than its diff:
```python
import jax
import jax.numpy as jnp
from jax import lax
from jax.experimental import pallas as pl
from jax.experimental.pallas import tpu as pltpu
from jax.sharding import PartitionSpec as P

ITERS = 3
PRODUCTS = [(i, j) for i in range(ITERS) for j in range(i + 1)]


def shifted(value, axis, step):
    count = lax.axis_size(axis)
    pairs = [(i, i + step) for i in range(count) if 0 <= i + step < count]
    return lax.ppermute(value, axis, pairs)


def copies_of_all(value, axes):
    count = 1
    for axis in axes:
        count *= lax.axis_size(axis)
    copies = jnp.broadcast_to(value, (count, *value.shape))
    return lax.all_to_all(copies, axes, 0, 0, tiled=True)


def spread(piece):
    here = copies_of_all(piece, ("pair",))
    here = here.reshape(-1, *piece.shape[1:])
    return shifted(here, "chain", 1), here, shifted(here, "chain", -1)


def live_cells(rank, first, half, width):
    rows = first + lax.broadcasted_iota(jnp.int32, (half, width), 0)
    columns = lax.broadcasted_iota(jnp.int32, (half, width), 1)
    return (rows < rank) & (columns < rank)


def start_kernel(side, ranks, amplitudes, own):
    count, half, width = amplitudes.shape
    for g in range(count):
        live = live_cells(ranks[g], side[0] * half, half, width)
        block = jnp.where(live, amplitudes[g].astype(jnp.float32), 0.0)
        own[g] = block.astype(jnp.bfloat16)


def masked(side, ranks, amplitudes):
    return pl.pallas_call(
        start_kernel,
        grid_spec=pltpu.PrefetchScalarGridSpec(
            num_scalar_prefetch=2,
            grid=(1,),
            in_specs=[pl.BlockSpec(amplitudes.shape, lambda i, *_: (0, 0, 0))],
            out_specs=pl.BlockSpec(amplitudes.shape, lambda i, *_: (0, 0, 0)),
        ),
        out_shape=jax.ShapeDtypeStruct(amplitudes.shape, jnp.bfloat16),
        name="masked",
    )(side, ranks, amplitudes)


def couple_kernel(slots, side, weights, low, here, high, over, out, window, stack):
    pair = pl.program_id(0)
    terms, width = over.shape[1], over.shape[2]
    half = here.shape[1]
    first = pl.multiple_of(side[0] * half, half)

    @pl.when(pair == 0)
    def _():
        frag = here.shape[0]
        window[0:frag] = low[...]
        window[frag : 2 * frag] = here[...]
        window[2 * frag : 3 * frag] = high[...]
        stack[...] = jnp.zeros_like(stack)

    for n in range(terms):
        block = window[slots[pair * terms + n]]
        right = lax.dot_general(
            block, over[0, n], (((1,), (1,)), ((), ())), preferred_element_type=jnp.float32
        )
        right = (right * weights[pair * terms + n]).astype(jnp.bfloat16)
        stack[pl.ds(pl.multiple_of(n * width + first, half), half), :] = right
    left = jnp.concatenate([over[0, n] for n in range(terms)], axis=1)
    both = jnp.dot(left, stack[...], preferred_element_type=jnp.float32)
    out[0, 0] = both[:half]
    out[1, 0] = both[half:]


def couple(slots, side, weights, low, here, high, over):
    count, terms, width, _ = over.shape
    frag, half, _ = here.shape
    whole = pl.BlockSpec((frag, half, width), lambda g, *_: (0, 0, 0))
    grid_spec = pltpu.PrefetchScalarGridSpec(
        num_scalar_prefetch=3,
        grid=(count,),
        in_specs=[
            whole,
            whole,
            whole,
            pl.BlockSpec((1, terms, width, width), lambda g, *_: (g, 0, 0, 0)),
        ],
        out_specs=pl.BlockSpec((2, 1, half, width), lambda g, *_: (0, g, 0, 0)),
        scratch_shapes=[
            pltpu.VMEM((3 * frag, half, width), jnp.bfloat16),
            pltpu.VMEM((terms * width, width), jnp.bfloat16),
        ],
    )
    return pl.pallas_call(
        couple_kernel,
        grid_spec=grid_spec,
        out_shape=jax.ShapeDtypeStruct((2, count, half, width), jnp.float32),
        compiler_params=pltpu.CompilerParams(
            dimension_semantics=("arbitrary",), vmem_limit_bytes=24 * 1024 * 1024
        ),
        name="couple",
    )(slots, side, weights, low, here, high, over)


def products_kernel(scale, parts, mask, *refs):
    held, (last, sums) = refs[:-2], refs[-2:]
    last[...] = mask[...] * (parts[0] + parts[1]) - held[-1][...]
    terms = [ref[...] * scale for ref in held] + [last[...] * scale]
    lane = lax.broadcasted_iota(jnp.int32, sums.shape, 1)
    row = jnp.zeros(sums.shape, jnp.float32)
    for place, (i, j) in enumerate(PRODUCTS):
        row = jnp.where(lane == place, jnp.sum(terms[i] * terms[j]), row)
    sums[...] = row


def products(scale, parts, mask, held):
    shape = mask.shape
    return pl.pallas_call(
        lambda *refs: products_kernel(scale, *refs),
        out_shape=(
            jax.ShapeDtypeStruct(shape, jnp.float32),
            jax.ShapeDtypeStruct((1, shape[-1]), jnp.float32),
        ),
        name="products",
    )(parts, mask, *held)


def finish_kernel(copies, own, denom, *refs):
    terms, (amps, norms) = refs[:-2], refs[-2:]
    total = jnp.sum(copies[...], axis=0)
    gram = {}
    for place, (i, j) in enumerate(PRODUCTS):
        gram[i, j] = gram[j, i] = total[:, place : place + 1]
    one = jnp.ones_like(gram[0, 0])
    shares = [one] + [jnp.zeros_like(one)] * (ITERS - 1)
    sums = [jnp.zeros_like(one)] * ITERS
    for step_no in range(ITERS):
        square = jnp.zeros_like(one)
        for i in range(step_no + 1):
            for j in range(step_no + 1):
                square = square + (shares[i] * gram[i, j]) * shares[j]
        rms = jnp.sqrt(jnp.maximum(square, 0.0))
        norms[step_no] = rms[0, 0]
        factor = 1.0 / (1.0 + rms)
        sums = [held + factor * share for held, share in zip(sums, shares, strict=True)]
        shares = [shares[0]] + [
            shares[i] + factor * shares[i - 1] for i in range(1, ITERS)
        ]
    change = sum(held * ref[...].reshape(-1, own.shape[-1]) for held, ref in zip(sums, terms, strict=True))
    change = change.reshape(own.shape)
    amps[...] = (own[...].astype(jnp.float32) + change / denom[...]).astype(jnp.bfloat16)


def finish(copies, own, denom, terms):
    return pl.pallas_call(
        finish_kernel,
        out_shape=(
            jax.ShapeDtypeStruct(own.shape, jnp.bfloat16),
            jax.ShapeDtypeStruct((ITERS,), jnp.float32),
        ),
        out_specs=(pl.BlockSpec(memory_space=pltpu.VMEM), pl.BlockSpec(memory_space=pltpu.SMEM)),
        name="finish",
    )(copies, own, denom, *terms)


def per_device(
    amplitudes, integrals, intersections, coupling, pno_energies, pair_shift, ranks, neighbours
):
    count, half, width = amplitudes.shape
    chain_pos = lax.axis_index("chain")
    side = lax.axis_index("pno")
    first_row = side * half
    frag = count * lax.axis_size("pair")
    cells = frag * lax.axis_size("chain") * width * width
    sides = jnp.reshape(side, (1,)).astype(jnp.int32)
    own = masked(sides, ranks, amplitudes)
    columns = jnp.arange(width, dtype=jnp.int32)
    rows_here = first_row + jnp.arange(half, dtype=jnp.int32)
    live_cols = columns[None, :] < ranks[:, None]
    live_rows = rows_here[None, :] < ranks[:, None]
    mask = (live_rows[:, :, None] & live_cols[:, None, :]).astype(jnp.float32)
    energy_rows = lax.dynamic_slice_in_dim(pno_energies, first_row, half, 1)
    denom = energy_rows[:, :, None] + pno_energies[:, None, :] - pair_shift[:, None, None]
    slots = (neighbours - (chain_pos - 1) * frag).reshape(-1)
    weights = coupling.reshape(-1)
    over = pltpu.with_memory_space_constraint(intersections, pltpu.HBM)

    def coupled_parts(piece):
        low, here, high = spread(piece)
        parts = couple(slots, sides, weights, low, here, high, over)
        return lax.all_to_all(parts, "pno", 0, 0, tiled=True)

    parts = coupled_parts(own)
    ints = integrals.astype(jnp.float32)
    terms = [mask * (ints + (parts[0] + parts[1]) - denom * own.astype(jnp.float32))]
    for step_no in range(1, ITERS):
        parts = coupled_parts((terms[-1] / denom).astype(jnp.bfloat16))
        if step_no + 1 < ITERS:
            terms.append(mask * (parts[0] + parts[1]) - terms[-1])
    last, sums = products(cells**-0.5, parts, mask, terms)
    sums = jnp.sum(copies_of_all(sums, ("pair", "pno")), axis=0, keepdims=True)[0]
    return tuple(finish(copies_of_all(sums, ("chain",)), own, denom, terms + [last]))


def solution(mesh):
    in_specs = (
        P(("job", "chain", "pair"), "pno", None),
        P(("job", "chain", "pair"), "pno", None),
        P(("job", "chain", "pair"), None, None, None),
        P(("job", "chain", "pair"), None),
        P(("job", "chain", "pair"), None),
        P(("job", "chain", "pair")),
        P(("job", "chain", "pair")),
        P(("job", "chain", "pair"), None),
    )
    out_specs = (P(("job", "chain", "pair"), "pno", None), P("job"))
    return jax.shard_map(
        per_device, mesh=mesh, in_specs=in_specs, out_specs=out_specs, check_vma=False
    )
```

time: 530 us -> 280 us (0.53)
  waiting for transfers between devices: 237 us -> 86.1 us
  blocking collectives: 168 us -> 117 us
  matrix products: 43.6 us -> 0 us
  Pallas kernels: 0 us -> 35.8 us
  local copies, waits for them, and re-layouts: 32.1 us -> 4.69 us
  between operations: 16.1 us -> 0.78 us
  starting transfers between devices: 20.4 us -> 29.4 us
    all_gather x3 -> x0, waiting for transfers between devices: 224 us -> none  [spread_amps(): return lax.all_gather(beside, 'pair', axis=0, tiled=True)]
    psum x9 -> x0, blocking collectives: 156 us -> none  [over_axes(): value = lax.psum(value, axis)]
    all_to_all x3 -> x7, blocking collectives: 11.7 us -> 117 us  [the longest x4 104 us: copies_of_all(): return lax.all_to_all(copies, axes, 0, 0, tiled=True)]
    ppermute x6, waiting for transfers between devices: 12.6 us -> 62.9 us  [shifted(): return lax.ppermute(value, axis, pairs)]
    dot_general x6 -> x0, matrix products: 43.6 us -> none  [the longest x3 32.5 us: per_device(): jnp.einsum('pnac,pnbc->pnab', proj, intersections, preferred_element_type...]
    pallas_call x0 -> x6, Pallas kernels: none -> 35.8 us  [the longest x3 29.1 us: couple(): pl.pallas_call(couple_kernel, grid_spec=grid_spec, out_shape=jax.ShapeDty...]
    gather x3 -> x0, local copies, waits for them, and re-layouts: 31.2 us -> none  [per_device(): blocks = jnp.take(window, slots, axis=0)]
    all_to_all x0 -> x1, waiting for transfers between devices: none -> 23.2 us  [copies_of_all(): return lax.all_to_all(copies, axes, 0, 0, tiled=True)]
  transfers between devices with their start and end apart: 9 -> 7, of which waited for: 9 -> 7; matrix products, arithmetic and copies ran while one was open for 0% -> 2% of each run, Pallas kernels for 0% -> 0%
where the time goes in v1:
time: 280 us; the launch traced here: 279 us
  blocking collectives  117 us (42%)
  waiting for transfers between devices  86.1 us (31%)
  Pallas kernels  35.8 us (13%)
  starting transfers between devices  29.4 us (10%)
  local copies, waits for them, and re-layouts  4.69 us (2%)
  other arithmetic  4.66 us (2%)
    all_to_all x4, blocking collectives, copies_of_all(): return lax.all_to_all(copies, axes, 0, 0, tiled=True)  104 us
    ppermute x6, waiting for transfers between devices, shifted(): return lax.ppermute(value, axis, pairs)  62.9 us
    pallas_call x3, Pallas kernels, couple(): pl.pallas_call(couple_kernel, grid_spec=grid_spec, out_shape=jax.ShapeDty...  29.1 us
    all_to_all x1, waiting for transfers between devices, copies_of_all(): return lax.all_to_all(copies, axes, 0, 0, tiled=True)  23.2 us
    ppermute x6, starting transfers between devices, shifted(): return lax.ppermute(value, axis, pairs)  22.1 us
    all_to_all x3, blocking collectives, coupled_parts(): return lax.all_to_all(parts, 'pno', 0, 0, tiled=True)  12.9 us
    all_to_all x1, starting transfers between devices, copies_of_all(): return lax.all_to_all(copies, axes, 0, 0, tiled=True)  7.32 us
  transfers between devices with their start and end apart: 7, of which 7 were waited for; matrix products, arithmetic and copies ran while one was open for 2% of the time, Pallas kernels for 0%

profile of v1, /device:TPU:80, one launch (start us, length us, event | category | flops | bytes accessed | tf_op | source)
XLA Modules:
  0.0 278.7 jit_solution(13882607577663187784)
XLA Ops:
  0.7 2.4 masked.1.own
  3.0 2.1 broadcast_in_dim.10
  5.1 7.3 %all-to-all-start = ((bf16[8,6,64,128]{3,2,1,0:T(8,128)(2,1)}), bf16[8,6,64,128]{3,2,1,0:T(8,128)(2,1)S(1)}, u32[]{:S(2)}, u32[]{:S(2)}) async-start(bf16[8,6,64,128]{3,2,1,0:T(8,128)(2,1)} %broadcast_in_dim.10), calls=%async_computation | async-start | bytes 1572864 | tf_op jit(solution)/shard_map/all_to_all | solution.py:23
  12.4 23.2 %all-to-all-done = bf16[8,6,64,128]{3,2,1,0:T(8,128)(2,1)S(1)} async-done(((bf16[8,6,64,128]{3,2,1,0:T(8,128)(2,1)}), bf16[8,6,64,128]{3,2,1,0:T(8,128)(2,1)S(1)}, u32[]{:S(2)}, u32[]{:S(2)}) %all-to-all-start) | async-done | bytes 786464 | tf_op jit(solution)/shard_map/all_to_all | solution.py:23
  35.6 6.1 %collective-permute-start = (bf16[48,64,128]{2,1,0:T(8,128)(2,1)S(1)}, bf16[48,64,128]{2,1,0:T(8,128)(2,1)S(1)}, u32[]{:S(2)}, u32[]{:S(2)}) collective-permute-start(bf16[48,64,128]{2,1,0:T(8,128)(2,1)S(1)} %bitcast.20), channel_id=1, source_target_pairs={{0,16},{16,32},{32,48},{48,64},{64,80},{80,96},{96,112},{112,128},... | collective-permute-start | bytes 2359304 | tf_op jit(solution)/shard_map/ppermute | solution.py:15
  41.6 1.3 collective-permute-start.1
  43.7 0.8 reshape.80.weights
  46.7 11.8 %collective-permute-done.low = bf16[48,64,128]{2,1,0:T(8,128)(2,1)S(1)} collective-permute-done((bf16[48,64,128]{2,1,0:T(8,128)(2,1)S(1)}, bf16[48,64,128]{2,1,0:T(8,128)(2,1)S(1)}, u32[]{:S(2)}, u32[]{:S(2)}) %collective-permute-start) | collective-permute-done | bytes 786464 | tf_op jit(solution)/shard_map/ppermute | solution.py:15
  58.6 6.5 %collective-permute-done.1.high = bf16[48,64,128]{2,1,0:T(8,128)(2,1)S(1)} collective-permute-done((bf16[48,64,128]{2,1,0:T(8,128)(2,1)S(1)}, bf16[48,64,128]{2,1,0:T(8,128)(2,1)S(1)}, u32[]{:S(2)}, u32[]{:S(2)}) %collective-permute-start.1) | collective-permute-done | bytes 786464 | tf_op jit(solution)/shard_map/ppermute | solution.py:15
  65.1 9.7 %couple.3 = f32[2,6,64,128]{3,2,1,0:T(8,128)S(1)} custom-call(s32[192]{0:T(256)S(1)} %reshape.78.slots, s32[1]{0:T(128)} %bitcast.side, f32[192]{0:T(256)S(1)} %reshape.80.weights, bf16[48,64,128]{2,1,0:T(8,128)(2,1)S(1)} %collective-permute-done.low, bf16[48,64,128]{2,1,0:T(8,128)(2,1)S(1)} %bitcast.22, ...), custom_call_target="tpu_custom_call" | custom-call | tf_op jit(solution)/shard_map/couple/pallas_call | solution.py:106
  74.8 4.1 %all_to_all.40 = f32[2,6,64,128]{3,2,1,0:T(8,128)S(1)} all-to-all(f32[2,6,64,128]{3,2,1,0:T(8,128)S(1)} %couple.3), channel_id=1, replica_groups=mesh['job'=2,'chain'=16,'pair'=8,'pno'=2] {'pno'}, dimensions={0} | all-to-all | bytes 786432 | tf_op jit(solution)/shard_map/all_to_all | solution.py:203
  78.8 0.8 divide_convert_fusion.1
  79.9 26.1 %all_to_all.41 = bf16[8,6,64,128]{3,2,1,0:T(8,128)(2,1)S(1)} all-to-all(bf16[8,6,64,128]{3,2,1,0:T(8,128)(2,1)S(1)} %broadcast_in_dim.11), channel_id=1, replica_groups=mesh['job'=2,'chain'=16,'pair'=8,'pno'=2] {'pair'}, dimensions={0} | all-to-all | bytes 1572864 | tf_op jit(solution)/shard_map/all_to_all | solution.py:23
  106.0 6.1 %collective-permute-start.2 = (bf16[48,64,128]{2,1,0:T(8,128)(2,1)S(1)}, bf16[48,64,128]{2,1,0:T(8,128)(2,1)S(1)}, u32[]{:S(2)}, u32[]{:S(2)}) collective-permute-start(bf16[48,64,128]{2,1,0:T(8,128)(2,1)S(1)} %bitcast.26), channel_id=1, source_target_pairs={{0,16},{16,32},{32,48},{48,64},{64,80},{80,96},{96,112},{112,128},... | collective-permute-start | bytes 2359304 | tf_op jit(solution)/shard_map/ppermute | solution.py:15
  112.1 1.3 collective-permute-start.3
  113.4 15.6 %collective-permute-done.2.low = bf16[48,64,128]{2,1,0:T(8,128)(2,1)S(1)} collective-permute-done((bf16[48,64,128]{2,1,0:T(8,128)(2,1)S(1)}, bf16[48,64,128]{2,1,0:T(8,128)(2,1)S(1)}, u32[]{:S(2)}, u32[]{:S(2)}) %collective-permute-start.2) | collective-permute-done | bytes 786464 | tf_op jit(solution)/shard_map/ppermute | solution.py:15
  129.0 7.7 %collective-permute-done.3.high = bf16[48,64,128]{2,1,0:T(8,128)(2,1)S(1)} collective-permute-done((bf16[48,64,128]{2,1,0:T(8,128)(2,1)S(1)}, bf16[48,64,128]{2,1,0:T(8,128)(2,1)S(1)}, u32[]{:S(2)}, u32[]{:S(2)}) %collective-permute-start.3) | collective-permute-done | bytes 786464 | tf_op jit(solution)/shard_map/ppermute | solution.py:15
  136.7 9.7 %couple.4 = f32[2,6,64,128]{3,2,1,0:T(8,128)S(1)} custom-call(s32[192]{0:T(256)S(1)} %reshape.78.slots, s32[1]{0:T(128)} %bitcast.side, f32[192]{0:T(256)S(1)} %reshape.80.weights, bf16[48,64,128]{2,1,0:T(8,128)(2,1)S(1)} %collective-permute-done.2.low, bf16[48,64,128]{2,1,0:T(8,128)(2,1)S(1)} %bitcast.28, ...), custom_call_target="tpu_custom_call" | custom-call | tf_op jit(solution)/shard_map/couple/pallas_call | solution.py:106
  146.4 4.1 %all_to_all.42 = f32[2,6,64,128]{3,2,1,0:T(8,128)S(1)} all-to-all(f32[2,6,64,128]{3,2,1,0:T(8,128)S(1)} %couple.4), channel_id=1, replica_groups=mesh['job'=2,'chain'=16,'pair'=8,'pno'=2] {'pno'}, dimensions={0} | all-to-all | bytes 786432 | tf_op jit(solution)/shard_map/all_to_all | solution.py:203
  150.5 0.9 divide_convert_fusion
  151.5 26.2 %all_to_all.43 = bf16[8,6,64,128]{3,2,1,0:T(8,128)(2,1)S(1)} all-to-all(bf16[8,6,64,128]{3,2,1,0:T(8,128)(2,1)S(1)} %broadcast_in_dim.12), channel_id=1, replica_groups=mesh['job'=2,'chain'=16,'pair'=8,'pno'=2] {'pair'}, dimensions={0} | all-to-all | bytes 1572864 | tf_op jit(solution)/shard_map/all_to_all | solution.py:23
  177.7 6.1 %collective-permute-start.4 = (bf16[48,64,128]{2,1,0:T(8,128)(2,1)S(1)}, bf16[48,64,128]{2,1,0:T(8,128)(2,1)S(1)}, u32[]{:S(2)}, u32[]{:S(2)}) collective-permute-start(bf16[48,64,128]{2,1,0:T(8,128)(2,1)S(1)} %bitcast.23), channel_id=1, source_target_pairs={{0,16},{16,32},{32,48},{48,64},{64,80},{80,96},{96,112},{112,128},... | collective-permute-start | bytes 2359304 | tf_op jit(solution)/shard_map/ppermute | solution.py:15
  183.7 1.3 collective-permute-start.5
  185.1 0.8 and_convert_fusion.refs_1_
  185.9 14.8 %collective-permute-done.4.low = bf16[48,64,128]{2,1,0:T(8,128)(2,1)S(1)} collective-permute-done((bf16[48,64,128]{2,1,0:T(8,128)(2,1)S(1)}, bf16[48,64,128]{2,1,0:T(8,128)(2,1)S(1)}, u32[]{:S(2)}, u32[]{:S(2)}) %collective-permute-start.4) | collective-permute-done | bytes 786464 | tf_op jit(solution)/shard_map/ppermute | solution.py:15
  200.6 6.5 %collective-permute-done.5.high = bf16[48,64,128]{2,1,0:T(8,128)(2,1)S(1)} collective-permute-done((bf16[48,64,128]{2,1,0:T(8,128)(2,1)S(1)}, bf16[48,64,128]{2,1,0:T(8,128)(2,1)S(1)}, u32[]{:S(2)}, u32[]{:S(2)}) %collective-permute-start.5) | collective-permute-done | bytes 786464 | tf_op jit(solution)/shard_map/ppermute | solution.py:15
  207.1 9.7 %couple.5 = f32[2,6,64,128]{3,2,1,0:T(8,128)S(1)} custom-call(s32[192]{0:T(256)S(1)} %reshape.78.slots, s32[1]{0:T(128)} %bitcast.side, f32[192]{0:T(256)S(1)} %reshape.80.weights, bf16[48,64,128]{2,1,0:T(8,128)(2,1)S(1)} %collective-permute-done.4.low, bf16[48,64,128]{2,1,0:T(8,128)(2,1)S(1)} %bitcast.25, ...), custom_call_target="tpu_custom_call" | custom-call | tf_op jit(solution)/shard_map/couple/pallas_call | solution.py:106
  216.8 4.8 %all_to_all.44.refs_0_ = f32[2,6,64,128]{3,2,1,0:T(8,128)} all-to-all(f32[2,6,64,128]{3,2,1,0:T(8,128)S(1)} %couple.5), channel_id=1, replica_groups=mesh['job'=2,'chain'=16,'pair'=8,'pno'=2] {'pno'}, dimensions={0} | all-to-all | bytes 786432 | tf_op jit(solution)/shard_map/all_to_all | solution.py:203
  221.6 2.0 products.1
  224.3 10.2 %all_to_all.45 = f32[16,1,128]{2,1,0:T(1,128)S(1)} all-to-all(f32[16,1,128]{2,1,0:T(1,128)S(1)} %broadcast_in_dim.13), channel_id=1, replica_groups=mesh['job'=2,'chain'=16,'pair'=8,'pno'=2] {'pair','pno'}, dimensions={0} | all-to-all | bytes 16384 | tf_op jit(solution)/shard_map/all_to_all | solution.py:23
  234.6 41.7 %all_to_all.46.copies = f32[16,1,128]{2,1,0:T(1,128)} all-to-all(f32[16,1,128]{2,1,0:T(1,128)S(1)} %broadcast_in_dim.28), channel_id=1, replica_groups=mesh['job'=2,'chain'=16,'pair'=8,'pno'=2] {'chain'}, dimensions={0} | all-to-all | bytes 16384 | tf_op jit(solution)/shard_map/all_to_all | solution.py:23
  276.3 2.4 finish.1
  (21 shorter events, 4.0 us)
Async XLA Ops:
  0.6 78.2 %copy-start.3 = (f32[6,128]{1,0:T(8,128)S(1)}, f32[6,128]{1,0:T(8,128)}, u32[]{:S(2)}) copy-start(f32[6,128]{1,0:T(8,128)} %param.12) | copy-start | bytes 9220
  0.6 78.2 %copy-start.4 = (f32[6]{0:T(128)S(1)}, f32[6]{0:T(128)}, u32[]{:S(2)}) copy-start(f32[6]{0:T(128)} %param.13) | copy-start | bytes 76
  0.7 78.2 %copy-start.2 = (bf16[6,64,128]{2,1,0:T(8,128)(2,1)S(1)}, bf16[6,64,128]{2,1,0:T(8,128)(2,1)}, u32[]{:S(2)}) copy-start(bf16[6,64,128]{2,1,0:T(8,128)(2,1)} %param.9) | copy-start | bytes 294916
  3.0 75.8 %copy-start.1 = (bf16[6,64,128]{2,1,0:T(8,128)(2,1)S(1)}, bf16[6,64,128]{2,1,0:T(8,128)(2,1)}, u32[]{:S(2)}) copy-start(bf16[6,64,128]{2,1,0:T(8,128)(2,1)} %masked.1.own) | copy-start | bytes 294916
  5.1 30.5 %all-to-all-start = ((bf16[8,6,64,128]{3,2,1,0:T(8,128)(2,1)}), bf16[8,6,64,128]{3,2,1,0:T(8,128)(2,1)S(1)}, u32[]{:S(2)}, u32[]{:S(2)}) async-start(bf16[8,6,64,128]{3,2,1,0:T(8,128)(2,1)} %broadcast_in_dim.10), calls=%async_computation | async-start | bytes 1572864 | tf_op jit(solution)/shard_map/all_to_all | solution.py:23
  35.6 23.0 %collective-permute-start = (bf16[48,64,128]{2,1,0:T(8,128)(2,1)S(1)}, bf16[48,64,128]{2,1,0:T(8,128)(2,1)S(1)}, u32[]{:S(2)}, u32[]{:S(2)}) collective-permute-start(bf16[48,64,128]{2,1,0:T(8,128)(2,1)S(1)} %bitcast.20), channel_id=1, source_target_pairs={{0,16},{16,32},{32,48},{48,64},{64,80},{80,96},{96,112},{112,128},... | collective-permute-start | bytes 2359304 | tf_op jit(solution)/shard_map/ppermute | solution.py:15
  41.6 23.4 %collective-permute-start.1 = (bf16[48,64,128]{2,1,0:T(8,128)(2,1)S(1)}, bf16[48,64,128]{2,1,0:T(8,128)(2,1)S(1)}, u32[]{:S(2)}, u32[]{:S(2)}) collective-permute-start(bf16[48,64,128]{2,1,0:T(8,128)(2,1)S(1)} %bitcast.21), channel_id=1, source_target_pairs={{16,0},{32,16},{48,32},{64,48},{80,64},{96,80},{112,96},{128,112},... | collective-permute-start | bytes 2359304 | tf_op jit(solution)/shard_map/ppermute | solution.py:15
  79.7 71.7 %copy-start = (f32[6,64,128]{2,1,0:T(8,128)}, f32[6,64,128]{2,1,0:T(8,128)S(1)}, u32[]{:S(2)}) copy-start(f32[6,64,128]{2,1,0:T(8,128)S(1)} %get-tuple-element.9.refs_2_.refs_0_) | copy-start | bytes 589828
  106.0 23.0 %collective-permute-start.2 = (bf16[48,64,128]{2,1,0:T(8,128)(2,1)S(1)}, bf16[48,64,128]{2,1,0:T(8,128)(2,1)S(1)}, u32[]{:S(2)}, u32[]{:S(2)}) collective-permute-start(bf16[48,64,128]{2,1,0:T(8,128)(2,1)S(1)} %bitcast.26), channel_id=1, source_target_pairs={{0,16},{16,32},{32,48},{48,64},{64,80},{80,96},{96,112},{112,128},... | collective-permute-start | bytes 2359304 | tf_op jit(solution)/shard_map/ppermute | solution.py:15
  112.1 24.6 %collective-permute-start.3 = (bf16[48,64,128]{2,1,0:T(8,128)(2,1)S(1)}, bf16[48,64,128]{2,1,0:T(8,128)(2,1)S(1)}, u32[]{:S(2)}, u32[]{:S(2)}) collective-permute-start(bf16[48,64,128]{2,1,0:T(8,128)(2,1)S(1)} %bitcast.27), channel_id=1, source_target_pairs={{16,0},{32,16},{48,32},{64,48},{80,64},{96,80},{112,96},{128,112},... | collective-permute-start | bytes 2359304 | tf_op jit(solution)/shard_map/ppermute | solution.py:15
  177.7 23.0 %collective-permute-start.4 = (bf16[48,64,128]{2,1,0:T(8,128)(2,1)S(1)}, bf16[48,64,128]{2,1,0:T(8,128)(2,1)S(1)}, u32[]{:S(2)}, u32[]{:S(2)}) collective-permute-start(bf16[48,64,128]{2,1,0:T(8,128)(2,1)S(1)} %bitcast.23), channel_id=1, source_target_pairs={{0,16},{16,32},{32,48},{48,64},{64,80},{80,96},{96,112},{112,128},... | collective-permute-start | bytes 2359304 | tf_op jit(solution)/shard_map/ppermute | solution.py:15
  183.7 23.4 %collective-permute-start.5 = (bf16[48,64,128]{2,1,0:T(8,128)(2,1)S(1)}, bf16[48,64,128]{2,1,0:T(8,128)(2,1)S(1)}, u32[]{:S(2)}, u32[]{:S(2)}) collective-permute-start(bf16[48,64,128]{2,1,0:T(8,128)(2,1)S(1)} %bitcast.24), channel_id=1, source_target_pairs={{16,0},{32,16},{48,32},{64,48},{80,64},{96,80},{112,96},{128,112},... | collective-permute-start | bytes 2359304 | tf_op jit(solution)/shard_map/ppermute | solution.py:15

commit v2 on v1

--- a/solution.py
+++ b/solution.py
@@ -9,9 +9,9 @@
 PRODUCTS = [(i, j) for i in range(ITERS) for j in range(i + 1)]
 
 
-def shifted(value, axis, step):
+def shifted(value, axis, step, around=False):
     count = lax.axis_size(axis)
-    pairs = [(i, i + step) for i in range(count) if 0 <= i + step < count]
+    pairs = [(i, (i + step) % count) for i in range(count) if around or 0 <= i + step < count]
     return lax.ppermute(value, axis, pairs)
 
 
@@ -23,10 +23,16 @@
     return lax.all_to_all(copies, axes, 0, 0, tiled=True)
 
 
-def spread(piece):
-    here = copies_of_all(piece, ("pair",))
-    here = here.reshape(-1, *piece.shape[1:])
-    return shifted(here, "chain", 1), here, shifted(here, "chain", -1)
+def spread(copies):
+    count = lax.axis_size("pair")
+    groups = [list(range(first, count, 2)) for first in range(2)]
+    near = lax.all_to_all(copies, "pair", 0, 0, tiled=True, axis_index_groups=groups)
+    near = near.reshape(-1, *copies.shape[2:])
+    low, high = shifted(near, "chain", 1), shifted(near, "chain", -1)
+    other = shifted(near, "pair", 1, around=True)
+    low_other = shifted(low, "pair", 1, around=True)
+    high_other = shifted(high, "pair", -1, around=True)
+    return low, low_other, near, other, high, high_other
 
 
 def live_cells(rank, first, half, width):
@@ -35,83 +41,133 @@
     return (rows < rank) & (columns < rank)
 
 
-def start_kernel(side, ranks, amplitudes, own):
+def start_kernel(side, ranks, amplitudes, own, copies):
     count, half, width = amplitudes.shape
     for g in range(count):
         live = live_cells(ranks[g], side[0] * half, half, width)
         block = jnp.where(live, amplitudes[g].astype(jnp.float32), 0.0)
-        own[g] = block.astype(jnp.bfloat16)
-
-
-def masked(side, ranks, amplitudes):
+        block = block.astype(jnp.bfloat16)
+        own[g] = block
+        for copy in range(copies.shape[0]):
+            copies[copy, g] = block
+
+
+def masked(side, ranks, amplitudes, count):
+    shape = amplitudes.shape
     return pl.pallas_call(
         start_kernel,
         grid_spec=pltpu.PrefetchScalarGridSpec(
             num_scalar_prefetch=2,
             grid=(1,),
-            in_specs=[pl.BlockSpec(amplitudes.shape, lambda i, *_: (0, 0, 0))],
-            out_specs=pl.BlockSpec(amplitudes.shape, lambda i, *_: (0, 0, 0)),
-        ),
-        out_shape=jax.ShapeDtypeStruct(amplitudes.shape, jnp.bfloat16),
+            in_specs=[pl.BlockSpec(shape, lambda i, *_: (0, 0, 0))],
+            out_specs=[
+                pl.BlockSpec(shape, lambda i, *_: (0, 0, 0)),
+                pl.BlockSpec((count, *shape), lambda i, *_: (0, 0, 0, 0)),
+            ],
+        ),
+        out_shape=(
+            jax.ShapeDtypeStruct(shape, jnp.bfloat16),
+            jax.ShapeDtypeStruct((count, *shape), jnp.bfloat16),
+        ),
         name="masked",
     )(side, ranks, amplitudes)
 
 
-def couple_kernel(slots, side, weights, low, here, high, over, out, window, stack):
-    pair = pl.program_id(0)
+def arrange_kernel(side, after, over, across, halves):
     terms, width = over.shape[1], over.shape[2]
-    half = here.shape[1]
-    first = pl.multiple_of(side[0] * half, half)
-
-    @pl.when(pair == 0)
-    def _():
-        frag = here.shape[0]
-        window[0:frag] = low[...]
-        window[frag : 2 * frag] = here[...]
-        window[2 * frag : 3 * frag] = high[...]
-        stack[...] = jnp.zeros_like(stack)
-
+    half = width // 2
+    row = lax.broadcasted_iota(jnp.int32, (width, width), 0)
+    lane = lax.broadcasted_iota(jnp.int32, (width, width), 1)
+    first = side[0] * half
+    even = ((lane < half) & (row == lane + first)).astype(jnp.bfloat16)
+    odd = ((lane >= half) & (row == lane - half + first)).astype(jnp.bfloat16)
+    picks = jnp.concatenate([even, odd], axis=0)
+    for n in range(0, terms, 2):
+        two = jnp.concatenate([over[0, n], over[0, n + 1]], axis=1)
+        picked = jnp.dot(two, picks, preferred_element_type=jnp.float32).astype(jnp.bfloat16)
+        halves[0, :, n * half : (n + 2) * half] = picked
     for n in range(terms):
-        block = window[slots[pair * terms + n]]
-        right = lax.dot_general(
-            block, over[0, n], (((1,), (1,)), ((), ())), preferred_element_type=jnp.float32
-        )
-        right = (right * weights[pair * terms + n]).astype(jnp.bfloat16)
-        stack[pl.ds(pl.multiple_of(n * width + first, half), half), :] = right
-    left = jnp.concatenate([over[0, n] for n in range(terms)], axis=1)
-    both = jnp.dot(left, stack[...], preferred_element_type=jnp.float32)
-    out[0, 0] = both[:half]
-    out[1, 0] = both[half:]
-
-
-def couple(slots, side, weights, low, here, high, over):
+        across[0, n] = over[0, n].T
+
+
+def arrange(side, after, over):
     count, terms, width, _ = over.shape
-    frag, half, _ = here.shape
-    whole = pl.BlockSpec((frag, half, width), lambda g, *_: (0, 0, 0))
-    grid_spec = pltpu.PrefetchScalarGridSpec(
-        num_scalar_prefetch=3,
-        grid=(count,),
-        in_specs=[
-            whole,
-            whole,
-            whole,
-            pl.BlockSpec((1, terms, width, width), lambda g, *_: (g, 0, 0, 0)),
-        ],
-        out_specs=pl.BlockSpec((2, 1, half, width), lambda g, *_: (0, g, 0, 0)),
-        scratch_shapes=[
-            pltpu.VMEM((3 * frag, half, width), jnp.bfloat16),
-            pltpu.VMEM((terms * width, width), jnp.bfloat16),
-        ],
-    )
-    return pl.pallas_call(
-        couple_kernel,
-        grid_spec=grid_spec,
-        out_shape=jax.ShapeDtypeStruct((2, count, half, width), jnp.float32),
+    across = (count, terms, width, width)
+    halves = (count, width, terms * width // 2)
+    return pl.pallas_call(
+        arrange_kernel,
+        grid_spec=pltpu.PrefetchScalarGridSpec(
+            num_scalar_prefetch=1,
+            grid=(count,),
+            in_specs=[
+                pl.BlockSpec((1, *after.shape[1:]), lambda g, *_: (0, 0, 0)),
+                pl.BlockSpec((1, *over.shape[1:]), lambda g, *_: (g, 0, 0, 0)),
+            ],
+            out_specs=[
+                pl.BlockSpec((1, *across[1:]), lambda g, *_: (g, 0, 0, 0)),
+                pl.BlockSpec((1, *halves[1:]), lambda g, *_: (g, 0, 0)),
+            ],
+        ),
+        out_shape=(
+            pltpu.VMEM(across, over.dtype),
+            pltpu.VMEM(halves, over.dtype),
+        ),
         compiler_params=pltpu.CompilerParams(
             dimension_semantics=("arbitrary",), vmem_limit_bytes=24 * 1024 * 1024
         ),
+        cost_estimate=pl.CostEstimate(flops=10**9, transcendentals=0, bytes_accessed=3 * over.size),
+        name="arrange",
+    )(side, after, over)
+
+
+def couple_kernel(slots, weights, across, halves, *refs):
+    pieces, (out, window, stacks) = refs[:-3], refs[-3:]
+    count, terms, width, _ = across.shape
+    size, half, _ = pieces[0].shape
+    for place, piece in enumerate(pieces):
+        window[place * size : (place + 1) * size] = piece[...]
+
+    def right_side(g, stack):
+        for n in range(terms):
+            place = g * terms + n
+            right = jnp.dot(
+                window[slots[place]], across[g, n], preferred_element_type=jnp.float32
+            )
+            stack[n * half : (n + 1) * half] = (right * weights[place]).astype(jnp.bfloat16)
+
+    def left_side(g, stack):
+        both = jnp.dot(halves[g], stack[...], preferred_element_type=jnp.float32)
+        out[0, g] = both[:half]
+        out[1, g] = both[half:]
+
+    right_side(0, stacks.at[0])
+
+    def step(g, carry):
+        right_side(g, stacks.at[lax.rem(g, 2)])
+        left_side(g - 1, stacks.at[lax.rem(g - 1, 2)])
+        return carry
+
+    lax.fori_loop(1, count, step, 0)
+    left_side(count - 1, stacks.at[(count - 1) % 2])
+
+
+def couple(slots, weights, across, halves, pieces):
+    count, terms, width, _ = across.shape
+    size, half, _ = pieces[0].shape
+    inside = pl.BlockSpec(memory_space=pltpu.VMEM)
+    scalars = pl.BlockSpec(memory_space=pltpu.SMEM)
+    return pl.pallas_call(
+        couple_kernel,
+        in_specs=[scalars, scalars] + [inside] * (2 + len(pieces)),
+        out_specs=inside,
+        out_shape=jax.ShapeDtypeStruct((2, count, half, width), jnp.float32),
+        scratch_shapes=[
+            pltpu.VMEM((len(pieces) * size, half, width), jnp.bfloat16),
+            pltpu.VMEM((2, terms * half, width), jnp.bfloat16),
+        ],
+        compiler_params=pltpu.CompilerParams(vmem_limit_bytes=24 * 1024 * 1024),
         name="couple",
-    )(slots, side, weights, low, here, high, over)
+    )(slots, weights, across, halves, *pieces)
 
 
 def products_kernel(scale, parts, mask, *refs):
@@ -185,7 +241,8 @@
     frag = count * lax.axis_size("pair")
     cells = frag * lax.axis_size("chain") * width * width
     sides = jnp.reshape(side, (1,)).astype(jnp.int32)
-    own = masked(sides, ranks, amplitudes)
+    near = lax.axis_size("pair") // 2
+    own, copies = masked(sides, ranks, amplitudes, near)
     columns = jnp.arange(width, dtype=jnp.int32)
     rows_here = first_row + jnp.arange(half, dtype=jnp.int32)
     live_cols = columns[None, :] < ranks[:, None]
@@ -193,25 +250,34 @@
     mask = (live_rows[:, :, None] & live_cols[:, None, :]).astype(jnp.float32)
     energy_rows = lax.dynamic_slice_in_dim(pno_energies, first_row, half, 1)
     denom = energy_rows[:, :, None] + pno_energies[:, None, :] - pair_shift[:, None, None]
-    slots = (neighbours - (chain_pos - 1) * frag).reshape(-1)
+    within = neighbours % frag
+    place = within // count
+    turn = (place - lax.axis_index("pair")) % 2
+    piece_no = 2 * (neighbours // frag - chain_pos + 1) + turn
+    slots = ((piece_no * near + place // 2) * count + within % count).reshape(-1)
     weights = coupling.reshape(-1)
     over = pltpu.with_memory_space_constraint(intersections, pltpu.HBM)
 
-    def coupled_parts(piece):
-        low, here, high = spread(piece)
-        parts = couple(slots, sides, weights, low, here, high, over)
+    kept = []
+
+    def coupled_parts(copies):
+        pieces = spread(copies)
+        if not kept:
+            kept.extend(arrange(sides, pieces[2], over))
+        parts = couple(slots, weights, *kept, pieces)
         return lax.all_to_all(parts, "pno", 0, 0, tiled=True)
 
-    parts = coupled_parts(own)
+    parts = coupled_parts(copies)
     ints = integrals.astype(jnp.float32)
     terms = [mask * (ints + (parts[0] + parts[1]) - denom * own.astype(jnp.float32))]
     for step_no in range(1, ITERS):
-        parts = coupled_parts((terms[-1] / denom).astype(jnp.bfloat16))
+        piece = (terms[-1] / denom).astype(jnp.bfloat16)
+        parts = coupled_parts(jnp.broadcast_to(piece, (near, *piece.shape)))
         if step_no + 1 < ITERS:
             terms.append(mask * (parts[0] + parts[1]) - terms[-1])
     last, sums = products(cells**-0.5, parts, mask, terms)
-    sums = jnp.sum(copies_of_all(sums, ("pair", "pno")), axis=0, keepdims=True)[0]
-    return tuple(finish(copies_of_all(sums, ("chain",)), own, denom, terms + [last]))
+    sums = jnp.sum(copies_of_all(sums, ("chain", "pno")), axis=0)
+    return tuple(finish(copies_of_all(sums, ("pair",)), own, denom, terms + [last]))
 
 
 def solution(mesh):

time: 280 us -> 246 us (0.88)
  waiting for transfers between devices: 86.1 us -> 51.5 us
  starting transfers between devices: 29.4 us -> 50.3 us
  Pallas kernels: 35.8 us -> 25.9 us
  blocking collectives: 117 us -> 109 us
    all_to_all x4 -> x2, blocking collectives: 104 us -> 57.2 us  [copies_of_all(): return lax.all_to_all(copies, axes, 0, 0, tiled=True)]
    all_to_all x0 -> x2, blocking collectives: none -> 38.6 us  [spread(): lax.all_to_all(copies, 'pair', 0, 0, tiled=True, axis_index_groups=groups)]
    ppermute x6 -> x15, waiting for transfers between devices: 62.9 us -> 38.6 us  [shifted(): return lax.ppermute(value, axis, pairs)]
    ppermute x6 -> x15, starting transfers between devices: 22.1 us -> 43 us  [shifted(): return lax.ppermute(value, axis, pairs)]
    all_to_all x1, waiting for transfers between devices: 23.2 us -> 12.9 us  [spread(): lax.all_to_all(copies, 'pair', 0, 0, tiled=True, axis_index_groups=groups)]
    pallas_call x3 -> x4, Pallas kernels: 29.1 us -> 19.1 us  [the longest x3 13.5 us: couple(): pl.pallas_call(couple_kernel, in_specs=[scalars, scalars] + [inside] * (2...]
  transfers between devices with their start and end apart: 7 -> 16, of which waited for: 7 -> 12; matrix products, arithmetic and copies ran while one was open for 2% -> 2% of each run, Pallas kernels for 0% -> 2%
where the time goes in v2:
time: 246 us; the launch traced here: 244 us
  blocking collectives  109 us (44%)
  waiting for transfers between devices  51.5 us (21%)
  starting transfers between devices  50.3 us (20%)
  Pallas kernels  25.9 us (11%)
  other arithmetic  4.71 us (2%)
    all_to_all x2, blocking collectives, copies_of_all(): return lax.all_to_all(copies, axes, 0, 0, tiled=True)  57.2 us
    ppermute x15, starting transfers between devices, shifted(): return lax.ppermute(value, axis, pairs)  43 us
    all_to_all x2, blocking collectives, spread(): lax.all_to_all(copies, 'pair', 0, 0, tiled=True, axis_index_groups=groups)  38.6 us
    ppermute x15, waiting for transfers between devices, shifted(): return lax.ppermute(value, axis, pairs)  38.6 us
    pallas_call x3, Pallas kernels, couple(): pl.pallas_call(couple_kernel, in_specs=[scalars, scalars] + [inside] * (2...  13.5 us
    all_to_all x3, blocking collectives, coupled_parts(): return lax.all_to_all(parts, 'pno', 0, 0, tiled=True)  12.9 us
    all_to_all x1, waiting for transfers between devices, spread(): lax.all_to_all(copies, 'pair', 0, 0, tiled=True, axis_index_groups=groups)  12.9 us
    all_to_all x1, starting transfers between devices, spread(): lax.all_to_all(copies, 'pair', 0, 0, tiled=True, axis_index_groups=groups)  7.31 us
  transfers between devices with their start and end apart: 16, of which 12 were waited for; matrix products, arithmetic and copies ran while one was open for 2% of the time, Pallas kernels for 2%

profile of v2, /device:TPU:80, one launch (start us, length us, event | category | flops | bytes accessed | tf_op | source)
XLA Modules:
  0.0 244.5 jit_solution(12084567349984578342)
XLA Ops:
  0.6 2.4 masked.1
  3.0 7.3 %all-to-all-start = ((bf16[4,6,64,128]{3,2,1,0:T(8,128)(2,1)}), bf16[4,6,64,128]{3,2,1,0:T(8,128)(2,1)S(1)}, u32[]{:S(2)}, u32[]{:S(2)}) async-start(bf16[4,6,64,128]{3,2,1,0:T(8,128)(2,1)} %get-tuple-element.8), calls=%async_computation | async-start | bytes 786432 | tf_op jit(solution)/shard_map/all_to_all | solution.py:29
  10.3 12.9 %all-to-all-done = bf16[4,6,64,128]{3,2,1,0:T(8,128)(2,1)S(1)} async-done(((bf16[4,6,64,128]{3,2,1,0:T(8,128)(2,1)}), bf16[4,6,64,128]{3,2,1,0:T(8,128)(2,1)S(1)}, u32[]{:S(2)}, u32[]{:S(2)}) %all-to-all-start) | async-done | bytes 393248 | tf_op jit(solution)/shard_map/all_to_all | solution.py:29
  23.2 6.0 %collective-permute-start = (bf16[24,64,128]{2,1,0:T(8,128)(2,1)S(1)}, bf16[24,64,128]{2,1,0:T(8,128)(2,1)S(1)}, u32[]{:S(2)}, u32[]{:S(2)}) collective-permute-start(bf16[24,64,128]{2,1,0:T(8,128)(2,1)S(1)} %bitcast.20), channel_id=1, source_target_pairs={{0,16},{16,32},{32,48},{48,64},{64,80},{80,96},{96,112},{112,128},... | collective-permute-start | bytes 1179656 | tf_op jit(solution)/shard_map/ppermute | solution.py:15
  33.7 2.4 collective-permute-start.2
  36.1 4.4 %collective-permute-start.1 = (bf16[24,64,128]{2,1,0:T(8,128)(2,1)S(1)}, bf16[24,64,128]{2,1,0:T(8,128)(2,1)S(1)}, u32[]{:S(2)}, u32[]{:S(2)}) collective-permute-start(bf16[24,64,128]{2,1,0:T(8,128)(2,1)S(1)} %collective-permute-done.refs_0_), channel_id=1, source_target_pairs={{0,2},{2,4},{4,6},{6,8},{8,10},{10,12},{12,14},{14,0},{1,3},{3,5},... | collective-permute-start | bytes 1179656 | tf_op jit(solution)/shard_map/ppermute | solution.py:15
  42.0 2.7 %collective-permute-start.4 = (bf16[24,64,128]{2,1,0:T(8,128)(2,1)S(1)}, bf16[24,64,128]{2,1,0:T(8,128)(2,1)S(1)}, u32[]{:S(2)}, u32[]{:S(2)}) collective-permute-start(bf16[24,64,128]{2,1,0:T(8,128)(2,1)S(1)} %collective-permute-done.3.refs_4_), channel_id=1, source_target_pairs={{0,14},{2,0},{4,2},{6,4},{8,6},{10,8},{12,10},{14,12},{1,15},{3,1}... | collective-permute-start | bytes 1179656 | tf_op jit(solution)/shard_map/ppermute | solution.py:15
  45.4 5.7 %arrange.1 = (bf16[6,32,128,128]{3,2,1,0:T(8,128)(2,1)S(1)}, bf16[6,128,2048]{2,1,0:T(8,128)(2,1)S(1)}) custom-call(s32[1]{0:T(128)} %bitcast.side, bf16[24,64,128]{2,1,0:T(8,128)(2,1)S(1)} %bitcast.23, bf16[6,32,128,128]{3,2,1,0:T(8,128)(2,1)} %over.1), custom_call_target="tpu_custom_call" | custom-call | flops 1000000000 | bytes 9437184 | tf_op jit(solution)/shard_map/arrange/pallas_call | solution.py:97
  51.1 2.5 %collective-permute-done.1.refs_1_ = bf16[24,64,128]{2,1,0:T(8,128)(2,1)S(1)} collective-permute-done((bf16[24,64,128]{2,1,0:T(8,128)(2,1)S(1)}, bf16[24,64,128]{2,1,0:T(8,128)(2,1)S(1)}, u32[]{:S(2)}, u32[]{:S(2)}) %collective-permute-start.1) | collective-permute-done | bytes 393248 | tf_op jit(solution)/shard_map/ppermute | solution.py:15
  53.6 4.5 %couple.3 = f32[2,6,64,128]{3,2,1,0:T(8,128)S(1)} custom-call(s32[192]{0:T(256)S(1)} %reshape.78.slots, f32[192]{0:T(256)S(1)} %reshape.79.weights, bf16[6,32,128,128]{3,2,1,0:T(8,128)(2,1)S(1)} %get-tuple-element.9.across, bf16[6,128,2048]{2,1,0:T(8,128)(2,1)S(1)} %get-tuple-element.10.halves, bf16[24,64,128]{2,1,0:T(8,128)(2,1)S(1)} %collective-permute-done.refs_0_, ...), custom_call_target="tpu_custom_call" | custom-call | tf_op jit(solution)/shard_map/couple/pallas_call | solution.py:159
  58.1 4.1 %all_to_all.40 = f32[2,6,64,128]{3,2,1,0:T(8,128)S(1)} all-to-all(f32[2,6,64,128]{3,2,1,0:T(8,128)S(1)} %couple.3), channel_id=1, replica_groups=mesh['job'=2,'chain'=16,'pair'=8,'pno'=2] {'pno'}, dimensions={0} | all-to-all | bytes 786432 | tf_op jit(solution)/shard_map/all_to_all | solution.py:268
  63.1 19.5 %all_to_all.41 = bf16[4,6,64,128]{3,2,1,0:T(8,128)(2,1)S(1)} all-to-all(bf16[4,6,64,128]{3,2,1,0:T(8,128)(2,1)S(1)} %broadcast_in_dim.8), channel_id=1, replica_groups={{0,4,8,12},{2,6,10,14},{1,5,9,13},{3,7,11,15},{16,20,24,28},{18,22,26,3..., dimensions={0} | all-to-all | bytes 786432 | tf_op jit(solution)/shard_map/all_to_all | solution.py:29
  82.7 5.9 %collective-permute-start.5 = (bf16[24,64,128]{2,1,0:T(8,128)(2,1)S(1)}, bf16[24,64,128]{2,1,0:T(8,128)(2,1)S(1)}, u32[]{:S(2)}, u32[]{:S(2)}) collective-permute-start(bf16[24,64,128]{2,1,0:T(8,128)(2,1)S(1)} %bitcast.29), channel_id=1, source_target_pairs={{0,16},{16,32},{32,48},{48,64},{64,80},{80,96},{96,112},{112,128},... | collective-permute-start | bytes 1179656 | tf_op jit(solution)/shard_map/ppermute | solution.py:15
  89.9 2.0 collective-permute-start.7
  91.8 4.0 %collective-permute-done.5.refs_0_ = bf16[24,64,128]{2,1,0:T(8,128)(2,1)S(1)} collective-permute-done((bf16[24,64,128]{2,1,0:T(8,128)(2,1)S(1)}, bf16[24,64,128]{2,1,0:T(8,128)(2,1)S(1)}, u32[]{:S(2)}, u32[]{:S(2)}) %collective-permute-start.5) | collective-permute-done | bytes 393248 | tf_op jit(solution)/shard_map/ppermute | solution.py:15
  97.7 5.7 %collective-permute-done.8.refs_4_ = bf16[24,64,128]{2,1,0:T(8,128)(2,1)S(1)} collective-permute-done((bf16[24,64,128]{2,1,0:T(8,128)(2,1)S(1)}, bf16[24,64,128]{2,1,0:T(8,128)(2,1)S(1)}, u32[]{:S(2)}, u32[]{:S(2)}) %collective-permute-start.8) | collective-permute-done | bytes 393248 | tf_op jit(solution)/shard_map/ppermute | solution.py:15
  105.4 5.5 %collective-permute-done.6.refs_1_ = bf16[24,64,128]{2,1,0:T(8,128)(2,1)S(1)} collective-permute-done((bf16[24,64,128]{2,1,0:T(8,128)(2,1)S(1)}, bf16[24,64,128]{2,1,0:T(8,128)(2,1)S(1)}, u32[]{:S(2)}, u32[]{:S(2)}) %collective-permute-start.6) | collective-permute-done | bytes 393248 | tf_op jit(solution)/shard_map/ppermute | solution.py:15
  110.9 3.2 %collective-permute-done.9.refs_5_ = bf16[24,64,128]{2,1,0:T(8,128)(2,1)S(1)} collective-permute-done((bf16[24,64,128]{2,1,0:T(8,128)(2,1)S(1)}, bf16[24,64,128]{2,1,0:T(8,128)(2,1)S(1)}, u32[]{:S(2)}, u32[]{:S(2)}) %collective-permute-start.9) | collective-permute-done | bytes 393248 | tf_op jit(solution)/shard_map/ppermute | solution.py:15
  114.1 4.5 %couple.4 = f32[2,6,64,128]{3,2,1,0:T(8,128)S(1)} custom-call(s32[192]{0:T(256)S(1)} %reshape.78.slots, f32[192]{0:T(256)S(1)} %reshape.79.weights, bf16[6,32,128,128]{3,2,1,0:T(8,128)(2,1)S(1)} %get-tuple-element.9.across, bf16[6,128,2048]{2,1,0:T(8,128)(2,1)S(1)} %get-tuple-element.10.halves, bf16[24,64,128]{2,1,0:T(8,128)(2,1)S(1)} %collective-permute-done.5.refs_0_, ...), custom_call_target="tpu_custom_call" | custom-call | tf_op jit(solution)/shard_map/couple/pallas_call | solution.py:159
  118.6 4.1 %all_to_all.42 = f32[2,6,64,128]{3,2,1,0:T(8,128)S(1)} all-to-all(f32[2,6,64,128]{3,2,1,0:T(8,128)S(1)} %couple.4), channel_id=1, replica_groups=mesh['job'=2,'chain'=16,'pair'=8,'pno'=2] {'pno'}, dimensions={0} | all-to-all | bytes 786432 | tf_op jit(solution)/shard_map/all_to_all | solution.py:268
  123.6 19.0 %all_to_all.43 = bf16[4,6,64,128]{3,2,1,0:T(8,128)(2,1)S(1)} all-to-all(bf16[4,6,64,128]{3,2,1,0:T(8,128)(2,1)S(1)} %broadcast_in_dim.9), channel_id=1, replica_groups={{0,4,8,12},{2,6,10,14},{1,5,9,13},{3,7,11,15},{16,20,24,28},{18,22,26,3..., dimensions={0} | all-to-all | bytes 786432 | tf_op jit(solution)/shard_map/all_to_all | solution.py:29
  142.7 6.0 %collective-permute-start.10 = (bf16[24,64,128]{2,1,0:T(8,128)(2,1)S(1)}, bf16[24,64,128]{2,1,0:T(8,128)(2,1)S(1)}, u32[]{:S(2)}, u32[]{:S(2)}) collective-permute-start(bf16[24,64,128]{2,1,0:T(8,128)(2,1)S(1)} %bitcast.25), channel_id=1, source_target_pairs={{0,16},{16,32},{32,48},{48,64},{64,80},{80,96},{96,112},{112,128},... | collective-permute-start | bytes 1179656 | tf_op jit(solution)/shard_map/ppermute | solution.py:15
  152.0 3.8 %collective-permute-done.10.refs_0_ = bf16[24,64,128]{2,1,0:T(8,128)(2,1)S(1)} collective-permute-done((bf16[24,64,128]{2,1,0:T(8,128)(2,1)S(1)}, bf16[24,64,128]{2,1,0:T(8,128)(2,1)S(1)}, u32[]{:S(2)}, u32[]{:S(2)}) %collective-permute-start.10) | collective-permute-done | bytes 393248 | tf_op jit(solution)/shard_map/ppermute | solution.py:15
  157.7 4.6 %collective-permute-done.13.refs_4_ = bf16[24,64,128]{2,1,0:T(8,128)(2,1)S(1)} collective-permute-done((bf16[24,64,128]{2,1,0:T(8,128)(2,1)S(1)}, bf16[24,64,128]{2,1,0:T(8,128)(2,1)S(1)}, u32[]{:S(2)}, u32[]{:S(2)}) %collective-permute-start.13) | collective-permute-done | bytes 393248 | tf_op jit(solution)/shard_map/ppermute | solution.py:15
  165.1 5.7 %collective-permute-done.11.refs_1_ = bf16[24,64,128]{2,1,0:T(8,128)(2,1)S(1)} collective-permute-done((bf16[24,64,128]{2,1,0:T(8,128)(2,1)S(1)}, bf16[24,64,128]{2,1,0:T(8,128)(2,1)S(1)}, u32[]{:S(2)}, u32[]{:S(2)}) %collective-permute-start.11) | collective-permute-done | bytes 393248 | tf_op jit(solution)/shard_map/ppermute | solution.py:15
  170.9 2.0 collective-permute-done.14.refs_5_
  172.9 4.5 %couple.5 = f32[2,6,64,128]{3,2,1,0:T(8,128)S(1)} custom-call(s32[192]{0:T(256)S(1)} %reshape.78.slots, f32[192]{0:T(256)S(1)} %reshape.79.weights, bf16[6,32,128,128]{3,2,1,0:T(8,128)(2,1)S(1)} %get-tuple-element.9.across, bf16[6,128,2048]{2,1,0:T(8,128)(2,1)S(1)} %get-tuple-element.10.halves, bf16[24,64,128]{2,1,0:T(8,128)(2,1)S(1)} %collective-permute-done.10.refs_0_, ...), custom_call_target="tpu_custom_call" | custom-call | tf_op jit(solution)/shard_map/couple/pallas_call | solution.py:159
  177.4 4.8 %all_to_all.44.refs_0_ = f32[2,6,64,128]{3,2,1,0:T(8,128)} all-to-all(f32[2,6,64,128]{3,2,1,0:T(8,128)S(1)} %couple.5), channel_id=1, replica_groups=mesh['job'=2,'chain'=16,'pair'=8,'pno'=2] {'pno'}, dimensions={0} | all-to-all | bytes 786432 | tf_op jit(solution)/shard_map/all_to_all | solution.py:268
  182.2 2.0 products.1
  184.9 44.8 %all_to_all.45 = f32[32,1,128]{2,1,0:T(1,128)S(1)} all-to-all(f32[32,1,128]{2,1,0:T(1,128)S(1)} %broadcast_in_dim.10), channel_id=1, replica_groups=mesh['job'=2,'chain'=16,'pair'=8,'pno'=2] {'chain','pno'}, dimensions={0} | all-to-all | bytes 32768 | tf_op jit(solution)/shard_map/all_to_all | solution.py:23
  229.7 12.5 %all_to_all.46.copies = f32[8,1,128]{2,1,0:T(1,128)} all-to-all(f32[8,1,128]{2,1,0:T(1,128)S(1)} %broadcast_in_dim.11), channel_id=1, replica_groups=mesh['job'=2,'chain'=16,'pair'=8,'pno'=2] {'pair'}, dimensions={0} | all-to-all | bytes 8192 | tf_op jit(solution)/shard_map/all_to_all | solution.py:23
  242.1 2.4 finish.1
  (39 shorter events, 22.4 us)
Async XLA Ops:
  3.0 20.2 %all-to-all-start = ((bf16[4,6,64,128]{3,2,1,0:T(8,128)(2,1)}), bf16[4,6,64,128]{3,2,1,0:T(8,128)(2,1)S(1)}, u32[]{:S(2)}, u32[]{:S(2)}) async-start(bf16[4,6,64,128]{3,2,1,0:T(8,128)(2,1)} %get-tuple-element.8), calls=%async_computation | async-start | bytes 786432 | tf_op jit(solution)/shard_map/all_to_all | solution.py:29
  23.2 12.8 %collective-permute-start = (bf16[24,64,128]{2,1,0:T(8,128)(2,1)S(1)}, bf16[24,64,128]{2,1,0:T(8,128)(2,1)S(1)}, u32[]{:S(2)}, u32[]{:S(2)}) collective-permute-start(bf16[24,64,128]{2,1,0:T(8,128)(2,1)S(1)} %bitcast.20), channel_id=1, source_target_pairs={{0,16},{16,32},{32,48},{48,64},{64,80},{80,96},{96,112},{112,128},... | collective-permute-start | bytes 1179656 | tf_op jit(solution)/shard_map/ppermute | solution.py:15
  29.3 12.7 %collective-permute-start.3 = (bf16[24,64,128]{2,1,0:T(8,128)(2,1)S(1)}, bf16[24,64,128]{2,1,0:T(8,128)(2,1)S(1)}, u32[]{:S(2)}, u32[]{:S(2)}) collective-permute-start(bf16[24,64,128]{2,1,0:T(8,128)(2,1)S(1)} %bitcast.21), channel_id=1, source_target_pairs={{16,0},{32,16},{48,32},{64,48},{80,64},{96,80},{112,96},{128,112},... | collective-permute-start | bytes 1179656 | tf_op jit(solution)/shard_map/ppermute | solution.py:15
  33.7 17.4 %collective-permute-start.2 = (bf16[24,64,128]{2,1,0:T(8,128)(2,1)S(1)}, bf16[24,64,128]{2,1,0:T(8,128)(2,1)S(1)}, u32[]{:S(2)}, u32[]{:S(2)}) collective-permute-start(bf16[24,64,128]{2,1,0:T(8,128)(2,1)S(1)} %bitcast.22), channel_id=1, source_target_pairs={{0,2},{2,4},{4,6},{6,8},{8,10},{10,12},{12,14},{14,0},{1,3},{3,5},... | collective-permute-start | bytes 1179656 | tf_op jit(solution)/shard_map/ppermute | solution.py:15
  36.1 17.6 %collective-permute-start.1 = (bf16[24,64,128]{2,1,0:T(8,128)(2,1)S(1)}, bf16[24,64,128]{2,1,0:T(8,128)(2,1)S(1)}, u32[]{:S(2)}, u32[]{:S(2)}) collective-permute-start(bf16[24,64,128]{2,1,0:T(8,128)(2,1)S(1)} %collective-permute-done.refs_0_), channel_id=1, source_target_pairs={{0,2},{2,4},{4,6},{6,8},{8,10},{10,12},{12,14},{14,0},{1,3},{3,5},... | collective-permute-start | bytes 1179656 | tf_op jit(solution)/shard_map/ppermute | solution.py:15
  42.0 11.7 %collective-permute-start.4 = (bf16[24,64,128]{2,1,0:T(8,128)(2,1)S(1)}, bf16[24,64,128]{2,1,0:T(8,128)(2,1)S(1)}, u32[]{:S(2)}, u32[]{:S(2)}) collective-permute-start(bf16[24,64,128]{2,1,0:T(8,128)(2,1)S(1)} %collective-permute-done.3.refs_4_), channel_id=1, source_target_pairs={{0,14},{2,0},{4,2},{6,4},{8,6},{10,8},{12,10},{14,12},{1,15},{3,1}... | collective-permute-start | bytes 1179656 | tf_op jit(solution)/shard_map/ppermute | solution.py:15
  53.6 8.6 %copy-start.1 = (bf16[6,64,128]{2,1,0:T(8,128)(2,1)S(1)}, bf16[6,64,128]{2,1,0:T(8,128)(2,1)}, u32[]{:S(2)}) copy-start(bf16[6,64,128]{2,1,0:T(8,128)(2,1)} %get-tuple-element.11.own) | copy-start | bytes 294916
  53.6 8.6 %copy-start.2 = (bf16[6,64,128]{2,1,0:T(8,128)(2,1)S(1)}, bf16[6,64,128]{2,1,0:T(8,128)(2,1)}, u32[]{:S(2)}) copy-start(bf16[6,64,128]{2,1,0:T(8,128)(2,1)} %param.9) | copy-start | bytes 294916
  53.6 8.6 %copy-start.3 = (f32[6,128]{1,0:T(8,128)S(1)}, f32[6,128]{1,0:T(8,128)}, u32[]{:S(2)}) copy-start(f32[6,128]{1,0:T(8,128)} %param.12) | copy-start | bytes 9220
  53.6 8.6 %copy-start.4 = (f32[6]{0:T(128)S(1)}, f32[6]{0:T(128)}, u32[]{:S(2)}) copy-start(f32[6]{0:T(128)} %param.13) | copy-start | bytes 76
  63.1 59.6 %copy-start = (f32[6,64,128]{2,1,0:T(8,128)}, f32[6,64,128]{2,1,0:T(8,128)S(1)}, u32[]{:S(2)}) copy-start(f32[6,64,128]{2,1,0:T(8,128)S(1)} %get-tuple-element.17.refs_2_.refs_0_) | copy-start | bytes 589828
  82.7 13.1 %collective-permute-start.5 = (bf16[24,64,128]{2,1,0:T(8,128)(2,1)S(1)}, bf16[24,64,128]{2,1,0:T(8,128)(2,1)S(1)}, u32[]{:S(2)}, u32[]{:S(2)}) collective-permute-start(bf16[24,64,128]{2,1,0:T(8,128)(2,1)S(1)} %bitcast.29), channel_id=1, source_target_pairs={{0,16},{16,32},{32,48},{48,64},{64,80},{80,96},{96,112},{112,128},... | collective-permute-start | bytes 1179656 | tf_op jit(solution)/shard_map/ppermute | solution.py:15
  88.6 14.9 %collective-permute-start.8 = (bf16[24,64,128]{2,1,0:T(8,128)(2,1)S(1)}, bf16[24,64,128]{2,1,0:T(8,128)(2,1)S(1)}, u32[]{:S(2)}, u32[]{:S(2)}) collective-permute-start(bf16[24,64,128]{2,1,0:T(8,128)(2,1)S(1)} %bitcast.30), channel_id=1, source_target_pairs={{16,0},{32,16},{48,32},{64,48},{80,64},{96,80},{112,96},{128,112},... | collective-permute-start | bytes 1179656 | tf_op jit(solution)/shard_map/ppermute | solution.py:15
  89.9 15.6 %collective-permute-start.7 = (bf16[24,64,128]{2,1,0:T(8,128)(2,1)S(1)}, bf16[24,64,128]{2,1,0:T(8,128)(2,1)S(1)}, u32[]{:S(2)}, u32[]{:S(2)}) collective-permute-start(bf16[24,64,128]{2,1,0:T(8,128)(2,1)S(1)} %bitcast.31), channel_id=1, source_target_pairs={{0,2},{2,4},{4,6},{6,8},{8,10},{10,12},{12,14},{14,0},{1,3},{3,5},... | collective-permute-start | bytes 1179656 | tf_op jit(solution)/shard_map/ppermute | solution.py:15
  95.8 15.1 %collective-permute-start.6 = (bf16[24,64,128]{2,1,0:T(8,128)(2,1)S(1)}, bf16[24,64,128]{2,1,0:T(8,128)(2,1)S(1)}, u32[]{:S(2)}, u32[]{:S(2)}) collective-permute-start(bf16[24,64,128]{2,1,0:T(8,128)(2,1)S(1)} %collective-permute-done.5.refs_0_), channel_id=1, source_target_pairs={{0,2},{2,4},{4,6},{6,8},{8,10},{10,12},{12,14},{14,0},{1,3},{3,5},... | collective-permute-start | bytes 1179656 | tf_op jit(solution)/shard_map/ppermute | solution.py:15
  103.5 10.6 %collective-permute-start.9 = (bf16[24,64,128]{2,1,0:T(8,128)(2,1)S(1)}, bf16[24,64,128]{2,1,0:T(8,128)(2,1)S(1)}, u32[]{:S(2)}, u32[]{:S(2)}) collective-permute-start(bf16[24,64,128]{2,1,0:T(8,128)(2,1)S(1)} %collective-permute-done.8.refs_4_), channel_id=1, source_target_pairs={{0,14},{2,0},{4,2},{6,4},{8,6},{10,8},{12,10},{14,12},{1,15},{3,1}... | collective-permute-start | bytes 1179656 | tf_op jit(solution)/shard_map/ppermute | solution.py:15
  142.7 13.1 %collective-permute-start.10 = (bf16[24,64,128]{2,1,0:T(8,128)(2,1)S(1)}, bf16[24,64,128]{2,1,0:T(8,128)(2,1)S(1)}, u32[]{:S(2)}, u32[]{:S(2)}) collective-permute-start(bf16[24,64,128]{2,1,0:T(8,128)(2,1)S(1)} %bitcast.25), channel_id=1, source_target_pairs={{0,16},{16,32},{32,48},{48,64},{64,80},{80,96},{96,112},{112,128},... | collective-permute-start | bytes 1179656 | tf_op jit(solution)/shard_map/ppermute | solution.py:15
  148.7 13.6 %collective-permute-start.13 = (bf16[24,64,128]{2,1,0:T(8,128)(2,1)S(1)}, bf16[24,64,128]{2,1,0:T(8,128)(2,1)S(1)}, u32[]{:S(2)}, u32[]{:S(2)}) collective-permute-start(bf16[24,64,128]{2,1,0:T(8,128)(2,1)S(1)} %bitcast.26), channel_id=1, source_target_pairs={{16,0},{32,16},{48,32},{64,48},{80,64},{96,80},{112,96},{128,112},... | collective-permute-start | bytes 1179656 | tf_op jit(solution)/shard_map/ppermute | solution.py:15
  150.0 15.1 %collective-permute-start.12 = (bf16[24,64,128]{2,1,0:T(8,128)(2,1)S(1)}, bf16[24,64,128]{2,1,0:T(8,128)(2,1)S(1)}, u32[]{:S(2)}, u32[]{:S(2)}) collective-permute-start(bf16[24,64,128]{2,1,0:T(8,128)(2,1)S(1)} %bitcast.27), channel_id=1, source_target_pairs={{0,2},{2,4},{4,6},{6,8},{8,10},{10,12},{12,14},{14,0},{1,3},{3,5},... | collective-permute-start | bytes 1179656 | tf_op jit(solution)/shard_map/ppermute | solution.py:15
  155.7 15.1 %collective-permute-start.11 = (bf16[24,64,128]{2,1,0:T(8,128)(2,1)S(1)}, bf16[24,64,128]{2,1,0:T(8,128)(2,1)S(1)}, u32[]{:S(2)}, u32[]{:S(2)}) collective-permute-start(bf16[24,64,128]{2,1,0:T(8,128)(2,1)S(1)} %collective-permute-done.10.refs_0_), channel_id=1, source_target_pairs={{0,2},{2,4},{4,6},{6,8},{8,10},{10,12},{12,14},{14,0},{1,3},{3,5},... | collective-permute-start | bytes 1179656 | tf_op jit(solution)/shard_map/ppermute | solution.py:15
  162.2 10.6 %collective-permute-start.14 = (bf16[24,64,128]{2,1,0:T(8,128)(2,1)S(1)}, bf16[24,64,128]{2,1,0:T(8,128)(2,1)S(1)}, u32[]{:S(2)}, u32[]{:S(2)}) collective-permute-start(bf16[24,64,128]{2,1,0:T(8,128)(2,1)S(1)} %collective-permute-done.13.refs_4_), channel_id=1, source_target_pairs={{0,14},{2,0},{4,2},{6,4},{8,6},{10,8},{12,10},{14,12},{1,15},{3,1}... | collective-permute-start | bytes 1179656 | tf_op jit(solution)/shard_map/ppermute | solution.py:15

commit v3 on v2

--- a/solution.py
+++ b/solution.py
@@ -9,30 +9,34 @@
 PRODUCTS = [(i, j) for i in range(ITERS) for j in range(i + 1)]
 
 
-def shifted(value, axis, step, around=False):
+def swapped(value, axis, first, around):
     count = lax.axis_size(axis)
-    pairs = [(i, (i + step) % count) for i in range(count) if around or 0 <= i + step < count]
+    pairs = []
+    for left in range(first, count, 2):
+        if left + 1 < count or around:
+            right = (left + 1) % count
+            pairs += [(left, right), (right, left)]
     return lax.ppermute(value, axis, pairs)
 
 
-def copies_of_all(value, axes):
-    count = 1
-    for axis in axes:
-        count *= lax.axis_size(axis)
-    copies = jnp.broadcast_to(value, (count, *value.shape))
-    return lax.all_to_all(copies, axes, 0, 0, tiled=True)
-
-
-def spread(copies):
+def joined(value, step, first):
     count = lax.axis_size("pair")
-    groups = [list(range(first, count, 2)) for first in range(2)]
-    near = lax.all_to_all(copies, "pair", 0, 0, tiled=True, axis_index_groups=groups)
-    near = near.reshape(-1, *copies.shape[2:])
-    low, high = shifted(near, "chain", 1), shifted(near, "chain", -1)
-    other = shifted(near, "pair", 1, around=True)
-    low_other = shifted(low, "pair", 1, around=True)
-    high_other = shifted(high, "pair", -1, around=True)
-    return low, low_other, near, other, high, high_other
+    groups = []
+    for start in range(first, first + count, 2 * step):
+        for parity in range(step):
+            left, right = (start + parity) % count, (start + step + parity) % count
+            groups.append(sorted([left, right]))
+    return lax.all_gather(value, "pair", axis=0, tiled=True, axis_index_groups=groups)
+
+
+def spread(piece):
+    near = joined(joined(piece, 2, 0), 2, 2)
+    ahead = swapped(near, "chain", 0, False)
+    behind = swapped(near, "chain", 1, False)
+    other = swapped(near, "pair", 0, True)
+    ahead_other = swapped(ahead, "pair", 1, True)
+    behind_other = swapped(behind, "pair", 0, True)
+    return near, other, ahead, ahead_other, behind, behind_other
 
 
 def live_cells(rank, first, half, width):
@@ -41,18 +45,15 @@
     return (rows < rank) & (columns < rank)
 
 
-def start_kernel(side, ranks, amplitudes, own, copies):
+def start_kernel(side, ranks, amplitudes, own):
     count, half, width = amplitudes.shape
     for g in range(count):
         live = live_cells(ranks[g], side[0] * half, half, width)
         block = jnp.where(live, amplitudes[g].astype(jnp.float32), 0.0)
-        block = block.astype(jnp.bfloat16)
-        own[g] = block
-        for copy in range(copies.shape[0]):
-            copies[copy, g] = block
-
-
-def masked(side, ranks, amplitudes, count):
+        own[g] = block.astype(jnp.bfloat16)
+
+
+def masked(side, ranks, amplitudes):
     shape = amplitudes.shape
     return pl.pallas_call(
         start_kernel,
@@ -60,15 +61,10 @@
             num_scalar_prefetch=2,
             grid=(1,),
             in_specs=[pl.BlockSpec(shape, lambda i, *_: (0, 0, 0))],
-            out_specs=[
-                pl.BlockSpec(shape, lambda i, *_: (0, 0, 0)),
-                pl.BlockSpec((count, *shape), lambda i, *_: (0, 0, 0, 0)),
-            ],
-        ),
-        out_shape=(
-            jax.ShapeDtypeStruct(shape, jnp.bfloat16),
-            jax.ShapeDtypeStruct((count, *shape), jnp.bfloat16),
-        ),
+            out_specs=pl.BlockSpec(shape, lambda i, *_: (0, 0, 0)),
+        ),
+        out_shape=jax.ShapeDtypeStruct(shape, jnp.bfloat16),
+        compiler_params=pltpu.CompilerParams(vmem_limit_bytes=8 * 1024 * 1024),
         name="masked",
     )(side, ranks, amplitudes)
 
@@ -120,8 +116,8 @@
     )(side, after, over)
 
 
-def couple_kernel(slots, weights, across, halves, *refs):
-    pieces, (out, window, stacks) = refs[:-3], refs[-3:]
+def couple_kernel(side, slots, weights, across, halves, *refs):
+    pieces, (mine, theirs, window, stacks) = refs[:-4], refs[-4:]
     count, terms, width, _ = across.shape
     size, half, _ = pieces[0].shape
     for place, piece in enumerate(pieces):
@@ -137,8 +133,9 @@
 
     def left_side(g, stack):
         both = jnp.dot(halves[g], stack[...], preferred_element_type=jnp.float32)
-        out[0, g] = both[:half]
-        out[1, g] = both[half:]
+        upper = side[0] == 0
+        mine[g] = jnp.where(upper, both[:half], both[half:])
+        theirs[g] = jnp.where(upper, both[half:], both[:half])
 
     right_side(0, stacks.at[0])
 
@@ -151,46 +148,50 @@
     left_side(count - 1, stacks.at[(count - 1) % 2])
 
 
-def couple(slots, weights, across, halves, pieces):
+def couple(side, slots, weights, across, halves, pieces):
     count, terms, width, _ = across.shape
     size, half, _ = pieces[0].shape
     inside = pl.BlockSpec(memory_space=pltpu.VMEM)
     scalars = pl.BlockSpec(memory_space=pltpu.SMEM)
     return pl.pallas_call(
         couple_kernel,
-        in_specs=[scalars, scalars] + [inside] * (2 + len(pieces)),
-        out_specs=inside,
-        out_shape=jax.ShapeDtypeStruct((2, count, half, width), jnp.float32),
+        in_specs=[scalars] * 3 + [inside] * (2 + len(pieces)),
+        out_specs=[inside] * 2,
+        out_shape=[jax.ShapeDtypeStruct((count, half, width), jnp.float32)] * 2,
         scratch_shapes=[
             pltpu.VMEM((len(pieces) * size, half, width), jnp.bfloat16),
             pltpu.VMEM((2, terms * half, width), jnp.bfloat16),
         ],
         compiler_params=pltpu.CompilerParams(vmem_limit_bytes=24 * 1024 * 1024),
         name="couple",
-    )(slots, weights, across, halves, *pieces)
-
-
-def products_kernel(scale, parts, mask, *refs):
+    )(side, slots, weights, across, halves, *pieces)
+
+
+def products_kernel(scale, mine, theirs, mask, *refs):
     held, (last, sums) = refs[:-2], refs[-2:]
-    last[...] = mask[...] * (parts[0] + parts[1]) - held[-1][...]
+    last[...] = mask[...] * (mine[...] + theirs[...]) - held[-1][...]
     terms = [ref[...] * scale for ref in held] + [last[...] * scale]
-    lane = lax.broadcasted_iota(jnp.int32, sums.shape, 1)
+    lane = lax.broadcasted_iota(jnp.int32, sums.shape, 2)
     row = jnp.zeros(sums.shape, jnp.float32)
     for place, (i, j) in enumerate(PRODUCTS):
         row = jnp.where(lane == place, jnp.sum(terms[i] * terms[j]), row)
     sums[...] = row
 
 
-def products(scale, parts, mask, held):
+def products(scale, mine, theirs, mask, held, count):
     shape = mask.shape
+    inside = pl.BlockSpec(memory_space=pltpu.VMEM)
     return pl.pallas_call(
         lambda *refs: products_kernel(scale, *refs),
+        in_specs=[inside] * (3 + len(held)),
+        out_specs=(inside, inside),
         out_shape=(
             jax.ShapeDtypeStruct(shape, jnp.float32),
-            jax.ShapeDtypeStruct((1, shape[-1]), jnp.float32),
-        ),
+            jax.ShapeDtypeStruct((count, 1, shape[-1]), jnp.float32),
+        ),
+        compiler_params=pltpu.CompilerParams(vmem_limit_bytes=8 * 1024 * 1024),
         name="products",
-    )(parts, mask, *held)
+    )(mine, theirs, mask, *held)
 
 
 def finish_kernel(copies, own, denom, *refs):
@@ -226,7 +227,9 @@
             jax.ShapeDtypeStruct(own.shape, jnp.bfloat16),
             jax.ShapeDtypeStruct((ITERS,), jnp.float32),
         ),
+        in_specs=[pl.BlockSpec(memory_space=pltpu.VMEM)] * (3 + len(terms)),
         out_specs=(pl.BlockSpec(memory_space=pltpu.VMEM), pl.BlockSpec(memory_space=pltpu.SMEM)),
+        compiler_params=pltpu.CompilerParams(vmem_limit_bytes=8 * 1024 * 1024),
         name="finish",
     )(copies, own, denom, *terms)
 
@@ -241,8 +244,7 @@
     frag = count * lax.axis_size("pair")
     cells = frag * lax.axis_size("chain") * width * width
     sides = jnp.reshape(side, (1,)).astype(jnp.int32)
-    near = lax.axis_size("pair") // 2
-    own, copies = masked(sides, ranks, amplitudes, near)
+    own = masked(sides, ranks, amplitudes)
     columns = jnp.arange(width, dtype=jnp.int32)
     rows_here = first_row + jnp.arange(half, dtype=jnp.int32)
     live_cols = columns[None, :] < ranks[:, None]
@@ -253,31 +255,36 @@
     within = neighbours % frag
     place = within // count
     turn = (place - lax.axis_index("pair")) % 2
-    piece_no = 2 * (neighbours // frag - chain_pos + 1) + turn
+    offset = neighbours // frag - chain_pos
+    facing = 1 - 2 * (chain_pos % 2)
+    piece_no = 2 * jnp.where(offset == 0, 0, jnp.where(offset == facing, 1, 2)) + turn
+    near = lax.axis_size("pair") // 2
     slots = ((piece_no * near + place // 2) * count + within % count).reshape(-1)
     weights = coupling.reshape(-1)
     over = pltpu.with_memory_space_constraint(intersections, pltpu.HBM)
 
     kept = []
 
-    def coupled_parts(copies):
-        pieces = spread(copies)
+    def coupled_parts(piece):
+        pieces = spread(piece)
         if not kept:
-            kept.extend(arrange(sides, pieces[2], over))
-        parts = couple(slots, weights, *kept, pieces)
-        return lax.all_to_all(parts, "pno", 0, 0, tiled=True)
-
-    parts = coupled_parts(copies)
+            kept.extend(arrange(sides, pieces[0], over))
+        mine, theirs = couple(sides, slots, weights, *kept, pieces)
+        return mine, swapped(theirs, "pno", 0, False)
+
+    mine, theirs = coupled_parts(own)
     ints = integrals.astype(jnp.float32)
-    terms = [mask * (ints + (parts[0] + parts[1]) - denom * own.astype(jnp.float32))]
+    terms = [mask * (ints + (mine + theirs) - denom * own.astype(jnp.float32))]
     for step_no in range(1, ITERS):
-        piece = (terms[-1] / denom).astype(jnp.bfloat16)
-        parts = coupled_parts(jnp.broadcast_to(piece, (near, *piece.shape)))
+        mine, theirs = coupled_parts((terms[-1] / denom).astype(jnp.bfloat16))
         if step_no + 1 < ITERS:
-            terms.append(mask * (parts[0] + parts[1]) - terms[-1])
-    last, sums = products(cells**-0.5, parts, mask, terms)
-    sums = jnp.sum(copies_of_all(sums, ("chain", "pno")), axis=0)
-    return tuple(finish(copies_of_all(sums, ("pair",)), own, denom, terms + [last]))
+            terms.append(mask * (mine + theirs) - terms[-1])
+    lines = lax.axis_size("chain") * lax.axis_size("pno")
+    last, sums = products(cells**-0.5, mine, theirs, mask, terms, lines)
+    sums = lax.all_to_all(sums, ("chain", "pno"), 0, 0, tiled=True)
+    sums = jnp.broadcast_to(jnp.sum(sums, axis=0), (lax.axis_size("pair"), 1, width))
+    sums = lax.all_to_all(sums, "pair", 0, 0, tiled=True)
+    return tuple(finish(sums, own, denom, terms + [last]))
 
 
 def solution(mesh):

time: 246 us -> 243 us (0.988)
  waiting for transfers between devices: 51.5 us -> 27.6 us
  starting transfers between devices: 50.3 us -> 70 us
  blocking collectives: 109 us -> 118 us
  Pallas kernels: 25.9 us -> 21.2 us
  other arithmetic: 4.71 us -> 1.41 us
    all_gather x0 -> x6, blocking collectives: none -> 55.1 us  [joined(): lax.all_gather(value, 'pair', axis=0, tiled=True, axis_index_groups=groups)]
    all_to_all x7 -> x2, blocking collectives: 109 us -> 63.2 us  [the longest x1 50.7 us: per_device(): sums = lax.all_to_all(sums, ('chain', 'pno'), 0, 0, tiled=True)]
    ppermute x15 -> x18, starting transfers between devices: 43 us -> 70 us  [swapped(): return lax.ppermute(value, axis, pairs)]
    all_to_all x1 -> x0, waiting for transfers between devices: 12.9 us -> none  [spread(): lax.all_to_all(copies, 'pair', 0, 0, tiled=True, axis_index_groups=groups)]
    ppermute x15 -> x18, waiting for transfers between devices: 38.6 us -> 27.6 us  [swapped(): return lax.ppermute(value, axis, pairs)]
    all_to_all x1 -> x0, starting transfers between devices: 7.31 us -> none  [spread(): lax.all_to_all(copies, 'pair', 0, 0, tiled=True, axis_index_groups=groups)]
  transfers between devices with their start and end apart: 16 -> 18, of which waited for: 12 -> 11; matrix products, arithmetic and copies ran while one was open for 2% -> 1% of each run, Pallas kernels for 2% -> 2%
where the time goes in v3:
time: 243 us; the launch traced here: 242 us
  blocking collectives  118 us (49%)
  starting transfers between devices  70 us (29%)
  waiting for transfers between devices  27.6 us (11%)
  Pallas kernels  21.2 us (9%)
  local copies, waits for them, and re-layouts  2.5 us (1%)
    ppermute x18, starting transfers between devices, swapped(): return lax.ppermute(value, axis, pairs)  70 us
    all_gather x6, blocking collectives, joined(): lax.all_gather(value, 'pair', axis=0, tiled=True, axis_index_groups=groups)  55.1 us
    all_to_all x1, blocking collectives, per_device(): sums = lax.all_to_all(sums, ('chain', 'pno'), 0, 0, tiled=True)  50.7 us
    ppermute x18, waiting for transfers between devices, swapped(): return lax.ppermute(value, axis, pairs)  27.6 us
    pallas_call x3, Pallas kernels, couple(): pl.pallas_call(couple_kernel, in_specs=[scalars] * 3 + [inside] * (2 + le...  13.6 us
    all_to_all x1, blocking collectives, per_device(): sums = lax.all_to_all(sums, 'pair', 0, 0, tiled=True)  12.5 us
    pallas_call x1, Pallas kernels, arrange(): pl.pallas_call(arrange_kernel, grid_spec=pltpu.PrefetchScalarGridSpec(num...  5.67 us
  transfers between devices with their start and end apart: 18, of which 11 were waited for; matrix products, arithmetic and copies ran while one was open for 1% of the time, Pallas kernels for 2%

profile of v3, /device:TPU:80, one launch (start us, length us, event | category | flops | bytes accessed | tf_op | source)
XLA Modules:
  0.0 241.9 jit_solution(1579781609149747367)
XLA Ops:
  2.8 8.4 %all_gather.18 = bf16[12,64,128]{2,1,0:T(8,128)(2,1)S(1)} all-gather(bf16[6,64,128]{2,1,0:T(8,128)(2,1)S(1)} %masked.1.own), channel_id=1, replica_groups={{0,4},{2,6},{8,12},{10,14},{1,5},{3,7},{9,13},{11,15},{16,20},{18,22},{..., dimensions={0}, use_global_device_ids=true | all-gather | bytes 294912 | tf_op jit(solution)/shard_map/all_gather | solution.py:29
  11.2 12.2 %all_gather.19.after.refs_0_ = bf16[24,64,128]{2,1,0:T(8,128)(2,1)S(1)} all-gather(bf16[12,64,128]{2,1,0:T(8,128)(2,1)S(1)} %all_gather.18), channel_id=1, replica_groups={{4,8},{6,10},{0,12},{2,14},{5,9},{7,11},{1,13},{3,15},{20,24},{22,26},{..., dimensions={0}, use_global_device_ids=true | all-gather | bytes 589824 | tf_op jit(solution)/shard_map/all_gather | solution.py:29
  23.4 6.0 %collective-permute-start.1 = (bf16[24,64,128]{2,1,0:T(8,128)(2,1)S(1)}, bf16[24,64,128]{2,1,0:T(8,128)(2,1)S(1)}, u32[]{:S(2)}, u32[]{:S(2)}) collective-permute-start(bf16[24,64,128]{2,1,0:T(8,128)(2,1)S(1)} %all_gather.19.after.refs_0_), channel_id=1, source_target_pairs={{0,16},{16,0},{32,48},{48,32},{64,80},{80,64},{96,112},{112,96},{1... | collective-permute-start | bytes 1179656 | tf_op jit(solution)/shard_map/ppermute | solution.py:19
  30.1 4.2 %collective-permute-start = (bf16[24,64,128]{2,1,0:T(8,128)(2,1)S(1)}, bf16[24,64,128]{2,1,0:T(8,128)(2,1)S(1)}, u32[]{:S(2)}, u32[]{:S(2)}) collective-permute-start(bf16[24,64,128]{2,1,0:T(8,128)(2,1)S(1)} %all_gather.19.after.refs_0_), channel_id=1, source_target_pairs={{0,2},{2,0},{4,6},{6,4},{8,10},{10,8},{12,14},{14,12},{1,3},{3,1},... | collective-permute-start | bytes 1179656 | tf_op jit(solution)/shard_map/ppermute | solution.py:19
  35.9 1.9 collective-permute-done.1.refs_2_
  37.7 3.2 %collective-permute-start.2 = (bf16[24,64,128]{2,1,0:T(8,128)(2,1)S(1)}, bf16[24,64,128]{2,1,0:T(8,128)(2,1)S(1)}, u32[]{:S(2)}, u32[]{:S(2)}) collective-permute-start(bf16[24,64,128]{2,1,0:T(8,128)(2,1)S(1)} %collective-permute-done.1.refs_2_), channel_id=1, source_target_pairs={{2,4},{4,2},{6,8},{8,6},{10,12},{12,10},{14,0},{0,14},{3,5},{5,3},... | collective-permute-start | bytes 1179656 | tf_op jit(solution)/shard_map/ppermute | solution.py:19
  41.0 5.6 %collective-permute-start.4 = (bf16[24,64,128]{2,1,0:T(8,128)(2,1)S(1)}, bf16[24,64,128]{2,1,0:T(8,128)(2,1)S(1)}, u32[]{:S(2)}, u32[]{:S(2)}) collective-permute-start(bf16[24,64,128]{2,1,0:T(8,128)(2,1)S(1)} %collective-permute-done.3.refs_4_), channel_id=1, source_target_pairs={{0,2},{2,0},{4,6},{6,4},{8,10},{10,8},{12,14},{14,12},{1,3},{3,1},... | collective-permute-start | bytes 1179656 | tf_op jit(solution)/shard_map/ppermute | solution.py:19
  46.5 5.7 %arrange.1 = (bf16[6,32,128,128]{3,2,1,0:T(8,128)(2,1)S(1)}, bf16[6,128,2048]{2,1,0:T(8,128)(2,1)S(1)}) custom-call(s32[1]{0:T(128)} %bitcast.side, bf16[24,64,128]{2,1,0:T(8,128)(2,1)S(1)} %all_gather.19.after.refs_0_, bf16[6,32,128,128]{3,2,1,0:T(8,128)(2,1)} %over.1), custom_call_target="tpu_custom_call" | custom-call | flops 1000000000 | bytes 9437184 | tf_op jit(solution)/shard_map/arrange/pallas_call | solution.py:93
  54.2 4.5 %couple.3 = (f32[6,64,128]{2,1,0:T(8,128)S(1)}, f32[6,64,128]{2,1,0:T(8,128)S(1)}) custom-call(s32[1]{0:T(128)} %bitcast.side, s32[192]{0:T(256)S(1)} %reshape.67.slots, f32[192]{0:T(256)S(1)} %reshape.68.weights, bf16[6,32,128,128]{3,2,1,0:T(8,128)(2,1)S(1)} %get-tuple-element.12.across, bf16[6,128,2048]{2,1,0:T(8,128)(2,1)S(1)} %get-tuple-element.13.halves, ...), custom_call_target="tpu_custom_call" | custom-call | tf_op jit(solution)/shard_map/couple/pallas_call | solution.py:156
  58.8 2.0 collective-permute-start.5
  62.3 8.5 %all_gather.20 = bf16[12,64,128]{2,1,0:T(8,128)(2,1)S(1)} all-gather(bf16[6,64,128]{2,1,0:T(8,128)(2,1)S(1)} %get-tuple-element.24), channel_id=1, replica_groups={{0,4},{2,6},{8,12},{10,14},{1,5},{3,7},{9,13},{11,15},{16,20},{18,22},{..., dimensions={0}, use_global_device_ids=true | all-gather | bytes 294912 | tf_op jit(solution)/shard_map/all_gather | solution.py:29
  70.9 8.6 %all_gather.21.refs_0_ = bf16[24,64,128]{2,1,0:T(8,128)(2,1)S(1)} all-gather(bf16[12,64,128]{2,1,0:T(8,128)(2,1)S(1)} %all_gather.20), channel_id=1, replica_groups={{4,8},{6,10},{0,12},{2,14},{5,9},{7,11},{1,13},{3,15},{20,24},{22,26},{..., dimensions={0}, use_global_device_ids=true | all-gather | bytes 589824 | tf_op jit(solution)/shard_map/all_gather | solution.py:29
  80.1 11.6 %collective-permute-start.7 = (bf16[24,64,128]{2,1,0:T(8,128)(2,1)S(1)}, bf16[24,64,128]{2,1,0:T(8,128)(2,1)S(1)}, u32[]{:S(2)}, u32[]{:S(2)}) collective-permute-start(bf16[24,64,128]{2,1,0:T(8,128)(2,1)S(1)} %all_gather.21.refs_0_), channel_id=1, source_target_pairs={{0,16},{16,0},{32,48},{48,32},{64,80},{80,64},{96,112},{112,96},{1... | collective-permute-start | bytes 1179656 | tf_op jit(solution)/shard_map/ppermute | solution.py:19
  91.7 5.8 %collective-permute-start.6 = (bf16[24,64,128]{2,1,0:T(8,128)(2,1)S(1)}, bf16[24,64,128]{2,1,0:T(8,128)(2,1)S(1)}, u32[]{:S(2)}, u32[]{:S(2)}) collective-permute-start(bf16[24,64,128]{2,1,0:T(8,128)(2,1)S(1)} %all_gather.21.refs_0_), channel_id=1, source_target_pairs={{0,2},{2,0},{4,6},{6,4},{8,10},{10,8},{12,14},{14,12},{1,3},{3,1},... | collective-permute-start | bytes 1179656 | tf_op jit(solution)/shard_map/ppermute | solution.py:19
  97.5 2.0 collective-permute-start.10
  100.4 4.1 %collective-permute-start.8 = (bf16[24,64,128]{2,1,0:T(8,128)(2,1)S(1)}, bf16[24,64,128]{2,1,0:T(8,128)(2,1)S(1)}, u32[]{:S(2)}, u32[]{:S(2)}) collective-permute-start(bf16[24,64,128]{2,1,0:T(8,128)(2,1)S(1)} %collective-permute-done.7.refs_2_), channel_id=1, source_target_pairs={{2,4},{4,2},{6,8},{8,6},{10,12},{12,10},{14,0},{0,14},{3,5},{5,3},... | collective-permute-start | bytes 1179656 | tf_op jit(solution)/shard_map/ppermute | solution.py:19
  104.6 2.9 %collective-permute-done.6.refs_1_ = bf16[24,64,128]{2,1,0:T(8,128)(2,1)S(1)} collective-permute-done((bf16[24,64,128]{2,1,0:T(8,128)(2,1)S(1)}, bf16[24,64,128]{2,1,0:T(8,128)(2,1)S(1)}, u32[]{:S(2)}, u32[]{:S(2)}) %collective-permute-start.6) | collective-permute-done | bytes 393248 | tf_op jit(solution)/shard_map/ppermute | solution.py:19
  107.4 7.2 %collective-permute-done.10.refs_5_ = bf16[24,64,128]{2,1,0:T(8,128)(2,1)S(1)} collective-permute-done((bf16[24,64,128]{2,1,0:T(8,128)(2,1)S(1)}, bf16[24,64,128]{2,1,0:T(8,128)(2,1)S(1)}, u32[]{:S(2)}, u32[]{:S(2)}) %collective-permute-start.10) | collective-permute-done | bytes 393248 | tf_op jit(solution)/shard_map/ppermute | solution.py:19
  114.6 4.5 %couple.4 = (f32[6,64,128]{2,1,0:T(8,128)S(1)}, f32[6,64,128]{2,1,0:T(8,128)S(1)}) custom-call(s32[1]{0:T(128)} %bitcast.side, s32[192]{0:T(256)S(1)} %reshape.67.slots, f32[192]{0:T(256)S(1)} %reshape.68.weights, bf16[6,32,128,128]{3,2,1,0:T(8,128)(2,1)S(1)} %get-tuple-element.12.across, bf16[6,128,2048]{2,1,0:T(8,128)(2,1)S(1)} %get-tuple-element.13.halves, ...), custom_call_target="tpu_custom_call" | custom-call | tf_op jit(solution)/shard_map/couple/pallas_call | solution.py:156
  119.2 2.0 collective-permute-start.11
  122.7 8.5 %all_gather.22 = bf16[12,64,128]{2,1,0:T(8,128)(2,1)S(1)} all-gather(bf16[6,64,128]{2,1,0:T(8,128)(2,1)S(1)} %get-tuple-element.22), channel_id=1, replica_groups={{0,4},{2,6},{8,12},{10,14},{1,5},{3,7},{9,13},{11,15},{16,20},{18,22},{..., dimensions={0}, use_global_device_ids=true | all-gather | bytes 294912 | tf_op jit(solution)/shard_map/all_gather | solution.py:29
  131.3 8.9 %all_gather.23.refs_0_ = bf16[24,64,128]{2,1,0:T(8,128)(2,1)S(1)} all-gather(bf16[12,64,128]{2,1,0:T(8,128)(2,1)S(1)} %all_gather.22), channel_id=1, replica_groups={{4,8},{6,10},{0,12},{2,14},{5,9},{7,11},{1,13},{3,15},{20,24},{22,26},{..., dimensions={0}, use_global_device_ids=true | all-gather | bytes 589824 | tf_op jit(solution)/shard_map/all_gather | solution.py:29
  140.2 4.8 %collective-permute-start.13 = (bf16[24,64,128]{2,1,0:T(8,128)(2,1)S(1)}, bf16[24,64,128]{2,1,0:T(8,128)(2,1)S(1)}, u32[]{:S(2)}, u32[]{:S(2)}) collective-permute-start(bf16[24,64,128]{2,1,0:T(8,128)(2,1)S(1)} %all_gather.23.refs_0_), channel_id=1, source_target_pairs={{0,16},{16,0},{32,48},{48,32},{64,80},{80,64},{96,112},{112,96},{1... | collective-permute-start | bytes 1179656 | tf_op jit(solution)/shard_map/ppermute | solution.py:19
  145.6 6.0 %collective-permute-start.12 = (bf16[24,64,128]{2,1,0:T(8,128)(2,1)S(1)}, bf16[24,64,128]{2,1,0:T(8,128)(2,1)S(1)}, u32[]{:S(2)}, u32[]{:S(2)}) collective-permute-start(bf16[24,64,128]{2,1,0:T(8,128)(2,1)S(1)} %all_gather.23.refs_0_), channel_id=1, source_target_pairs={{0,2},{2,0},{4,6},{6,4},{8,10},{10,8},{12,14},{14,12},{1,3},{3,1},... | collective-permute-start | bytes 1179656 | tf_op jit(solution)/shard_map/ppermute | solution.py:19
  153.0 4.4 %collective-permute-start.14 = (bf16[24,64,128]{2,1,0:T(8,128)(2,1)S(1)}, bf16[24,64,128]{2,1,0:T(8,128)(2,1)S(1)}, u32[]{:S(2)}, u32[]{:S(2)}) collective-permute-start(bf16[24,64,128]{2,1,0:T(8,128)(2,1)S(1)} %collective-permute-done.13.refs_2_), channel_id=1, source_target_pairs={{2,4},{4,2},{6,8},{8,6},{10,12},{12,10},{14,0},{0,14},{3,5},{5,3},... | collective-permute-start | bytes 1179656 | tf_op jit(solution)/shard_map/ppermute | solution.py:19
  157.5 4.4 %collective-permute-start.16 = (bf16[24,64,128]{2,1,0:T(8,128)(2,1)S(1)}, bf16[24,64,128]{2,1,0:T(8,128)(2,1)S(1)}, u32[]{:S(2)}, u32[]{:S(2)}) collective-permute-start(bf16[24,64,128]{2,1,0:T(8,128)(2,1)S(1)} %collective-permute-done.15.refs_4_), channel_id=1, source_target_pairs={{0,2},{2,0},{4,6},{6,4},{8,10},{10,8},{12,14},{14,12},{1,3},{3,1},... | collective-permute-start | bytes 1179656 | tf_op jit(solution)/shard_map/ppermute | solution.py:19
  161.9 3.5 %collective-permute-done.14.refs_3_ = bf16[24,64,128]{2,1,0:T(8,128)(2,1)S(1)} collective-permute-done((bf16[24,64,128]{2,1,0:T(8,128)(2,1)S(1)}, bf16[24,64,128]{2,1,0:T(8,128)(2,1)S(1)}, u32[]{:S(2)}, u32[]{:S(2)}) %collective-permute-start.14) | collective-permute-done | bytes 393248 | tf_op jit(solution)/shard_map/ppermute | solution.py:19
  165.4 3.9 %collective-permute-done.16.refs_5_ = bf16[24,64,128]{2,1,0:T(8,128)(2,1)S(1)} collective-permute-done((bf16[24,64,128]{2,1,0:T(8,128)(2,1)S(1)}, bf16[24,64,128]{2,1,0:T(8,128)(2,1)S(1)}, u32[]{:S(2)}, u32[]{:S(2)}) %collective-permute-start.16) | collective-permute-done | bytes 393248 | tf_op jit(solution)/shard_map/ppermute | solution.py:19
  169.3 4.5 %couple.5 = (f32[6,64,128]{2,1,0:T(8,128)S(1)}, f32[6,64,128]{2,1,0:T(8,128)S(1)}) custom-call(s32[1]{0:T(128)} %bitcast.side, s32[192]{0:T(256)S(1)} %reshape.67.slots, f32[192]{0:T(256)S(1)} %reshape.68.weights, bf16[6,32,128,128]{3,2,1,0:T(8,128)(2,1)S(1)} %get-tuple-element.12.across, bf16[6,128,2048]{2,1,0:T(8,128)(2,1)S(1)} %get-tuple-element.13.halves, ...), custom_call_target="tpu_custom_call" | custom-call | tf_op jit(solution)/shard_map/couple/pallas_call | solution.py:156
  173.9 2.0 collective-permute-start.17
  177.6 50.7 %all_to_all.10 = f32[32,1,128]{2,1,0:T(1,128)S(1)} all-to-all(f32[32,1,128]{2,1,0:T(1,128)S(1)} %get-tuple-element.20), channel_id=1, replica_groups=mesh['job'=2,'chain'=16,'pair'=8,'pno'=2] {'chain','pno'}, dimensions={0} | all-to-all | bytes 32768 | tf_op jit(solution)/shard_map/all_to_all | solution.py:284
  228.3 12.5 %all_to_all.11.copies = f32[8,1,128]{2,1,0:T(1,128)S(1)} all-to-all(f32[8,1,128]{2,1,0:T(1,128)S(1)} %broadcast_in_dim.8), channel_id=1, replica_groups=mesh['job'=2,'chain'=16,'pair'=8,'pno'=2] {'pair'}, dimensions={0} | all-to-all | bytes 8192 | tf_op jit(solution)/shard_map/all_to_all | solution.py:286
  (43 shorter events, 16.2 us)
Async XLA Ops:
  0.6 51.7 %copy-start.2 = (s32[6]{0:T(128)S(1)}, s32[6]{0:T(128)}, u32[]{:S(2)}) copy-start(s32[6]{0:T(128)} %ranks.1) | copy-start | bytes 76
  0.6 51.6 %copy-start.4 = (f32[6,128]{1,0:T(8,128)S(1)}, f32[6,128]{1,0:T(8,128)}, u32[]{:S(2)}) copy-start(f32[6,128]{1,0:T(8,128)} %param.12) | copy-start | bytes 9220
  0.7 0.9 copy-start
  1.6 0.7 copy-start.1
  23.4 14.4 %collective-permute-start.1 = (bf16[24,64,128]{2,1,0:T(8,128)(2,1)S(1)}, bf16[24,64,128]{2,1,0:T(8,128)(2,1)S(1)}, u32[]{:S(2)}, u32[]{:S(2)}) collective-permute-start(bf16[24,64,128]{2,1,0:T(8,128)(2,1)S(1)} %all_gather.19.after.refs_0_), channel_id=1, source_target_pairs={{0,16},{16,0},{32,48},{48,32},{64,80},{80,64},{96,112},{112,96},{1... | collective-permute-start | bytes 1179656 | tf_op jit(solution)/shard_map/ppermute | solution.py:19
  29.4 11.6 %collective-permute-start.3 = (bf16[24,64,128]{2,1,0:T(8,128)(2,1)S(1)}, bf16[24,64,128]{2,1,0:T(8,128)(2,1)S(1)}, u32[]{:S(2)}, u32[]{:S(2)}) collective-permute-start(bf16[24,64,128]{2,1,0:T(8,128)(2,1)S(1)} %all_gather.19.after.refs_0_), channel_id=1, source_target_pairs={{16,32},{32,16},{48,64},{64,48},{80,96},{96,80},{112,128},{128,112... | collective-permute-start | bytes 1179656 | tf_op jit(solution)/shard_map/ppermute | solution.py:19
  30.1 22.3 %collective-permute-start = (bf16[24,64,128]{2,1,0:T(8,128)(2,1)S(1)}, bf16[24,64,128]{2,1,0:T(8,128)(2,1)S(1)}, u32[]{:S(2)}, u32[]{:S(2)}) collective-permute-start(bf16[24,64,128]{2,1,0:T(8,128)(2,1)S(1)} %all_gather.19.after.refs_0_), channel_id=1, source_target_pairs={{0,2},{2,0},{4,6},{6,4},{8,10},{10,8},{12,14},{14,12},{1,3},{3,1},... | collective-permute-start | bytes 1179656 | tf_op jit(solution)/shard_map/ppermute | solution.py:19
  37.7 14.7 %collective-permute-start.2 = (bf16[24,64,128]{2,1,0:T(8,128)(2,1)S(1)}, bf16[24,64,128]{2,1,0:T(8,128)(2,1)S(1)}, u32[]{:S(2)}, u32[]{:S(2)}) collective-permute-start(bf16[24,64,128]{2,1,0:T(8,128)(2,1)S(1)} %collective-permute-done.1.refs_2_), channel_id=1, source_target_pairs={{2,4},{4,2},{6,8},{8,6},{10,12},{12,10},{14,0},{0,14},{3,5},{5,3},... | collective-permute-start | bytes 1179656 | tf_op jit(solution)/shard_map/ppermute | solution.py:19
  41.0 13.3 %collective-permute-start.4 = (bf16[24,64,128]{2,1,0:T(8,128)(2,1)S(1)}, bf16[24,64,128]{2,1,0:T(8,128)(2,1)S(1)}, u32[]{:S(2)}, u32[]{:S(2)}) collective-permute-start(bf16[24,64,128]{2,1,0:T(8,128)(2,1)S(1)} %collective-permute-done.3.refs_4_), channel_id=1, source_target_pairs={{0,2},{2,0},{4,6},{6,4},{8,10},{10,8},{12,14},{14,12},{1,3},{3,1},... | collective-permute-start | bytes 1179656 | tf_op jit(solution)/shard_map/ppermute | solution.py:19
  52.2 9.9 %copy-start.3 = (bf16[6,64,128]{2,1,0:T(8,128)(2,1)S(1)}, bf16[6,64,128]{2,1,0:T(8,128)(2,1)}, u32[]{:S(2)}) copy-start(bf16[6,64,128]{2,1,0:T(8,128)(2,1)} %param.9) | copy-start | bytes 294916
  52.2 9.9 %copy-start.5 = (f32[6]{0:T(128)S(1)}, f32[6]{0:T(128)}, u32[]{:S(2)}) copy-start(f32[6]{0:T(128)} %param.13) | copy-start | bytes 76
  58.8 3.4 %collective-permute-start.5 = (f32[6,64,128]{2,1,0:T(8,128)S(1)}, f32[6,64,128]{2,1,0:T(8,128)S(1)}, u32[]{:S(2)}, u32[]{:S(2)}) collective-permute-start(f32[6,64,128]{2,1,0:T(8,128)S(1)} %get-tuple-element.15), channel_id=1, source_target_pairs={{0,1},{1,0},{2,3},{3,2},{4,5},{5,4},{6,7},{7,6},{8,9},{9,8},{10,11... | collective-permute-start | bytes 589832 | tf_op jit(solution)/shard_map/ppermute | solution.py:19
  79.4 18.1 %collective-permute-start.9 = (bf16[24,64,128]{2,1,0:T(8,128)(2,1)S(1)}, bf16[24,64,128]{2,1,0:T(8,128)(2,1)S(1)}, u32[]{:S(2)}, u32[]{:S(2)}) collective-permute-start(bf16[24,64,128]{2,1,0:T(8,128)(2,1)S(1)} %all_gather.21.refs_0_), channel_id=1, source_target_pairs={{16,32},{32,16},{48,64},{64,48},{80,96},{96,80},{112,128},{128,112... | collective-permute-start | bytes 1179656 | tf_op jit(solution)/shard_map/ppermute | solution.py:19
  80.1 20.3 %collective-permute-start.7 = (bf16[24,64,128]{2,1,0:T(8,128)(2,1)S(1)}, bf16[24,64,128]{2,1,0:T(8,128)(2,1)S(1)}, u32[]{:S(2)}, u32[]{:S(2)}) collective-permute-start(bf16[24,64,128]{2,1,0:T(8,128)(2,1)S(1)} %all_gather.21.refs_0_), channel_id=1, source_target_pairs={{0,16},{16,0},{32,48},{48,32},{64,80},{80,64},{96,112},{112,96},{1... | collective-permute-start | bytes 1179656 | tf_op jit(solution)/shard_map/ppermute | solution.py:19
  91.7 15.8 %collective-permute-start.6 = (bf16[24,64,128]{2,1,0:T(8,128)(2,1)S(1)}, bf16[24,64,128]{2,1,0:T(8,128)(2,1)S(1)}, u32[]{:S(2)}, u32[]{:S(2)}) collective-permute-start(bf16[24,64,128]{2,1,0:T(8,128)(2,1)S(1)} %all_gather.21.refs_0_), channel_id=1, source_target_pairs={{0,2},{2,0},{4,6},{6,4},{8,10},{10,8},{12,14},{14,12},{1,3},{3,1},... | collective-permute-start | bytes 1179656 | tf_op jit(solution)/shard_map/ppermute | solution.py:19
  97.5 17.1 %collective-permute-start.10 = (bf16[24,64,128]{2,1,0:T(8,128)(2,1)S(1)}, bf16[24,64,128]{2,1,0:T(8,128)(2,1)S(1)}, u32[]{:S(2)}, u32[]{:S(2)}) collective-permute-start(bf16[24,64,128]{2,1,0:T(8,128)(2,1)S(1)} %collective-permute-done.9.refs_4_), channel_id=1, source_target_pairs={{0,2},{2,0},{4,6},{6,4},{8,10},{10,8},{12,14},{14,12},{1,3},{3,1},... | collective-permute-start | bytes 1179656 | tf_op jit(solution)/shard_map/ppermute | solution.py:19
  100.4 14.2 %collective-permute-start.8 = (bf16[24,64,128]{2,1,0:T(8,128)(2,1)S(1)}, bf16[24,64,128]{2,1,0:T(8,128)(2,1)S(1)}, u32[]{:S(2)}, u32[]{:S(2)}) collective-permute-start(bf16[24,64,128]{2,1,0:T(8,128)(2,1)S(1)} %collective-permute-done.7.refs_2_), channel_id=1, source_target_pairs={{2,4},{4,2},{6,8},{8,6},{10,12},{12,10},{14,0},{0,14},{3,5},{5,3},... | collective-permute-start | bytes 1179656 | tf_op jit(solution)/shard_map/ppermute | solution.py:19
  119.2 3.4 %collective-permute-start.11 = (f32[6,64,128]{2,1,0:T(8,128)S(1)}, f32[6,64,128]{2,1,0:T(8,128)S(1)}, u32[]{:S(2)}, u32[]{:S(2)}) collective-permute-start(f32[6,64,128]{2,1,0:T(8,128)S(1)} %get-tuple-element.17), channel_id=1, source_target_pairs={{0,1},{1,0},{2,3},{3,2},{4,5},{5,4},{6,7},{7,6},{8,9},{9,8},{10,11... | collective-permute-start | bytes 589832 | tf_op jit(solution)/shard_map/ppermute | solution.py:19
  140.2 12.9 %collective-permute-start.13 = (bf16[24,64,128]{2,1,0:T(8,128)(2,1)S(1)}, bf16[24,64,128]{2,1,0:T(8,128)(2,1)S(1)}, u32[]{:S(2)}, u32[]{:S(2)}) collective-permute-start(bf16[24,64,128]{2,1,0:T(8,128)(2,1)S(1)} %all_gather.23.refs_0_), channel_id=1, source_target_pairs={{0,16},{16,0},{32,48},{48,32},{64,80},{80,64},{96,112},{112,96},{1... | collective-permute-start | bytes 1179656 | tf_op jit(solution)/shard_map/ppermute | solution.py:19
  144.9 12.5 %collective-permute-start.15 = (bf16[24,64,128]{2,1,0:T(8,128)(2,1)S(1)}, bf16[24,64,128]{2,1,0:T(8,128)(2,1)S(1)}, u32[]{:S(2)}, u32[]{:S(2)}) collective-permute-start(bf16[24,64,128]{2,1,0:T(8,128)(2,1)S(1)} %all_gather.23.refs_0_), channel_id=1, source_target_pairs={{16,32},{32,16},{48,64},{64,48},{80,96},{96,80},{112,128},{128,112... | collective-permute-start | bytes 1179656 | tf_op jit(solution)/shard_map/ppermute | solution.py:19
  145.6 16.2 %collective-permute-start.12 = (bf16[24,64,128]{2,1,0:T(8,128)(2,1)S(1)}, bf16[24,64,128]{2,1,0:T(8,128)(2,1)S(1)}, u32[]{:S(2)}, u32[]{:S(2)}) collective-permute-start(bf16[24,64,128]{2,1,0:T(8,128)(2,1)S(1)} %all_gather.23.refs_0_), channel_id=1, source_target_pairs={{0,2},{2,0},{4,6},{6,4},{8,10},{10,8},{12,14},{14,12},{1,3},{3,1},... | collective-permute-start | bytes 1179656 | tf_op jit(solution)/shard_map/ppermute | solution.py:19
  153.0 12.4 %collective-permute-start.14 = (bf16[24,64,128]{2,1,0:T(8,128)(2,1)S(1)}, bf16[24,64,128]{2,1,0:T(8,128)(2,1)S(1)}, u32[]{:S(2)}, u32[]{:S(2)}) collective-permute-start(bf16[24,64,128]{2,1,0:T(8,128)(2,1)S(1)} %collective-permute-done.13.refs_2_), channel_id=1, source_target_pairs={{2,4},{4,2},{6,8},{8,6},{10,12},{12,10},{14,0},{0,14},{3,5},{5,3},... | collective-permute-start | bytes 1179656 | tf_op jit(solution)/shard_map/ppermute | solution.py:19
  157.5 11.9 %collective-permute-start.16 = (bf16[24,64,128]{2,1,0:T(8,128)(2,1)S(1)}, bf16[24,64,128]{2,1,0:T(8,128)(2,1)S(1)}, u32[]{:S(2)}, u32[]{:S(2)}) collective-permute-start(bf16[24,64,128]{2,1,0:T(8,128)(2,1)S(1)} %collective-permute-done.15.refs_4_), channel_id=1, source_target_pairs={{0,2},{2,0},{4,6},{6,4},{8,10},{10,8},{12,14},{14,12},{1,3},{3,1},... | collective-permute-start | bytes 1179656 | tf_op jit(solution)/shard_map/ppermute | solution.py:19
  173.9 3.4 %collective-permute-start.17 = (f32[6,64,128]{2,1,0:T(8,128)S(1)}, f32[6,64,128]{2,1,0:T(8,128)S(1)}, u32[]{:S(2)}, u32[]{:S(2)}) collective-permute-start(f32[6,64,128]{2,1,0:T(8,128)S(1)} %get-tuple-element.19), channel_id=1, source_target_pairs={{0,1},{1,0},{2,3},{3,2},{4,5},{5,4},{6,7},{7,6},{8,9},{9,8},{10,11... | collective-permute-start | bytes 589832 | tf_op jit(solution)/shard_map/ppermute | solution.py:19

commit v4 on v3

--- a/solution.py
+++ b/solution.py
@@ -9,13 +9,9 @@
 PRODUCTS = [(i, j) for i in range(ITERS) for j in range(i + 1)]
 
 
-def swapped(value, axis, first, around):
+def shifted(value, axis, step, around=False):
     count = lax.axis_size(axis)
-    pairs = []
-    for left in range(first, count, 2):
-        if left + 1 < count or around:
-            right = (left + 1) % count
-            pairs += [(left, right), (right, left)]
+    pairs = [(i, (i + step) % count) for i in range(count) if around or 0 <= i + step < count]
     return lax.ppermute(value, axis, pairs)
 
 
@@ -26,17 +22,18 @@
         for parity in range(step):
             left, right = (start + parity) % count, (start + step + parity) % count
             groups.append(sorted([left, right]))
-    return lax.all_gather(value, "pair", axis=0, tiled=True, axis_index_groups=groups)
+    both = jnp.broadcast_to(value, (2, *value.shape))
+    both = lax.all_to_all(both, "pair", 0, 0, tiled=True, axis_index_groups=groups)
+    return both.reshape(-1, *value.shape[1:])
 
 
 def spread(piece):
     near = joined(joined(piece, 2, 0), 2, 2)
-    ahead = swapped(near, "chain", 0, False)
-    behind = swapped(near, "chain", 1, False)
-    other = swapped(near, "pair", 0, True)
-    ahead_other = swapped(ahead, "pair", 1, True)
-    behind_other = swapped(behind, "pair", 0, True)
-    return near, other, ahead, ahead_other, behind, behind_other
+    low, high = shifted(near, "chain", 1), shifted(near, "chain", -1)
+    other = shifted(near, "pair", -1, around=True)
+    low_other = shifted(low, "pair", 1, around=True)
+    high_other = shifted(high, "pair", -1, around=True)
+    return low, low_other, near, other, high, high_other
 
 
 def live_cells(rank, first, half, width):
@@ -171,14 +168,14 @@
     held, (last, sums) = refs[:-2], refs[-2:]
     last[...] = mask[...] * (mine[...] + theirs[...]) - held[-1][...]
     terms = [ref[...] * scale for ref in held] + [last[...] * scale]
-    lane = lax.broadcasted_iota(jnp.int32, sums.shape, 2)
+    lane = lax.broadcasted_iota(jnp.int32, sums.shape, 1)
     row = jnp.zeros(sums.shape, jnp.float32)
     for place, (i, j) in enumerate(PRODUCTS):
         row = jnp.where(lane == place, jnp.sum(terms[i] * terms[j]), row)
     sums[...] = row
 
 
-def products(scale, mine, theirs, mask, held, count):
+def products(scale, mine, theirs, mask, held):
     shape = mask.shape
     inside = pl.BlockSpec(memory_space=pltpu.VMEM)
     return pl.pallas_call(
@@ -187,7 +184,7 @@
         out_specs=(inside, inside),
         out_shape=(
             jax.ShapeDtypeStruct(shape, jnp.float32),
-            jax.ShapeDtypeStruct((count, 1, shape[-1]), jnp.float32),
+            jax.ShapeDtypeStruct((1, shape[-1]), jnp.float32),
         ),
         compiler_params=pltpu.CompilerParams(vmem_limit_bytes=8 * 1024 * 1024),
         name="products",
@@ -255,9 +252,7 @@
     within = neighbours % frag
     place = within // count
     turn = (place - lax.axis_index("pair")) % 2
-    offset = neighbours // frag - chain_pos
-    facing = 1 - 2 * (chain_pos % 2)
-    piece_no = 2 * jnp.where(offset == 0, 0, jnp.where(offset == facing, 1, 2)) + turn
+    piece_no = 2 * (neighbours // frag - chain_pos + 1) + turn
     near = lax.axis_size("pair") // 2
     slots = ((piece_no * near + place // 2) * count + within % count).reshape(-1)
     weights = coupling.reshape(-1)
@@ -268,9 +263,9 @@
     def coupled_parts(piece):
         pieces = spread(piece)
         if not kept:
-            kept.extend(arrange(sides, pieces[0], over))
+            kept.extend(arrange(sides, pieces[2], over))
         mine, theirs = couple(sides, slots, weights, *kept, pieces)
-        return mine, swapped(theirs, "pno", 0, False)
+        return mine, shifted(theirs, "pno", 1, around=True)
 
     mine, theirs = coupled_parts(own)
     ints = integrals.astype(jnp.float32)
@@ -279,12 +274,11 @@
         mine, theirs = coupled_parts((terms[-1] / denom).astype(jnp.bfloat16))
         if step_no + 1 < ITERS:
             terms.append(mask * (mine + theirs) - terms[-1])
-    lines = lax.axis_size("chain") * lax.axis_size("pno")
-    last, sums = products(cells**-0.5, mine, theirs, mask, terms, lines)
-    sums = lax.all_to_all(sums, ("chain", "pno"), 0, 0, tiled=True)
-    sums = jnp.broadcast_to(jnp.sum(sums, axis=0), (lax.axis_size("pair"), 1, width))
-    sums = lax.all_to_all(sums, "pair", 0, 0, tiled=True)
-    return tuple(finish(sums, own, denom, terms + [last]))
+    last, sums = products(cells**-0.5, mine, theirs, mask, terms)
+    sums = sums + shifted(sums, "pno", 1, around=True)
+    rest = ("chain", "pair")
+    sums = jnp.broadcast_to(sums, (lax.axis_size(rest), *sums.shape))
+    return tuple(finish(lax.all_to_all(sums, rest, 0, 0, tiled=True), own, denom, terms + [last]))
 
 
 def solution(mesh):

time: 243 us -> 258 us (1.062)
  waiting for transfers between devices: 27.6 us -> 34.7 us
  blocking collectives: 118 us -> 124 us
    all_to_all x2 -> x7, blocking collectives: 63.2 us -> 124 us  [the longest x6 67.5 us: joined(): lax.all_to_all(both, 'pair', 0, 0, tiled=True, axis_index_groups=groups)]
    all_gather x6 -> x0, blocking collectives: 55.1 us -> none  [joined(): lax.all_gather(value, 'pair', axis=0, tiled=True, axis_index_groups=groups)]
    ppermute x18 -> x19, waiting for transfers between devices: 27.6 us -> 34.7 us  [shifted(): return lax.ppermute(value, axis, pairs)]
    ppermute x18 -> x19, starting transfers between devices: 70 us -> 70.3 us  [shifted(): return lax.ppermute(value, axis, pairs)]
  transfers between devices with their start and end apart: 18 -> 19, of which waited for: 11 -> 13; matrix products, arithmetic and copies ran while one was open for 1% -> 1% of each run, Pallas kernels for 2% -> 2%
where the time goes in v4:
time: 258 us; the launch traced here: 257 us
  blocking collectives  124 us (48%)
  starting transfers between devices  70.3 us (27%)
  waiting for transfers between devices  34.7 us (13%)
  Pallas kernels  21.2 us (8%)
  local copies, waits for them, and re-layouts  3.55 us (1%)
    ppermute x19, starting transfers between devices, shifted(): return lax.ppermute(value, axis, pairs)  70.3 us
    all_to_all x6, blocking collectives, joined(): lax.all_to_all(both, 'pair', 0, 0, tiled=True, axis_index_groups=groups)  67.5 us
    all_to_all x1, blocking collectives, per_device(): lax.all_to_all(sums, rest, 0, 0, tiled=True)  56.2 us
    ppermute x19, waiting for transfers between devices, shifted(): return lax.ppermute(value, axis, pairs)  34.7 us
    pallas_call x3, Pallas kernels, couple(): pl.pallas_call(couple_kernel, in_specs=[scalars] * 3 + [inside] * (2 + le...  13.5 us
    pallas_call x1, Pallas kernels, arrange(): pl.pallas_call(arrange_kernel, grid_spec=pltpu.PrefetchScalarGridSpec(num...  5.66 us
  transfers between devices with their start and end apart: 19, of which 13 were waited for; matrix products, arithmetic and copies ran while one was open for 1% of the time, Pallas kernels for 2%

profile of v4, /device:TPU:80, one launch (start us, length us, event | category | flops | bytes accessed | tf_op | source)
XLA Modules:
  0.0 256.5 jit_solution(16303422140848299758)
XLA Ops:
  2.8 11.3 %all_to_all.35 = bf16[2,6,64,128]{3,2,1,0:T(8,128)(2,1)S(1)} all-to-all(bf16[2,6,64,128]{3,2,1,0:T(8,128)(2,1)S(1)} %broadcast_in_dim.14), channel_id=1, replica_groups={{0,4},{2,6},{8,12},{10,14},{1,5},{3,7},{9,13},{11,15},{16,20},{18,22},{..., dimensions={0} | all-to-all | bytes 393216 | tf_op jit(solution)/shard_map/all_to_all | solution.py:26
  14.2 12.0 %all_to_all.36 = bf16[2,12,64,128]{3,2,1,0:T(8,128)(2,1)S(1)} all-to-all(bf16[2,12,64,128]{3,2,1,0:T(8,128)(2,1)S(1)} %broadcast_in_dim.15), channel_id=1, replica_groups={{4,8},{6,10},{0,12},{2,14},{5,9},{7,11},{1,13},{3,15},{20,24},{22,26},{..., dimensions={0} | all-to-all | bytes 786432 | tf_op jit(solution)/shard_map/all_to_all | solution.py:26
  26.2 6.0 %collective-permute-start = (bf16[24,64,128]{2,1,0:T(8,128)(2,1)S(1)}, bf16[24,64,128]{2,1,0:T(8,128)(2,1)S(1)}, u32[]{:S(2)}, u32[]{:S(2)}) collective-permute-start(bf16[24,64,128]{2,1,0:T(8,128)(2,1)S(1)} %bitcast.9), channel_id=1, source_target_pairs={{0,16},{16,32},{32,48},{48,64},{64,80},{80,96},{96,112},{112,128},... | collective-permute-start | bytes 1179656 | tf_op jit(solution)/shard_map/ppermute | solution.py:15
  35.9 5.1 %collective-permute-start.2 = (bf16[24,64,128]{2,1,0:T(8,128)(2,1)S(1)}, bf16[24,64,128]{2,1,0:T(8,128)(2,1)S(1)}, u32[]{:S(2)}, u32[]{:S(2)}) collective-permute-start(bf16[24,64,128]{2,1,0:T(8,128)(2,1)S(1)} %bitcast.11), channel_id=1, source_target_pairs={{0,14},{2,0},{4,2},{6,4},{8,6},{10,8},{12,10},{14,12},{1,15},{3,1}... | collective-permute-start | bytes 1179656 | tf_op jit(solution)/shard_map/ppermute | solution.py:15
  41.0 6.3 %collective-permute-start.1 = (bf16[24,64,128]{2,1,0:T(8,128)(2,1)S(1)}, bf16[24,64,128]{2,1,0:T(8,128)(2,1)S(1)}, u32[]{:S(2)}, u32[]{:S(2)}) collective-permute-start(bf16[24,64,128]{2,1,0:T(8,128)(2,1)S(1)} %collective-permute-done.refs_0_), channel_id=1, source_target_pairs={{0,2},{2,4},{4,6},{6,8},{8,10},{10,12},{12,14},{14,0},{1,3},{3,5},... | collective-permute-start | bytes 1179656 | tf_op jit(solution)/shard_map/ppermute | solution.py:15
  47.3 4.6 %collective-permute-start.4 = (bf16[24,64,128]{2,1,0:T(8,128)(2,1)S(1)}, bf16[24,64,128]{2,1,0:T(8,128)(2,1)S(1)}, u32[]{:S(2)}, u32[]{:S(2)}) collective-permute-start(bf16[24,64,128]{2,1,0:T(8,128)(2,1)S(1)} %collective-permute-done.3.refs_4_), channel_id=1, source_target_pairs={{0,14},{2,0},{4,2},{6,4},{8,6},{10,8},{12,10},{14,12},{1,15},{3,1}... | collective-permute-start | bytes 1179656 | tf_op jit(solution)/shard_map/ppermute | solution.py:15
  52.6 5.7 %arrange.1 = (bf16[6,32,128,128]{3,2,1,0:T(8,128)(2,1)S(1)}, bf16[6,128,2048]{2,1,0:T(8,128)(2,1)S(1)}) custom-call(s32[1]{0:T(128)} %bitcast.side, bf16[24,64,128]{2,1,0:T(8,128)(2,1)S(1)} %bitcast.12, bf16[6,32,128,128]{3,2,1,0:T(8,128)(2,1)} %over.1), custom_call_target="tpu_custom_call" | custom-call | flops 1000000000 | bytes 9437184 | tf_op jit(solution)/shard_map/arrange/pallas_call | solution.py:90
  58.4 3.4 %collective-permute-done.4.refs_5_ = bf16[24,64,128]{2,1,0:T(8,128)(2,1)S(1)} collective-permute-done((bf16[24,64,128]{2,1,0:T(8,128)(2,1)S(1)}, bf16[24,64,128]{2,1,0:T(8,128)(2,1)S(1)}, u32[]{:S(2)}, u32[]{:S(2)}) %collective-permute-start.4) | collective-permute-done | bytes 393248 | tf_op jit(solution)/shard_map/ppermute | solution.py:15
  61.7 4.5 %couple.3 = (f32[6,64,128]{2,1,0:T(8,128)S(1)}, f32[6,64,128]{2,1,0:T(8,128)S(1)}) custom-call(s32[1]{0:T(128)} %bitcast.side, s32[192]{0:T(256)S(1)} %reshape.83.slots, f32[192]{0:T(256)S(1)} %reshape.84.weights, bf16[6,32,128,128]{3,2,1,0:T(8,128)(2,1)S(1)} %get-tuple-element.12.across, bf16[6,128,2048]{2,1,0:T(8,128)(2,1)S(1)} %get-tuple-element.13.halves, ...), custom_call_target="tpu_custom_call" | custom-call | tf_op jit(solution)/shard_map/couple/pallas_call | solution.py:153
  66.2 2.0 collective-permute-start.5
  69.8 11.4 %all_to_all.37 = bf16[2,6,64,128]{3,2,1,0:T(8,128)(2,1)S(1)} all-to-all(bf16[2,6,64,128]{3,2,1,0:T(8,128)(2,1)S(1)} %broadcast_in_dim.32), channel_id=1, replica_groups={{0,4},{2,6},{8,12},{10,14},{1,5},{3,7},{9,13},{11,15},{16,20},{18,22},{..., dimensions={0} | all-to-all | bytes 393216 | tf_op jit(solution)/shard_map/all_to_all | solution.py:26
  81.4 11.5 %all_to_all.38 = bf16[2,12,64,128]{3,2,1,0:T(8,128)(2,1)S(1)} all-to-all(bf16[2,12,64,128]{3,2,1,0:T(8,128)(2,1)S(1)} %broadcast_in_dim.33), channel_id=1, replica_groups={{4,8},{6,10},{0,12},{2,14},{5,9},{7,11},{1,13},{3,15},{20,24},{22,26},{..., dimensions={0} | all-to-all | bytes 786432 | tf_op jit(solution)/shard_map/all_to_all | solution.py:26
  94.1 6.7 %collective-permute-start.6 = (bf16[24,64,128]{2,1,0:T(8,128)(2,1)S(1)}, bf16[24,64,128]{2,1,0:T(8,128)(2,1)S(1)}, u32[]{:S(2)}, u32[]{:S(2)}) collective-permute-start(bf16[24,64,128]{2,1,0:T(8,128)(2,1)S(1)} %bitcast.19), channel_id=1, source_target_pairs={{0,16},{16,32},{32,48},{48,64},{64,80},{80,96},{96,112},{112,128},... | collective-permute-start | bytes 1179656 | tf_op jit(solution)/shard_map/ppermute | solution.py:15
  100.8 2.8 %collective-permute-start.8 = (bf16[24,64,128]{2,1,0:T(8,128)(2,1)S(1)}, bf16[24,64,128]{2,1,0:T(8,128)(2,1)S(1)}, u32[]{:S(2)}, u32[]{:S(2)}) collective-permute-start(bf16[24,64,128]{2,1,0:T(8,128)(2,1)S(1)} %bitcast.20), channel_id=1, source_target_pairs={{0,14},{2,0},{4,2},{6,4},{8,6},{10,8},{12,10},{14,12},{1,15},{3,1}... | collective-permute-start | bytes 1179656 | tf_op jit(solution)/shard_map/ppermute | solution.py:15
  103.6 3.5 %collective-permute-done.9.refs_4_ = bf16[24,64,128]{2,1,0:T(8,128)(2,1)S(1)} collective-permute-done((bf16[24,64,128]{2,1,0:T(8,128)(2,1)S(1)}, bf16[24,64,128]{2,1,0:T(8,128)(2,1)S(1)}, u32[]{:S(2)}, u32[]{:S(2)}) %collective-permute-start.9) | collective-permute-done | bytes 393248 | tf_op jit(solution)/shard_map/ppermute | solution.py:15
  109.0 4.0 %collective-permute-start.7 = (bf16[24,64,128]{2,1,0:T(8,128)(2,1)S(1)}, bf16[24,64,128]{2,1,0:T(8,128)(2,1)S(1)}, u32[]{:S(2)}, u32[]{:S(2)}) collective-permute-start(bf16[24,64,128]{2,1,0:T(8,128)(2,1)S(1)} %collective-permute-done.6.refs_0_), channel_id=1, source_target_pairs={{0,2},{2,4},{4,6},{6,8},{8,10},{10,12},{12,14},{14,0},{1,3},{3,5},... | collective-permute-start | bytes 1179656 | tf_op jit(solution)/shard_map/ppermute | solution.py:15
  113.0 2.0 collective-permute-done.8.refs_3_
  114.9 5.9 %collective-permute-done.10.refs_5_ = bf16[24,64,128]{2,1,0:T(8,128)(2,1)S(1)} collective-permute-done((bf16[24,64,128]{2,1,0:T(8,128)(2,1)S(1)}, bf16[24,64,128]{2,1,0:T(8,128)(2,1)S(1)}, u32[]{:S(2)}, u32[]{:S(2)}) %collective-permute-start.10) | collective-permute-done | bytes 393248 | tf_op jit(solution)/shard_map/ppermute | solution.py:15
  120.9 2.6 %collective-permute-done.7.refs_1_ = bf16[24,64,128]{2,1,0:T(8,128)(2,1)S(1)} collective-permute-done((bf16[24,64,128]{2,1,0:T(8,128)(2,1)S(1)}, bf16[24,64,128]{2,1,0:T(8,128)(2,1)S(1)}, u32[]{:S(2)}, u32[]{:S(2)}) %collective-permute-start.7) | collective-permute-done | bytes 393248 | tf_op jit(solution)/shard_map/ppermute | solution.py:15
  123.5 4.5 %couple.4 = (f32[6,64,128]{2,1,0:T(8,128)S(1)}, f32[6,64,128]{2,1,0:T(8,128)S(1)}) custom-call(s32[1]{0:T(128)} %bitcast.side, s32[192]{0:T(256)S(1)} %reshape.83.slots, f32[192]{0:T(256)S(1)} %reshape.84.weights, bf16[6,32,128,128]{3,2,1,0:T(8,128)(2,1)S(1)} %get-tuple-element.12.across, bf16[6,128,2048]{2,1,0:T(8,128)(2,1)S(1)} %get-tuple-element.13.halves, ...), custom_call_target="tpu_custom_call" | custom-call | tf_op jit(solution)/shard_map/couple/pallas_call | solution.py:153
  131.6 10.4 %all_to_all.39 = bf16[2,6,64,128]{3,2,1,0:T(8,128)(2,1)S(1)} all-to-all(bf16[2,6,64,128]{3,2,1,0:T(8,128)(2,1)S(1)} %broadcast_in_dim.34), channel_id=1, replica_groups={{0,4},{2,6},{8,12},{10,14},{1,5},{3,7},{9,13},{11,15},{16,20},{18,22},{..., dimensions={0} | all-to-all | bytes 393216 | tf_op jit(solution)/shard_map/all_to_all | solution.py:26
  142.1 10.8 %all_to_all.40 = bf16[2,12,64,128]{3,2,1,0:T(8,128)(2,1)S(1)} all-to-all(bf16[2,12,64,128]{3,2,1,0:T(8,128)(2,1)S(1)} %broadcast_in_dim.35), channel_id=1, replica_groups={{4,8},{6,10},{0,12},{2,14},{5,9},{7,11},{1,13},{3,15},{20,24},{22,26},{..., dimensions={0} | all-to-all | bytes 786432 | tf_op jit(solution)/shard_map/all_to_all | solution.py:26
  153.0 7.3 %collective-permute-start.12 = (bf16[24,64,128]{2,1,0:T(8,128)(2,1)S(1)}, bf16[24,64,128]{2,1,0:T(8,128)(2,1)S(1)}, u32[]{:S(2)}, u32[]{:S(2)}) collective-permute-start(bf16[24,64,128]{2,1,0:T(8,128)(2,1)S(1)} %bitcast.14), channel_id=1, source_target_pairs={{0,16},{16,32},{32,48},{48,64},{64,80},{80,96},{96,112},{112,128},... | collective-permute-start | bytes 1179656 | tf_op jit(solution)/shard_map/ppermute | solution.py:15
  161.6 4.5 %collective-permute-start.14 = (bf16[24,64,128]{2,1,0:T(8,128)(2,1)S(1)}, bf16[24,64,128]{2,1,0:T(8,128)(2,1)S(1)}, u32[]{:S(2)}, u32[]{:S(2)}) collective-permute-start(bf16[24,64,128]{2,1,0:T(8,128)(2,1)S(1)} %bitcast.16), channel_id=1, source_target_pairs={{0,14},{2,0},{4,2},{6,4},{8,6},{10,8},{12,10},{14,12},{1,15},{3,1}... | collective-permute-start | bytes 1179656 | tf_op jit(solution)/shard_map/ppermute | solution.py:15
  166.0 2.3 collective-permute-done.12.refs_0_
  168.3 5.7 %collective-permute-start.13 = (bf16[24,64,128]{2,1,0:T(8,128)(2,1)S(1)}, bf16[24,64,128]{2,1,0:T(8,128)(2,1)S(1)}, u32[]{:S(2)}, u32[]{:S(2)}) collective-permute-start(bf16[24,64,128]{2,1,0:T(8,128)(2,1)S(1)} %collective-permute-done.12.refs_0_), channel_id=1, source_target_pairs={{0,2},{2,4},{4,6},{6,8},{8,10},{10,12},{12,14},{14,0},{1,3},{3,5},... | collective-permute-start | bytes 1179656 | tf_op jit(solution)/shard_map/ppermute | solution.py:15
  174.8 3.7 %collective-permute-start.16 = (bf16[24,64,128]{2,1,0:T(8,128)(2,1)S(1)}, bf16[24,64,128]{2,1,0:T(8,128)(2,1)S(1)}, u32[]{:S(2)}, u32[]{:S(2)}) collective-permute-start(bf16[24,64,128]{2,1,0:T(8,128)(2,1)S(1)} %collective-permute-done.15.refs_4_), channel_id=1, source_target_pairs={{0,14},{2,0},{4,2},{6,4},{8,6},{10,8},{12,10},{14,12},{1,15},{3,1}... | collective-permute-start | bytes 1179656 | tf_op jit(solution)/shard_map/ppermute | solution.py:15
  178.6 2.6 %collective-permute-done.13.refs_1_ = bf16[24,64,128]{2,1,0:T(8,128)(2,1)S(1)} collective-permute-done((bf16[24,64,128]{2,1,0:T(8,128)(2,1)S(1)}, bf16[24,64,128]{2,1,0:T(8,128)(2,1)S(1)}, u32[]{:S(2)}, u32[]{:S(2)}) %collective-permute-start.13) | collective-permute-done | bytes 393248 | tf_op jit(solution)/shard_map/ppermute | solution.py:15
  181.2 6.6 %collective-permute-done.16.refs_5_ = bf16[24,64,128]{2,1,0:T(8,128)(2,1)S(1)} collective-permute-done((bf16[24,64,128]{2,1,0:T(8,128)(2,1)S(1)}, bf16[24,64,128]{2,1,0:T(8,128)(2,1)S(1)}, u32[]{:S(2)}, u32[]{:S(2)}) %collective-permute-start.16) | collective-permute-done | bytes 393248 | tf_op jit(solution)/shard_map/ppermute | solution.py:15
  187.8 4.5 %couple.5 = (f32[6,64,128]{2,1,0:T(8,128)S(1)}, f32[6,64,128]{2,1,0:T(8,128)S(1)}) custom-call(s32[1]{0:T(128)} %bitcast.side, s32[192]{0:T(256)S(1)} %reshape.83.slots, f32[192]{0:T(256)S(1)} %reshape.84.weights, bf16[6,32,128,128]{3,2,1,0:T(8,128)(2,1)S(1)} %get-tuple-element.12.across, bf16[6,128,2048]{2,1,0:T(8,128)(2,1)S(1)} %get-tuple-element.13.halves, ...), custom_call_target="tpu_custom_call" | custom-call | tf_op jit(solution)/shard_map/couple/pallas_call | solution.py:153
  195.9 2.1 collective-permute-start.18
  199.1 56.2 %all_to_all.41.copies = f32[128,1,128]{2,1,0:T(1,128)S(1)} all-to-all(f32[128,1,128]{2,1,0:T(1,128)S(1)} %broadcast_in_dim.36), channel_id=1, replica_groups=mesh['job'=2,'chain'=16,'pair'=8,'pno'=2] {'chain','pair'}, dimensions={0} | all-to-all | bytes 131072 | tf_op jit(solution)/shard_map/all_to_all | solution.py:281
  (50 shorter events, 23.3 us)
Async XLA Ops:
  0.6 0.9 copy-start
  1.5 0.7 copy-start.1
  26.2 14.8 %collective-permute-start = (bf16[24,64,128]{2,1,0:T(8,128)(2,1)S(1)}, bf16[24,64,128]{2,1,0:T(8,128)(2,1)S(1)}, u32[]{:S(2)}, u32[]{:S(2)}) collective-permute-start(bf16[24,64,128]{2,1,0:T(8,128)(2,1)S(1)} %bitcast.9), channel_id=1, source_target_pairs={{0,16},{16,32},{32,48},{48,64},{64,80},{80,96},{96,112},{112,128},... | collective-permute-start | bytes 1179656 | tf_op jit(solution)/shard_map/ppermute | solution.py:15
  32.2 15.1 %collective-permute-start.3 = (bf16[24,64,128]{2,1,0:T(8,128)(2,1)S(1)}, bf16[24,64,128]{2,1,0:T(8,128)(2,1)S(1)}, u32[]{:S(2)}, u32[]{:S(2)}) collective-permute-start(bf16[24,64,128]{2,1,0:T(8,128)(2,1)S(1)} %bitcast.10), channel_id=1, source_target_pairs={{16,0},{32,16},{48,32},{64,48},{80,64},{96,80},{112,96},{128,112},... | collective-permute-start | bytes 1179656 | tf_op jit(solution)/shard_map/ppermute | solution.py:15
  35.9 22.4 %collective-permute-start.2 = (bf16[24,64,128]{2,1,0:T(8,128)(2,1)S(1)}, bf16[24,64,128]{2,1,0:T(8,128)(2,1)S(1)}, u32[]{:S(2)}, u32[]{:S(2)}) collective-permute-start(bf16[24,64,128]{2,1,0:T(8,128)(2,1)S(1)} %bitcast.11), channel_id=1, source_target_pairs={{0,14},{2,0},{4,2},{6,4},{8,6},{10,8},{12,10},{14,12},{1,15},{3,1}... | collective-permute-start | bytes 1179656 | tf_op jit(solution)/shard_map/ppermute | solution.py:15
  41.0 17.3 %collective-permute-start.1 = (bf16[24,64,128]{2,1,0:T(8,128)(2,1)S(1)}, bf16[24,64,128]{2,1,0:T(8,128)(2,1)S(1)}, u32[]{:S(2)}, u32[]{:S(2)}) collective-permute-start(bf16[24,64,128]{2,1,0:T(8,128)(2,1)S(1)} %collective-permute-done.refs_0_), channel_id=1, source_target_pairs={{0,2},{2,4},{4,6},{6,8},{8,10},{10,12},{12,14},{14,0},{1,3},{3,5},... | collective-permute-start | bytes 1179656 | tf_op jit(solution)/shard_map/ppermute | solution.py:15
  47.3 14.4 %collective-permute-start.4 = (bf16[24,64,128]{2,1,0:T(8,128)(2,1)S(1)}, bf16[24,64,128]{2,1,0:T(8,128)(2,1)S(1)}, u32[]{:S(2)}, u32[]{:S(2)}) collective-permute-start(bf16[24,64,128]{2,1,0:T(8,128)(2,1)S(1)} %collective-permute-done.3.refs_4_), channel_id=1, source_target_pairs={{0,14},{2,0},{4,2},{6,4},{8,6},{10,8},{12,10},{14,12},{1,15},{3,1}... | collective-permute-start | bytes 1179656 | tf_op jit(solution)/shard_map/ppermute | solution.py:15
  58.3 9.9 %copy-start.2 = (s32[6]{0:T(128)S(1)}, s32[6]{0:T(128)}, u32[]{:S(2)}) copy-start(s32[6]{0:T(128)} %ranks.1) | copy-start | bytes 76
  58.3 11.3 %copy-start.3 = (bf16[6,64,128]{2,1,0:T(8,128)(2,1)S(1)}, bf16[6,64,128]{2,1,0:T(8,128)(2,1)}, u32[]{:S(2)}) copy-start(bf16[6,64,128]{2,1,0:T(8,128)(2,1)} %param.9) | copy-start | bytes 294916
  58.3 11.3 %copy-start.4 = (f32[6,128]{1,0:T(8,128)S(1)}, f32[6,128]{1,0:T(8,128)}, u32[]{:S(2)}) copy-start(f32[6,128]{1,0:T(8,128)} %param.12) | copy-start | bytes 9220
  58.3 11.3 %copy-start.5 = (f32[6]{0:T(128)S(1)}, f32[6]{0:T(128)}, u32[]{:S(2)}) copy-start(f32[6]{0:T(128)} %param.13) | copy-start | bytes 76
  66.2 3.4 %collective-permute-start.5 = (f32[6,64,128]{2,1,0:T(8,128)S(1)}, f32[6,64,128]{2,1,0:T(8,128)S(1)}, u32[]{:S(2)}, u32[]{:S(2)}) collective-permute-start(f32[6,64,128]{2,1,0:T(8,128)S(1)} %get-tuple-element.15), channel_id=1, source_target_pairs={{0,1},{1,0},{2,3},{3,2},{4,5},{5,4},{6,7},{7,6},{8,9},{9,8},{10,11... | collective-permute-start | bytes 589832 | tf_op jit(solution)/shard_map/ppermute | solution.py:15
  92.8 14.2 %collective-permute-start.9 = (bf16[24,64,128]{2,1,0:T(8,128)(2,1)S(1)}, bf16[24,64,128]{2,1,0:T(8,128)(2,1)S(1)}, u32[]{:S(2)}, u32[]{:S(2)}) collective-permute-start(bf16[24,64,128]{2,1,0:T(8,128)(2,1)S(1)} %bitcast.18), channel_id=1, source_target_pairs={{16,0},{32,16},{48,32},{64,48},{80,64},{96,80},{112,96},{128,112},... | collective-permute-start | bytes 1179656 | tf_op jit(solution)/shard_map/ppermute | solution.py:15
  94.1 14.9 %collective-permute-start.6 = (bf16[24,64,128]{2,1,0:T(8,128)(2,1)S(1)}, bf16[24,64,128]{2,1,0:T(8,128)(2,1)S(1)}, u32[]{:S(2)}, u32[]{:S(2)}) collective-permute-start(bf16[24,64,128]{2,1,0:T(8,128)(2,1)S(1)} %bitcast.19), channel_id=1, source_target_pairs={{0,16},{16,32},{32,48},{48,64},{64,80},{80,96},{96,112},{112,128},... | collective-permute-start | bytes 1179656 | tf_op jit(solution)/shard_map/ppermute | solution.py:15
  100.8 14.1 %collective-permute-start.8 = (bf16[24,64,128]{2,1,0:T(8,128)(2,1)S(1)}, bf16[24,64,128]{2,1,0:T(8,128)(2,1)S(1)}, u32[]{:S(2)}, u32[]{:S(2)}) collective-permute-start(bf16[24,64,128]{2,1,0:T(8,128)(2,1)S(1)} %bitcast.20), channel_id=1, source_target_pairs={{0,14},{2,0},{4,2},{6,4},{8,6},{10,8},{12,10},{14,12},{1,15},{3,1}... | collective-permute-start | bytes 1179656 | tf_op jit(solution)/shard_map/ppermute | solution.py:15
  107.1 13.8 %collective-permute-start.10 = (bf16[24,64,128]{2,1,0:T(8,128)(2,1)S(1)}, bf16[24,64,128]{2,1,0:T(8,128)(2,1)S(1)}, u32[]{:S(2)}, u32[]{:S(2)}) collective-permute-start(bf16[24,64,128]{2,1,0:T(8,128)(2,1)S(1)} %collective-permute-done.9.refs_4_), channel_id=1, source_target_pairs={{0,14},{2,0},{4,2},{6,4},{8,6},{10,8},{12,10},{14,12},{1,15},{3,1}... | collective-permute-start | bytes 1179656 | tf_op jit(solution)/shard_map/ppermute | solution.py:15
  109.0 14.5 %collective-permute-start.7 = (bf16[24,64,128]{2,1,0:T(8,128)(2,1)S(1)}, bf16[24,64,128]{2,1,0:T(8,128)(2,1)S(1)}, u32[]{:S(2)}, u32[]{:S(2)}) collective-permute-start(bf16[24,64,128]{2,1,0:T(8,128)(2,1)S(1)} %collective-permute-done.6.refs_0_), channel_id=1, source_target_pairs={{0,2},{2,4},{4,6},{6,8},{8,10},{10,12},{12,14},{14,0},{1,3},{3,5},... | collective-permute-start | bytes 1179656 | tf_op jit(solution)/shard_map/ppermute | solution.py:15
  128.0 3.4 %collective-permute-start.11 = (f32[6,64,128]{2,1,0:T(8,128)S(1)}, f32[6,64,128]{2,1,0:T(8,128)S(1)}, u32[]{:S(2)}, u32[]{:S(2)}) collective-permute-start(f32[6,64,128]{2,1,0:T(8,128)S(1)} %get-tuple-element.17), channel_id=1, source_target_pairs={{0,1},{1,0},{2,3},{3,2},{4,5},{5,4},{6,7},{7,6},{8,9},{9,8},{10,11... | collective-permute-start | bytes 589832 | tf_op jit(solution)/shard_map/ppermute | solution.py:15
  153.0 15.4 %collective-permute-start.12 = (bf16[24,64,128]{2,1,0:T(8,128)(2,1)S(1)}, bf16[24,64,128]{2,1,0:T(8,128)(2,1)S(1)}, u32[]{:S(2)}, u32[]{:S(2)}) collective-permute-start(bf16[24,64,128]{2,1,0:T(8,128)(2,1)S(1)} %bitcast.14), channel_id=1, source_target_pairs={{0,16},{16,32},{32,48},{48,64},{64,80},{80,96},{96,112},{112,128},... | collective-permute-start | bytes 1179656 | tf_op jit(solution)/shard_map/ppermute | solution.py:15
  160.2 14.6 %collective-permute-start.15 = (bf16[24,64,128]{2,1,0:T(8,128)(2,1)S(1)}, bf16[24,64,128]{2,1,0:T(8,128)(2,1)S(1)}, u32[]{:S(2)}, u32[]{:S(2)}) collective-permute-start(bf16[24,64,128]{2,1,0:T(8,128)(2,1)S(1)} %bitcast.15), channel_id=1, source_target_pairs={{16,0},{32,16},{48,32},{64,48},{80,64},{96,80},{112,96},{128,112},... | collective-permute-start | bytes 1179656 | tf_op jit(solution)/shard_map/ppermute | solution.py:15
  161.6 17.0 %collective-permute-start.14 = (bf16[24,64,128]{2,1,0:T(8,128)(2,1)S(1)}, bf16[24,64,128]{2,1,0:T(8,128)(2,1)S(1)}, u32[]{:S(2)}, u32[]{:S(2)}) collective-permute-start(bf16[24,64,128]{2,1,0:T(8,128)(2,1)S(1)} %bitcast.16), channel_id=1, source_target_pairs={{0,14},{2,0},{4,2},{6,4},{8,6},{10,8},{12,10},{14,12},{1,15},{3,1}... | collective-permute-start | bytes 1179656 | tf_op jit(solution)/shard_map/ppermute | solution.py:15
  168.3 12.9 %collective-permute-start.13 = (bf16[24,64,128]{2,1,0:T(8,128)(2,1)S(1)}, bf16[24,64,128]{2,1,0:T(8,128)(2,1)S(1)}, u32[]{:S(2)}, u32[]{:S(2)}) collective-permute-start(bf16[24,64,128]{2,1,0:T(8,128)(2,1)S(1)} %collective-permute-done.12.refs_0_), channel_id=1, source_target_pairs={{0,2},{2,4},{4,6},{6,8},{8,10},{10,12},{12,14},{14,0},{1,3},{3,5},... | collective-permute-start | bytes 1179656 | tf_op jit(solution)/shard_map/ppermute | solution.py:15
  174.8 12.9 %collective-permute-start.16 = (bf16[24,64,128]{2,1,0:T(8,128)(2,1)S(1)}, bf16[24,64,128]{2,1,0:T(8,128)(2,1)S(1)}, u32[]{:S(2)}, u32[]{:S(2)}) collective-permute-start(bf16[24,64,128]{2,1,0:T(8,128)(2,1)S(1)} %collective-permute-done.15.refs_4_), channel_id=1, source_target_pairs={{0,14},{2,0},{4,2},{6,4},{8,6},{10,8},{12,10},{14,12},{1,15},{3,1}... | collective-permute-start | bytes 1179656 | tf_op jit(solution)/shard_map/ppermute | solution.py:15
  192.3 3.4 %collective-permute-start.17 = (f32[6,64,128]{2,1,0:T(8,128)S(1)}, f32[6,64,128]{2,1,0:T(8,128)S(1)}, u32[]{:S(2)}, u32[]{:S(2)}) collective-permute-start(f32[6,64,128]{2,1,0:T(8,128)S(1)} %get-tuple-element.19), channel_id=1, source_target_pairs={{0,1},{1,0},{2,3},{3,2},{4,5},{5,4},{6,7},{7,6},{8,9},{9,8},{10,11... | collective-permute-start | bytes 589832 | tf_op jit(solution)/shard_map/ppermute | solution.py:15
  195.9 3.1 %collective-permute-start.18 = (f32[1,128]{1,0:T(1,128)S(1)}, f32[1,128]{1,0:T(1,128)S(1)}, u32[]{:S(2)}, u32[]{:S(2)}) collective-permute-start(f32[1,128]{1,0:T(1,128)S(1)} %get-tuple-element.20), channel_id=1, source_target_pairs={{0,1},{1,0},{2,3},{3,2},{4,5},{5,4},{6,7},{7,6},{8,9},{9,8},{10,11... | collective-permute-start | bytes 1544 | tf_op jit(solution)/shard_map/ppermute | solution.py:15

commit v5 on v4

--- a/solution.py
+++ b/solution.py
@@ -15,22 +15,14 @@
     return lax.ppermute(value, axis, pairs)
 
 
-def joined(value, step, first):
+def spread(piece):
     count = lax.axis_size("pair")
-    groups = []
-    for start in range(first, first + count, 2 * step):
-        for parity in range(step):
-            left, right = (start + parity) % count, (start + step + parity) % count
-            groups.append(sorted([left, right]))
-    both = jnp.broadcast_to(value, (2, *value.shape))
-    both = lax.all_to_all(both, "pair", 0, 0, tiled=True, axis_index_groups=groups)
-    return both.reshape(-1, *value.shape[1:])
-
-
-def spread(piece):
-    near = joined(joined(piece, 2, 0), 2, 2)
+    groups = [list(range(first, count, 2)) for first in range(2)]
+    copies = jnp.broadcast_to(piece, (len(groups[0]), *piece.shape))
+    near = lax.all_to_all(copies, "pair", 0, 0, tiled=True, axis_index_groups=groups)
+    near = near.reshape(-1, *piece.shape[1:])
     low, high = shifted(near, "chain", 1), shifted(near, "chain", -1)
-    other = shifted(near, "pair", -1, around=True)
+    other = shifted(near, "pair", 1, around=True)
     low_other = shifted(low, "pair", 1, around=True)
     high_other = shifted(high, "pair", -1, around=True)
     return low, low_other, near, other, high, high_other
@@ -168,14 +160,14 @@
     held, (last, sums) = refs[:-2], refs[-2:]
     last[...] = mask[...] * (mine[...] + theirs[...]) - held[-1][...]
     terms = [ref[...] * scale for ref in held] + [last[...] * scale]
-    lane = lax.broadcasted_iota(jnp.int32, sums.shape, 1)
+    lane = lax.broadcasted_iota(jnp.int32, sums.shape, 2)
     row = jnp.zeros(sums.shape, jnp.float32)
     for place, (i, j) in enumerate(PRODUCTS):
         row = jnp.where(lane == place, jnp.sum(terms[i] * terms[j]), row)
     sums[...] = row
 
 
-def products(scale, mine, theirs, mask, held):
+def products(scale, mine, theirs, mask, held, count):
     shape = mask.shape
     inside = pl.BlockSpec(memory_space=pltpu.VMEM)
     return pl.pallas_call(
@@ -184,7 +176,7 @@
         out_specs=(inside, inside),
         out_shape=(
             jax.ShapeDtypeStruct(shape, jnp.float32),
-            jax.ShapeDtypeStruct((1, shape[-1]), jnp.float32),
+            jax.ShapeDtypeStruct((count, 1, shape[-1]), jnp.float32),
         ),
         compiler_params=pltpu.CompilerParams(vmem_limit_bytes=8 * 1024 * 1024),
         name="products",
@@ -274,11 +266,12 @@
         mine, theirs = coupled_parts((terms[-1] / denom).astype(jnp.bfloat16))
         if step_no + 1 < ITERS:
             terms.append(mask * (mine + theirs) - terms[-1])
-    last, sums = products(cells**-0.5, mine, theirs, mask, terms)
-    sums = sums + shifted(sums, "pno", 1, around=True)
-    rest = ("chain", "pair")
-    sums = jnp.broadcast_to(sums, (lax.axis_size(rest), *sums.shape))
-    return tuple(finish(lax.all_to_all(sums, rest, 0, 0, tiled=True), own, denom, terms + [last]))
+    lines = lax.axis_size("chain") * lax.axis_size("pno")
+    last, sums = products(cells**-0.5, mine, theirs, mask, terms, lines)
+    sums = lax.all_to_all(sums, ("chain", "pno"), 0, 0, tiled=True)
+    sums = jnp.broadcast_to(jnp.sum(sums, axis=0), (lax.axis_size("pair"), 1, width))
+    sums = lax.all_to_all(sums, "pair", 0, 0, tiled=True)
+    return tuple(finish(sums, own, denom, terms + [last]))
 
 
 def solution(mesh):

time: 258 us -> 237 us (0.919)
  starting transfers between devices: 70.3 us -> 49.9 us
  blocking collectives: 124 us -> 115 us
  waiting for transfers between devices: 34.7 us -> 43.3 us
    ppermute x19 -> x18, starting transfers between devices: 70.3 us -> 49.9 us  [shifted(): return lax.ppermute(value, axis, pairs)]
    all_to_all x7 -> x5, blocking collectives: 124 us -> 115 us  [the longest x3 57.6 us: spread(): lax.all_to_all(copies, 'pair', 0, 0, tiled=True, axis_index_groups=groups)]
    ppermute x19 -> x18, waiting for transfers between devices: 34.7 us -> 43.3 us  [shifted(): return lax.ppermute(value, axis, pairs)]
  transfers between devices with their start and end apart: 19 -> 18, of which waited for: 13 -> 15; matrix products, arithmetic and copies ran while one was open for 1% -> 1% of each run, Pallas kernels for 2% -> 2%
where the time goes in v5:
time: 237 us; the launch traced here: 236 us
  blocking collectives  115 us (49%)
  starting transfers between devices  49.9 us (21%)
  waiting for transfers between devices  43.3 us (18%)
  Pallas kernels  21.1 us (9%)
  local copies, waits for them, and re-layouts  3.4 us (1%)
    all_to_all x3, blocking collectives, spread(): lax.all_to_all(copies, 'pair', 0, 0, tiled=True, axis_index_groups=groups)  57.6 us
    ppermute x18, starting transfers between devices, shifted(): return lax.ppermute(value, axis, pairs)  49.9 us
    all_to_all x1, blocking collectives, per_device(): sums = lax.all_to_all(sums, ('chain', 'pno'), 0, 0, tiled=True)  45 us
    ppermute x18, waiting for transfers between devices, shifted(): return lax.ppermute(value, axis, pairs)  43.3 us
    pallas_call x3, Pallas kernels, couple(): pl.pallas_call(couple_kernel, in_specs=[scalars] * 3 + [inside] * (2 + le...  13.5 us
    all_to_all x1, blocking collectives, per_device(): sums = lax.all_to_all(sums, 'pair', 0, 0, tiled=True)  12.2 us
    pallas_call x1, Pallas kernels, arrange(): pl.pallas_call(arrange_kernel, grid_spec=pltpu.PrefetchScalarGridSpec(num...  5.67 us
  transfers between devices with their start and end apart: 18, of which 15 were waited for; matrix products, arithmetic and copies ran while one was open for 1% of the time, Pallas kernels for 2%

profile of v5, /device:TPU:80, one launch (start us, length us, event | category | flops | bytes accessed | tf_op | source)
XLA Modules:
  0.0 235.5 jit_solution(16871830469857854206)
XLA Ops:
  2.8 20.7 %all_to_all.25 = bf16[4,6,64,128]{3,2,1,0:T(8,128)(2,1)S(1)} all-to-all(bf16[4,6,64,128]{3,2,1,0:T(8,128)(2,1)S(1)} %broadcast_in_dim.8), channel_id=1, replica_groups={{0,4,8,12},{2,6,10,14},{1,5,9,13},{3,7,11,15},{16,20,24,28},{18,22,26,3..., dimensions={0} | all-to-all | bytes 786432 | tf_op jit(solution)/shard_map/all_to_all | solution.py:22
  23.6 6.0 %collective-permute-start = (bf16[24,64,128]{2,1,0:T(8,128)(2,1)S(1)}, bf16[24,64,128]{2,1,0:T(8,128)(2,1)S(1)}, u32[]{:S(2)}, u32[]{:S(2)}) collective-permute-start(bf16[24,64,128]{2,1,0:T(8,128)(2,1)S(1)} %bitcast.4), channel_id=1, source_target_pairs={{0,16},{16,32},{32,48},{48,64},{64,80},{80,96},{96,112},{112,128},... | collective-permute-start | bytes 1179656 | tf_op jit(solution)/shard_map/ppermute | solution.py:15
  33.3 2.0 collective-permute-start.2
  36.6 2.6 %collective-permute-start.1 = (bf16[24,64,128]{2,1,0:T(8,128)(2,1)S(1)}, bf16[24,64,128]{2,1,0:T(8,128)(2,1)S(1)}, u32[]{:S(2)}, u32[]{:S(2)}) collective-permute-start(bf16[24,64,128]{2,1,0:T(8,128)(2,1)S(1)} %collective-permute-done.refs_0_), channel_id=1, source_target_pairs={{0,2},{2,4},{4,6},{6,8},{8,10},{10,12},{12,14},{14,0},{1,3},{3,5},... | collective-permute-start | bytes 1179656 | tf_op jit(solution)/shard_map/ppermute | solution.py:15
  39.2 3.9 %collective-permute-done.3.refs_4_ = bf16[24,64,128]{2,1,0:T(8,128)(2,1)S(1)} collective-permute-done((bf16[24,64,128]{2,1,0:T(8,128)(2,1)S(1)}, bf16[24,64,128]{2,1,0:T(8,128)(2,1)S(1)}, u32[]{:S(2)}, u32[]{:S(2)}) %collective-permute-start.3) | collective-permute-done | bytes 393248 | tf_op jit(solution)/shard_map/ppermute | solution.py:15
  43.1 1.9 collective-permute-start.4
  45.8 5.7 %arrange.1 = (bf16[6,32,128,128]{3,2,1,0:T(8,128)(2,1)S(1)}, bf16[6,128,2048]{2,1,0:T(8,128)(2,1)S(1)}) custom-call(s32[1]{0:T(128)} %bitcast.side, bf16[24,64,128]{2,1,0:T(8,128)(2,1)S(1)} %bitcast.7, bf16[6,32,128,128]{3,2,1,0:T(8,128)(2,1)} %over.1), custom_call_target="tpu_custom_call" | custom-call | flops 1000000000 | bytes 9437184 | tf_op jit(solution)/shard_map/arrange/pallas_call | solution.py:82
  51.6 2.5 %collective-permute-done.1.refs_1_ = bf16[24,64,128]{2,1,0:T(8,128)(2,1)S(1)} collective-permute-done((bf16[24,64,128]{2,1,0:T(8,128)(2,1)S(1)}, bf16[24,64,128]{2,1,0:T(8,128)(2,1)S(1)}, u32[]{:S(2)}, u32[]{:S(2)}) %collective-permute-start.1) | collective-permute-done | bytes 393248 | tf_op jit(solution)/shard_map/ppermute | solution.py:15
  54.1 4.5 %couple.3 = (f32[6,64,128]{2,1,0:T(8,128)S(1)}, f32[6,64,128]{2,1,0:T(8,128)S(1)}) custom-call(s32[1]{0:T(128)} %bitcast.side, s32[192]{0:T(256)S(1)} %reshape.76.slots, f32[192]{0:T(256)S(1)} %reshape.77.weights, bf16[6,32,128,128]{3,2,1,0:T(8,128)(2,1)S(1)} %get-tuple-element.12.across, bf16[6,128,2048]{2,1,0:T(8,128)(2,1)S(1)} %get-tuple-element.13.halves, ...), custom_call_target="tpu_custom_call" | custom-call | tf_op jit(solution)/shard_map/couple/pallas_call | solution.py:145
  58.6 2.0 collective-permute-start.5
  62.2 18.7 %all_to_all.26 = bf16[4,6,64,128]{3,2,1,0:T(8,128)(2,1)S(1)} all-to-all(bf16[4,6,64,128]{3,2,1,0:T(8,128)(2,1)S(1)} %broadcast_in_dim.9), channel_id=1, replica_groups={{0,4,8,12},{2,6,10,14},{1,5,9,13},{3,7,11,15},{16,20,24,28},{18,22,26,3..., dimensions={0} | all-to-all | bytes 786432 | tf_op jit(solution)/shard_map/all_to_all | solution.py:22
  82.3 6.7 %collective-permute-start.6 = (bf16[24,64,128]{2,1,0:T(8,128)(2,1)S(1)}, bf16[24,64,128]{2,1,0:T(8,128)(2,1)S(1)}, u32[]{:S(2)}, u32[]{:S(2)}) collective-permute-start(bf16[24,64,128]{2,1,0:T(8,128)(2,1)S(1)} %bitcast.14), channel_id=1, source_target_pairs={{0,16},{16,32},{32,48},{48,64},{64,80},{80,96},{96,112},{112,128},... | collective-permute-start | bytes 1179656 | tf_op jit(solution)/shard_map/ppermute | solution.py:15
  89.0 2.0 collective-permute-start.8
  90.9 3.9 %collective-permute-done.9.refs_4_ = bf16[24,64,128]{2,1,0:T(8,128)(2,1)S(1)} collective-permute-done((bf16[24,64,128]{2,1,0:T(8,128)(2,1)S(1)}, bf16[24,64,128]{2,1,0:T(8,128)(2,1)S(1)}, u32[]{:S(2)}, u32[]{:S(2)}) %collective-permute-start.9) | collective-permute-done | bytes 393248 | tf_op jit(solution)/shard_map/ppermute | solution.py:15
  94.8 1.9 collective-permute-start.10
  96.8 4.0 %collective-permute-start.7 = (bf16[24,64,128]{2,1,0:T(8,128)(2,1)S(1)}, bf16[24,64,128]{2,1,0:T(8,128)(2,1)S(1)}, u32[]{:S(2)}, u32[]{:S(2)}) collective-permute-start(bf16[24,64,128]{2,1,0:T(8,128)(2,1)S(1)} %collective-permute-done.6.refs_0_), channel_id=1, source_target_pairs={{0,2},{2,4},{4,6},{6,8},{8,10},{10,12},{12,14},{14,0},{1,3},{3,5},... | collective-permute-start | bytes 1179656 | tf_op jit(solution)/shard_map/ppermute | solution.py:15
  102.3 3.4 %collective-permute-done.10.refs_5_ = bf16[24,64,128]{2,1,0:T(8,128)(2,1)S(1)} collective-permute-done((bf16[24,64,128]{2,1,0:T(8,128)(2,1)S(1)}, bf16[24,64,128]{2,1,0:T(8,128)(2,1)S(1)}, u32[]{:S(2)}, u32[]{:S(2)}) %collective-permute-start.10) | collective-permute-done | bytes 393248 | tf_op jit(solution)/shard_map/ppermute | solution.py:15
  105.7 4.1 %collective-permute-done.7.refs_1_ = bf16[24,64,128]{2,1,0:T(8,128)(2,1)S(1)} collective-permute-done((bf16[24,64,128]{2,1,0:T(8,128)(2,1)S(1)}, bf16[24,64,128]{2,1,0:T(8,128)(2,1)S(1)}, u32[]{:S(2)}, u32[]{:S(2)}) %collective-permute-start.7) | collective-permute-done | bytes 393248 | tf_op jit(solution)/shard_map/ppermute | solution.py:15
  109.8 4.5 %couple.4 = (f32[6,64,128]{2,1,0:T(8,128)S(1)}, f32[6,64,128]{2,1,0:T(8,128)S(1)}) custom-call(s32[1]{0:T(128)} %bitcast.side, s32[192]{0:T(256)S(1)} %reshape.76.slots, f32[192]{0:T(256)S(1)} %reshape.77.weights, bf16[6,32,128,128]{3,2,1,0:T(8,128)(2,1)S(1)} %get-tuple-element.12.across, bf16[6,128,2048]{2,1,0:T(8,128)(2,1)S(1)} %get-tuple-element.13.halves, ...), custom_call_target="tpu_custom_call" | custom-call | tf_op jit(solution)/shard_map/couple/pallas_call | solution.py:145
  114.3 2.0 collective-permute-start.11
  118.0 18.1 %all_to_all.27 = bf16[4,6,64,128]{3,2,1,0:T(8,128)(2,1)S(1)} all-to-all(bf16[4,6,64,128]{3,2,1,0:T(8,128)(2,1)S(1)} %broadcast_in_dim.10), channel_id=1, replica_groups={{0,4,8,12},{2,6,10,14},{1,5,9,13},{3,7,11,15},{16,20,24,28},{18,22,26,3..., dimensions={0} | all-to-all | bytes 786432 | tf_op jit(solution)/shard_map/all_to_all | solution.py:22
  136.1 7.2 %collective-permute-start.12 = (bf16[24,64,128]{2,1,0:T(8,128)(2,1)S(1)}, bf16[24,64,128]{2,1,0:T(8,128)(2,1)S(1)}, u32[]{:S(2)}, u32[]{:S(2)}) collective-permute-start(bf16[24,64,128]{2,1,0:T(8,128)(2,1)S(1)} %bitcast.9), channel_id=1, source_target_pairs={{0,16},{16,32},{32,48},{48,64},{64,80},{80,96},{96,112},{112,128},... | collective-permute-start | bytes 1179656 | tf_op jit(solution)/shard_map/ppermute | solution.py:15
  144.7 2.0 collective-permute-start.14
  146.6 4.5 %collective-permute-done.12.refs_0_ = bf16[24,64,128]{2,1,0:T(8,128)(2,1)S(1)} collective-permute-done((bf16[24,64,128]{2,1,0:T(8,128)(2,1)S(1)}, bf16[24,64,128]{2,1,0:T(8,128)(2,1)S(1)}, u32[]{:S(2)}, u32[]{:S(2)}) %collective-permute-start.12) | collective-permute-done | bytes 393248 | tf_op jit(solution)/shard_map/ppermute | solution.py:15
  153.1 4.6 %collective-permute-done.15.refs_4_ = bf16[24,64,128]{2,1,0:T(8,128)(2,1)S(1)} collective-permute-done((bf16[24,64,128]{2,1,0:T(8,128)(2,1)S(1)}, bf16[24,64,128]{2,1,0:T(8,128)(2,1)S(1)}, u32[]{:S(2)}, u32[]{:S(2)}) %collective-permute-start.15) | collective-permute-done | bytes 393248 | tf_op jit(solution)/shard_map/ppermute | solution.py:15
  157.6 1.9 collective-permute-start.16
  159.8 6.5 %collective-permute-done.13.refs_1_ = bf16[24,64,128]{2,1,0:T(8,128)(2,1)S(1)} collective-permute-done((bf16[24,64,128]{2,1,0:T(8,128)(2,1)S(1)}, bf16[24,64,128]{2,1,0:T(8,128)(2,1)S(1)}, u32[]{:S(2)}, u32[]{:S(2)}) %collective-permute-start.13) | collective-permute-done | bytes 393248 | tf_op jit(solution)/shard_map/ppermute | solution.py:15
  166.2 2.8 %collective-permute-done.16.refs_5_ = bf16[24,64,128]{2,1,0:T(8,128)(2,1)S(1)} collective-permute-done((bf16[24,64,128]{2,1,0:T(8,128)(2,1)S(1)}, bf16[24,64,128]{2,1,0:T(8,128)(2,1)S(1)}, u32[]{:S(2)}, u32[]{:S(2)}) %collective-permute-start.16) | collective-permute-done | bytes 393248 | tf_op jit(solution)/shard_map/ppermute | solution.py:15
  169.0 4.5 %couple.5 = (f32[6,64,128]{2,1,0:T(8,128)S(1)}, f32[6,64,128]{2,1,0:T(8,128)S(1)}) custom-call(s32[1]{0:T(128)} %bitcast.side, s32[192]{0:T(256)S(1)} %reshape.76.slots, f32[192]{0:T(256)S(1)} %reshape.77.weights, bf16[6,32,128,128]{3,2,1,0:T(8,128)(2,1)S(1)} %get-tuple-element.12.across, bf16[6,128,2048]{2,1,0:T(8,128)(2,1)S(1)} %get-tuple-element.13.halves, ...), custom_call_target="tpu_custom_call" | custom-call | tf_op jit(solution)/shard_map/couple/pallas_call | solution.py:145
  173.5 2.0 collective-permute-start.17
  177.2 45.0 %all_to_all.28 = f32[32,1,128]{2,1,0:T(1,128)S(1)} all-to-all(f32[32,1,128]{2,1,0:T(1,128)S(1)} %get-tuple-element.20), channel_id=1, replica_groups=mesh['job'=2,'chain'=16,'pair'=8,'pno'=2] {'chain','pno'}, dimensions={0} | all-to-all | bytes 32768 | tf_op jit(solution)/shard_map/all_to_all | solution.py:271
  222.3 12.2 %all_to_all.29.copies = f32[8,1,128]{2,1,0:T(1,128)S(1)} all-to-all(f32[8,1,128]{2,1,0:T(1,128)S(1)} %broadcast_in_dim.11), channel_id=1, replica_groups=mesh['job'=2,'chain'=16,'pair'=8,'pno'=2] {'pair'}, dimensions={0} | all-to-all | bytes 8192 | tf_op jit(solution)/shard_map/all_to_all | solution.py:273
  (43 shorter events, 20.5 us)
Async XLA Ops:
  0.6 0.9 copy-start
  1.5 0.7 copy-start.1
  23.6 13.1 %collective-permute-start = (bf16[24,64,128]{2,1,0:T(8,128)(2,1)S(1)}, bf16[24,64,128]{2,1,0:T(8,128)(2,1)S(1)}, u32[]{:S(2)}, u32[]{:S(2)}) collective-permute-start(bf16[24,64,128]{2,1,0:T(8,128)(2,1)S(1)} %bitcast.4), channel_id=1, source_target_pairs={{0,16},{16,32},{32,48},{48,64},{64,80},{80,96},{96,112},{112,128},... | collective-permute-start | bytes 1179656 | tf_op jit(solution)/shard_map/ppermute | solution.py:15
  29.6 13.5 %collective-permute-start.3 = (bf16[24,64,128]{2,1,0:T(8,128)(2,1)S(1)}, bf16[24,64,128]{2,1,0:T(8,128)(2,1)S(1)}, u32[]{:S(2)}, u32[]{:S(2)}) collective-permute-start(bf16[24,64,128]{2,1,0:T(8,128)(2,1)S(1)} %bitcast.5), channel_id=1, source_target_pairs={{16,0},{32,16},{48,32},{64,48},{80,64},{96,80},{112,96},{128,112},... | collective-permute-start | bytes 1179656 | tf_op jit(solution)/shard_map/ppermute | solution.py:15
  33.3 18.3 %collective-permute-start.2 = (bf16[24,64,128]{2,1,0:T(8,128)(2,1)S(1)}, bf16[24,64,128]{2,1,0:T(8,128)(2,1)S(1)}, u32[]{:S(2)}, u32[]{:S(2)}) collective-permute-start(bf16[24,64,128]{2,1,0:T(8,128)(2,1)S(1)} %bitcast.6), channel_id=1, source_target_pairs={{0,2},{2,4},{4,6},{6,8},{8,10},{10,12},{12,14},{14,0},{1,3},{3,5},... | collective-permute-start | bytes 1179656 | tf_op jit(solution)/shard_map/ppermute | solution.py:15
  36.6 17.4 %collective-permute-start.1 = (bf16[24,64,128]{2,1,0:T(8,128)(2,1)S(1)}, bf16[24,64,128]{2,1,0:T(8,128)(2,1)S(1)}, u32[]{:S(2)}, u32[]{:S(2)}) collective-permute-start(bf16[24,64,128]{2,1,0:T(8,128)(2,1)S(1)} %collective-permute-done.refs_0_), channel_id=1, source_target_pairs={{0,2},{2,4},{4,6},{6,8},{8,10},{10,12},{12,14},{14,0},{1,3},{3,5},... | collective-permute-start | bytes 1179656 | tf_op jit(solution)/shard_map/ppermute | solution.py:15
  43.1 10.9 %collective-permute-start.4 = (bf16[24,64,128]{2,1,0:T(8,128)(2,1)S(1)}, bf16[24,64,128]{2,1,0:T(8,128)(2,1)S(1)}, u32[]{:S(2)}, u32[]{:S(2)}) collective-permute-start(bf16[24,64,128]{2,1,0:T(8,128)(2,1)S(1)} %collective-permute-done.3.refs_4_), channel_id=1, source_target_pairs={{0,14},{2,0},{4,2},{6,4},{8,6},{10,8},{12,10},{14,12},{1,15},{3,1}... | collective-permute-start | bytes 1179656 | tf_op jit(solution)/shard_map/ppermute | solution.py:15
  51.5 9.0 %copy-start.2 = (s32[6]{0:T(128)S(1)}, s32[6]{0:T(128)}, u32[]{:S(2)}) copy-start(s32[6]{0:T(128)} %ranks.1) | copy-start | bytes 76
  51.5 10.4 %copy-start.3 = (bf16[6,64,128]{2,1,0:T(8,128)(2,1)S(1)}, bf16[6,64,128]{2,1,0:T(8,128)(2,1)}, u32[]{:S(2)}) copy-start(bf16[6,64,128]{2,1,0:T(8,128)(2,1)} %param.9) | copy-start | bytes 294916
  51.5 10.4 %copy-start.4 = (f32[6,128]{1,0:T(8,128)S(1)}, f32[6,128]{1,0:T(8,128)}, u32[]{:S(2)}) copy-start(f32[6,128]{1,0:T(8,128)} %param.12) | copy-start | bytes 9220
  51.5 10.4 %copy-start.5 = (f32[6]{0:T(128)S(1)}, f32[6]{0:T(128)}, u32[]{:S(2)}) copy-start(f32[6]{0:T(128)} %param.13) | copy-start | bytes 76
  58.6 3.4 %collective-permute-start.5 = (f32[6,64,128]{2,1,0:T(8,128)S(1)}, f32[6,64,128]{2,1,0:T(8,128)S(1)}, u32[]{:S(2)}, u32[]{:S(2)}) collective-permute-start(f32[6,64,128]{2,1,0:T(8,128)S(1)} %get-tuple-element.15), channel_id=1, source_target_pairs={{0,1},{1,0},{2,3},{3,2},{4,5},{5,4},{6,7},{7,6},{8,9},{9,8},{10,11... | collective-permute-start | bytes 589832 | tf_op jit(solution)/shard_map/ppermute | solution.py:15
  81.0 13.8 %collective-permute-start.9 = (bf16[24,64,128]{2,1,0:T(8,128)(2,1)S(1)}, bf16[24,64,128]{2,1,0:T(8,128)(2,1)S(1)}, u32[]{:S(2)}, u32[]{:S(2)}) collective-permute-start(bf16[24,64,128]{2,1,0:T(8,128)(2,1)S(1)} %bitcast.13), channel_id=1, source_target_pairs={{16,0},{32,16},{48,32},{64,48},{80,64},{96,80},{112,96},{128,112},... | collective-permute-start | bytes 1179656 | tf_op jit(solution)/shard_map/ppermute | solution.py:15
  82.3 14.5 %collective-permute-start.6 = (bf16[24,64,128]{2,1,0:T(8,128)(2,1)S(1)}, bf16[24,64,128]{2,1,0:T(8,128)(2,1)S(1)}, u32[]{:S(2)}, u32[]{:S(2)}) collective-permute-start(bf16[24,64,128]{2,1,0:T(8,128)(2,1)S(1)} %bitcast.14), channel_id=1, source_target_pairs={{0,16},{16,32},{32,48},{48,64},{64,80},{80,96},{96,112},{112,128},... | collective-permute-start | bytes 1179656 | tf_op jit(solution)/shard_map/ppermute | solution.py:15
  89.0 13.4 %collective-permute-start.8 = (bf16[24,64,128]{2,1,0:T(8,128)(2,1)S(1)}, bf16[24,64,128]{2,1,0:T(8,128)(2,1)S(1)}, u32[]{:S(2)}, u32[]{:S(2)}) collective-permute-start(bf16[24,64,128]{2,1,0:T(8,128)(2,1)S(1)} %bitcast.15), channel_id=1, source_target_pairs={{0,2},{2,4},{4,6},{6,8},{8,10},{10,12},{12,14},{14,0},{1,3},{3,5},... | collective-permute-start | bytes 1179656 | tf_op jit(solution)/shard_map/ppermute | solution.py:15
  94.8 10.9 %collective-permute-start.10 = (bf16[24,64,128]{2,1,0:T(8,128)(2,1)S(1)}, bf16[24,64,128]{2,1,0:T(8,128)(2,1)S(1)}, u32[]{:S(2)}, u32[]{:S(2)}) collective-permute-start(bf16[24,64,128]{2,1,0:T(8,128)(2,1)S(1)} %collective-permute-done.9.refs_4_), channel_id=1, source_target_pairs={{0,14},{2,0},{4,2},{6,4},{8,6},{10,8},{12,10},{14,12},{1,15},{3,1}... | collective-permute-start | bytes 1179656 | tf_op jit(solution)/shard_map/ppermute | solution.py:15
  96.8 13.1 %collective-permute-start.7 = (bf16[24,64,128]{2,1,0:T(8,128)(2,1)S(1)}, bf16[24,64,128]{2,1,0:T(8,128)(2,1)S(1)}, u32[]{:S(2)}, u32[]{:S(2)}) collective-permute-start(bf16[24,64,128]{2,1,0:T(8,128)(2,1)S(1)} %collective-permute-done.6.refs_0_), channel_id=1, source_target_pairs={{0,2},{2,4},{4,6},{6,8},{8,10},{10,12},{12,14},{14,0},{1,3},{3,5},... | collective-permute-start | bytes 1179656 | tf_op jit(solution)/shard_map/ppermute | solution.py:15
  114.3 3.4 %collective-permute-start.11 = (f32[6,64,128]{2,1,0:T(8,128)S(1)}, f32[6,64,128]{2,1,0:T(8,128)S(1)}, u32[]{:S(2)}, u32[]{:S(2)}) collective-permute-start(f32[6,64,128]{2,1,0:T(8,128)S(1)} %get-tuple-element.17), channel_id=1, source_target_pairs={{0,1},{1,0},{2,3},{3,2},{4,5},{5,4},{6,7},{7,6},{8,9},{9,8},{10,11... | collective-permute-start | bytes 589832 | tf_op jit(solution)/shard_map/ppermute | solution.py:15
  136.1 15.0 %collective-permute-start.12 = (bf16[24,64,128]{2,1,0:T(8,128)(2,1)S(1)}, bf16[24,64,128]{2,1,0:T(8,128)(2,1)S(1)}, u32[]{:S(2)}, u32[]{:S(2)}) collective-permute-start(bf16[24,64,128]{2,1,0:T(8,128)(2,1)S(1)} %bitcast.9), channel_id=1, source_target_pairs={{0,16},{16,32},{32,48},{48,64},{64,80},{80,96},{96,112},{112,128},... | collective-permute-start | bytes 1179656 | tf_op jit(solution)/shard_map/ppermute | solution.py:15
  143.3 14.3 %collective-permute-start.15 = (bf16[24,64,128]{2,1,0:T(8,128)(2,1)S(1)}, bf16[24,64,128]{2,1,0:T(8,128)(2,1)S(1)}, u32[]{:S(2)}, u32[]{:S(2)}) collective-permute-start(bf16[24,64,128]{2,1,0:T(8,128)(2,1)S(1)} %bitcast.10), channel_id=1, source_target_pairs={{16,0},{32,16},{48,32},{64,48},{80,64},{96,80},{112,96},{128,112},... | collective-permute-start | bytes 1179656 | tf_op jit(solution)/shard_map/ppermute | solution.py:15
  144.7 15.1 %collective-permute-start.14 = (bf16[24,64,128]{2,1,0:T(8,128)(2,1)S(1)}, bf16[24,64,128]{2,1,0:T(8,128)(2,1)S(1)}, u32[]{:S(2)}, u32[]{:S(2)}) collective-permute-start(bf16[24,64,128]{2,1,0:T(8,128)(2,1)S(1)} %bitcast.11), channel_id=1, source_target_pairs={{0,2},{2,4},{4,6},{6,8},{8,10},{10,12},{12,14},{14,0},{1,3},{3,5},... | collective-permute-start | bytes 1179656 | tf_op jit(solution)/shard_map/ppermute | solution.py:15
  151.1 15.1 %collective-permute-start.13 = (bf16[24,64,128]{2,1,0:T(8,128)(2,1)S(1)}, bf16[24,64,128]{2,1,0:T(8,128)(2,1)S(1)}, u32[]{:S(2)}, u32[]{:S(2)}) collective-permute-start(bf16[24,64,128]{2,1,0:T(8,128)(2,1)S(1)} %collective-permute-done.12.refs_0_), channel_id=1, source_target_pairs={{0,2},{2,4},{4,6},{6,8},{8,10},{10,12},{12,14},{14,0},{1,3},{3,5},... | collective-permute-start | bytes 1179656 | tf_op jit(solution)/shard_map/ppermute | solution.py:15
  157.6 11.4 %collective-permute-start.16 = (bf16[24,64,128]{2,1,0:T(8,128)(2,1)S(1)}, bf16[24,64,128]{2,1,0:T(8,128)(2,1)S(1)}, u32[]{:S(2)}, u32[]{:S(2)}) collective-permute-start(bf16[24,64,128]{2,1,0:T(8,128)(2,1)S(1)} %collective-permute-done.15.refs_4_), channel_id=1, source_target_pairs={{0,14},{2,0},{4,2},{6,4},{8,6},{10,8},{12,10},{14,12},{1,15},{3,1}... | collective-permute-start | bytes 1179656 | tf_op jit(solution)/shard_map/ppermute | solution.py:15
  173.5 3.4 %collective-permute-start.17 = (f32[6,64,128]{2,1,0:T(8,128)S(1)}, f32[6,64,128]{2,1,0:T(8,128)S(1)}, u32[]{:S(2)}, u32[]{:S(2)}) collective-permute-start(f32[6,64,128]{2,1,0:T(8,128)S(1)} %get-tuple-element.19), channel_id=1, source_target_pairs={{0,1},{1,0},{2,3},{3,2},{4,5},{5,4},{6,7},{7,6},{8,9},{9,8},{10,11... | collective-permute-start | bytes 589832 | tf_op jit(solution)/shard_map/ppermute | solution.py:15

commit v6 on v5

--- a/solution.py
+++ b/solution.py
@@ -15,17 +15,28 @@
     return lax.ppermute(value, axis, pairs)
 
 
+def crossed(value, axis, step, around):
+    count, sides = lax.axis_size(axis), lax.axis_size("pno")
+    pairs = []
+    for i in range(count):
+        for side in range(sides):
+            to = i + (step if side % 2 == 0 else -step)
+            if around or 0 <= to < count:
+                pairs.append((i * sides + side, to % count * sides + side))
+    return lax.ppermute(value, (axis, "pno"), pairs)
+
+
 def spread(piece):
     count = lax.axis_size("pair")
     groups = [list(range(first, count, 2)) for first in range(2)]
     copies = jnp.broadcast_to(piece, (len(groups[0]), *piece.shape))
     near = lax.all_to_all(copies, "pair", 0, 0, tiled=True, axis_index_groups=groups)
     near = near.reshape(-1, *piece.shape[1:])
-    low, high = shifted(near, "chain", 1), shifted(near, "chain", -1)
-    other = shifted(near, "pair", 1, around=True)
-    low_other = shifted(low, "pair", 1, around=True)
-    high_other = shifted(high, "pair", -1, around=True)
-    return low, low_other, near, other, high, high_other
+    fore, back = crossed(near, "chain", 1, False), crossed(near, "chain", -1, False)
+    other = crossed(near, "pair", 1, True)
+    fore_other = crossed(fore, "pair", 1, True)
+    back_other = crossed(back, "pair", -1, True)
+    return fore, fore_other, near, other, back, back_other
 
 
 def live_cells(rank, first, half, width):
@@ -129,8 +140,8 @@
     right_side(0, stacks.at[0])
 
     def step(g, carry):
+        left_side(g - 1, stacks.at[lax.rem(g - 1, 2)])
         right_side(g, stacks.at[lax.rem(g, 2)])
-        left_side(g - 1, stacks.at[lax.rem(g - 1, 2)])
         return carry
 
     lax.fori_loop(1, count, step, 0)
@@ -244,7 +255,8 @@
     within = neighbours % frag
     place = within // count
     turn = (place - lax.axis_index("pair")) % 2
-    piece_no = 2 * (neighbours // frag - chain_pos + 1) + turn
+    offset = neighbours // frag - chain_pos
+    piece_no = 2 * (jnp.where(side == 0, offset, -offset) + 1) + turn
     near = lax.axis_size("pair") // 2
     slots = ((piece_no * near + place // 2) * count + within % count).reshape(-1)
     weights = coupling.reshape(-1)

time: 237 us -> 232 us (0.979)
  waiting for transfers between devices: 43.3 us -> 36.2 us
  blocking collectives: 115 us -> 118 us
    ppermute x0 -> x15, starting transfers between devices: none -> 44.9 us  [crossed(): return lax.ppermute(value, (axis, 'pno'), pairs)]
    ppermute x18 -> x3, starting transfers between devices: 49.9 us -> 5.85 us  [shifted(): return lax.ppermute(value, axis, pairs)]
    ppermute x18 -> x3, waiting for transfers between devices: 43.3 us -> 4.02 us  [shifted(): return lax.ppermute(value, axis, pairs)]
    ppermute x0 -> x15, waiting for transfers between devices: none -> 32.1 us  [crossed(): return lax.ppermute(value, (axis, 'pno'), pairs)]
    all_to_all x1, blocking collectives: 45 us -> 51.3 us  [per_device(): sums = lax.all_to_all(sums, ('chain', 'pno'), 0, 0, tiled=True)]
  transfers between devices with their start and end apart: 18 -> 18, of which waited for: 15 -> 14; matrix products, arithmetic and copies ran while one was open for 1% -> 1% of each run, Pallas kernels for 2% -> 2%
where the time goes in v6:
time: 232 us
  blocking collectives  118 us (51%)
  starting transfers between devices  50.8 us (22%)
  waiting for transfers between devices  36.2 us (16%)
  Pallas kernels  20.2 us (9%)
  local copies, waits for them, and re-layouts  3.4 us (1%)
    all_to_all x3, blocking collectives, spread(): lax.all_to_all(copies, 'pair', 0, 0, tiled=True, axis_index_groups=groups)  55.7 us
    all_to_all x1, blocking collectives, per_device(): sums = lax.all_to_all(sums, ('chain', 'pno'), 0, 0, tiled=True)  51.3 us
    ppermute x15, starting transfers between devices, crossed(): return lax.ppermute(value, (axis, 'pno'), pairs)  44.9 us
    ppermute x15, waiting for transfers between devices, crossed(): return lax.ppermute(value, (axis, 'pno'), pairs)  32.1 us
    pallas_call x3, Pallas kernels, couple(): pl.pallas_call(couple_kernel, in_specs=[scalars] * 3 + [inside] * (2 + le...  12.5 us
    all_to_all x1, blocking collectives, per_device(): sums = lax.all_to_all(sums, 'pair', 0, 0, tiled=True)  10.9 us
    ppermute x3, starting transfers between devices, shifted(): return lax.ppermute(value, axis, pairs)  5.85 us
    pallas_call x1, Pallas kernels, arrange(): pl.pallas_call(arrange_kernel, grid_spec=pltpu.PrefetchScalarGridSpec(num...  5.67 us
  transfers between devices with their start and end apart: 18, of which 14 were waited for; matrix products, arithmetic and copies ran while one was open for 1% of the time, Pallas kernels for 2%

profile of v6, /device:TPU:80, one launch (start us, length us, event | category | flops | bytes accessed | tf_op | source)
XLA Modules:
  0.0 231.5 jit_solution(6660655555665661278)
XLA Ops:
  2.8 20.7 %all_to_all.25 = bf16[4,6,64,128]{3,2,1,0:T(8,128)(2,1)S(1)} all-to-all(bf16[4,6,64,128]{3,2,1,0:T(8,128)(2,1)S(1)} %broadcast_in_dim.8), channel_id=1, replica_groups={{0,4,8,12},{2,6,10,14},{1,5,9,13},{3,7,11,15},{16,20,24,28},{18,22,26,3..., dimensions={0} | all-to-all | bytes 786432 | tf_op jit(solution)/shard_map/all_to_all | solution.py:33
  23.6 6.0 %collective-permute-start = (bf16[24,64,128]{2,1,0:T(8,128)(2,1)S(1)}, bf16[24,64,128]{2,1,0:T(8,128)(2,1)S(1)}, u32[]{:S(2)}, u32[]{:S(2)}) collective-permute-start(bf16[24,64,128]{2,1,0:T(8,128)(2,1)S(1)} %bitcast.4), channel_id=1, source_target_pairs={{0,16},{16,32},{17,1},{32,48},{33,17},{48,64},{49,33},{64,80},{65,... | collective-permute-start | bytes 1179656 | tf_op jit(solution)/shard_map/ppermute | solution.py:26
  33.3 2.0 collective-permute-start.2
  35.3 3.3 %collective-permute-done.refs_0_ = bf16[24,64,128]{2,1,0:T(8,128)(2,1)S(1)} collective-permute-done((bf16[24,64,128]{2,1,0:T(8,128)(2,1)S(1)}, bf16[24,64,128]{2,1,0:T(8,128)(2,1)S(1)}, u32[]{:S(2)}, u32[]{:S(2)}) %collective-permute-start) | collective-permute-done | bytes 393248 | tf_op jit(solution)/shard_map/ppermute | solution.py:26
  38.6 1.9 collective-permute-start.1
  41.4 4.3 %collective-permute-start.4 = (bf16[24,64,128]{2,1,0:T(8,128)(2,1)S(1)}, bf16[24,64,128]{2,1,0:T(8,128)(2,1)S(1)}, u32[]{:S(2)}, u32[]{:S(2)}) collective-permute-start(bf16[24,64,128]{2,1,0:T(8,128)(2,1)S(1)} %collective-permute-done.3.refs_4_), channel_id=1, source_target_pairs={{0,14},{1,3},{2,0},{3,5},{4,2},{5,7},{6,4},{7,9},{8,6},{9,11},{10,... | collective-permute-start | bytes 1179656 | tf_op jit(solution)/shard_map/ppermute | solution.py:26
  46.5 5.7 %arrange.1 = (bf16[6,32,128,128]{3,2,1,0:T(8,128)(2,1)S(1)}, bf16[6,128,2048]{2,1,0:T(8,128)(2,1)S(1)}) custom-call(s32[1]{0:T(128)} %bitcast.side, bf16[24,64,128]{2,1,0:T(8,128)(2,1)S(1)} %bitcast.7, bf16[6,32,128,128]{3,2,1,0:T(8,128)(2,1)} %over.1), custom_call_target="tpu_custom_call" | custom-call | flops 1000000000 | bytes 9437184 | tf_op jit(solution)/shard_map/arrange/pallas_call | solution.py:93
  52.6 4.2 %couple.3 = (f32[6,64,128]{2,1,0:T(8,128)S(1)}, f32[6,64,128]{2,1,0:T(8,128)S(1)}) custom-call(s32[1]{0:T(128)} %bitcast.side, s32[192]{0:T(256)S(1)} %reshape.76.slots, f32[192]{0:T(256)S(1)} %reshape.77.weights, bf16[6,32,128,128]{3,2,1,0:T(8,128)(2,1)S(1)} %get-tuple-element.12.across, bf16[6,128,2048]{2,1,0:T(8,128)(2,1)S(1)} %get-tuple-element.13.halves, ...), custom_call_target="tpu_custom_call" | custom-call | tf_op jit(solution)/shard_map/couple/pallas_call | solution.py:156
  56.8 2.0 collective-permute-start.5
  60.4 17.6 %all_to_all.26 = bf16[4,6,64,128]{3,2,1,0:T(8,128)(2,1)S(1)} all-to-all(bf16[4,6,64,128]{3,2,1,0:T(8,128)(2,1)S(1)} %broadcast_in_dim.9), channel_id=1, replica_groups={{0,4,8,12},{2,6,10,14},{1,5,9,13},{3,7,11,15},{16,20,24,28},{18,22,26,3..., dimensions={0} | all-to-all | bytes 786432 | tf_op jit(solution)/shard_map/all_to_all | solution.py:33
  79.4 7.2 %collective-permute-start.6 = (bf16[24,64,128]{2,1,0:T(8,128)(2,1)S(1)}, bf16[24,64,128]{2,1,0:T(8,128)(2,1)S(1)}, u32[]{:S(2)}, u32[]{:S(2)}) collective-permute-start(bf16[24,64,128]{2,1,0:T(8,128)(2,1)S(1)} %bitcast.14), channel_id=1, source_target_pairs={{0,16},{16,32},{17,1},{32,48},{33,17},{48,64},{49,33},{64,80},{65,... | collective-permute-start | bytes 1179656 | tf_op jit(solution)/shard_map/ppermute | solution.py:26
  86.6 2.7 %collective-permute-start.8 = (bf16[24,64,128]{2,1,0:T(8,128)(2,1)S(1)}, bf16[24,64,128]{2,1,0:T(8,128)(2,1)S(1)}, u32[]{:S(2)}, u32[]{:S(2)}) collective-permute-start(bf16[24,64,128]{2,1,0:T(8,128)(2,1)S(1)} %bitcast.15), channel_id=1, source_target_pairs={{0,2},{1,15},{2,4},{3,1},{4,6},{5,3},{6,8},{7,5},{8,10},{9,7},{10,... | collective-permute-start | bytes 1179656 | tf_op jit(solution)/shard_map/ppermute | solution.py:26
  89.3 2.0 collective-permute-done.9.refs_4_
  91.3 4.2 %collective-permute-start.10 = (bf16[24,64,128]{2,1,0:T(8,128)(2,1)S(1)}, bf16[24,64,128]{2,1,0:T(8,128)(2,1)S(1)}, u32[]{:S(2)}, u32[]{:S(2)}) collective-permute-start(bf16[24,64,128]{2,1,0:T(8,128)(2,1)S(1)} %collective-permute-done.9.refs_4_), channel_id=1, source_target_pairs={{0,14},{1,3},{2,0},{3,5},{4,2},{5,7},{6,4},{7,9},{8,6},{9,11},{10,... | collective-permute-start | bytes 1179656 | tf_op jit(solution)/shard_map/ppermute | solution.py:26
  95.5 2.0 collective-permute-start.7
  97.5 3.3 %collective-permute-done.8.refs_3_ = bf16[24,64,128]{2,1,0:T(8,128)(2,1)S(1)} collective-permute-done((bf16[24,64,128]{2,1,0:T(8,128)(2,1)S(1)}, bf16[24,64,128]{2,1,0:T(8,128)(2,1)S(1)}, u32[]{:S(2)}, u32[]{:S(2)}) %collective-permute-start.8) | collective-permute-done | bytes 393248 | tf_op jit(solution)/shard_map/ppermute | solution.py:26
  100.9 3.5 %collective-permute-done.10.refs_5_ = bf16[24,64,128]{2,1,0:T(8,128)(2,1)S(1)} collective-permute-done((bf16[24,64,128]{2,1,0:T(8,128)(2,1)S(1)}, bf16[24,64,128]{2,1,0:T(8,128)(2,1)S(1)}, u32[]{:S(2)}, u32[]{:S(2)}) %collective-permute-start.10) | collective-permute-done | bytes 393248 | tf_op jit(solution)/shard_map/ppermute | solution.py:26
  104.3 2.1 collective-permute-done.7.refs_1_
  106.5 4.2 %couple.4 = (f32[6,64,128]{2,1,0:T(8,128)S(1)}, f32[6,64,128]{2,1,0:T(8,128)S(1)}) custom-call(s32[1]{0:T(128)} %bitcast.side, s32[192]{0:T(256)S(1)} %reshape.76.slots, f32[192]{0:T(256)S(1)} %reshape.77.weights, bf16[6,32,128,128]{3,2,1,0:T(8,128)(2,1)S(1)} %get-tuple-element.12.across, bf16[6,128,2048]{2,1,0:T(8,128)(2,1)S(1)} %get-tuple-element.13.halves, ...), custom_call_target="tpu_custom_call" | custom-call | tf_op jit(solution)/shard_map/couple/pallas_call | solution.py:156
  110.6 2.0 collective-permute-start.11
  114.3 17.3 %all_to_all.27 = bf16[4,6,64,128]{3,2,1,0:T(8,128)(2,1)S(1)} all-to-all(bf16[4,6,64,128]{3,2,1,0:T(8,128)(2,1)S(1)} %broadcast_in_dim.10), channel_id=1, replica_groups={{0,4,8,12},{2,6,10,14},{1,5,9,13},{3,7,11,15},{16,20,24,28},{18,22,26,3..., dimensions={0} | all-to-all | bytes 786432 | tf_op jit(solution)/shard_map/all_to_all | solution.py:33
  131.6 4.3 %collective-permute-start.12 = (bf16[24,64,128]{2,1,0:T(8,128)(2,1)S(1)}, bf16[24,64,128]{2,1,0:T(8,128)(2,1)S(1)}, u32[]{:S(2)}, u32[]{:S(2)}) collective-permute-start(bf16[24,64,128]{2,1,0:T(8,128)(2,1)S(1)} %bitcast.9), channel_id=1, source_target_pairs={{0,16},{16,32},{17,1},{32,48},{33,17},{48,64},{49,33},{64,80},{65,... | collective-permute-start | bytes 1179656 | tf_op jit(solution)/shard_map/ppermute | solution.py:26
  137.2 2.0 collective-permute-start.14
  139.2 5.7 %collective-permute-done.12.refs_0_ = bf16[24,64,128]{2,1,0:T(8,128)(2,1)S(1)} collective-permute-done((bf16[24,64,128]{2,1,0:T(8,128)(2,1)S(1)}, bf16[24,64,128]{2,1,0:T(8,128)(2,1)S(1)}, u32[]{:S(2)}, u32[]{:S(2)}) %collective-permute-start.12) | collective-permute-done | bytes 393248 | tf_op jit(solution)/shard_map/ppermute | solution.py:26
  144.9 1.9 collective-permute-start.13
  146.9 3.7 %collective-permute-done.15.refs_4_ = bf16[24,64,128]{2,1,0:T(8,128)(2,1)S(1)} collective-permute-done((bf16[24,64,128]{2,1,0:T(8,128)(2,1)S(1)}, bf16[24,64,128]{2,1,0:T(8,128)(2,1)S(1)}, u32[]{:S(2)}, u32[]{:S(2)}) %collective-permute-start.15) | collective-permute-done | bytes 393248 | tf_op jit(solution)/shard_map/ppermute | solution.py:26
  150.6 2.5 %collective-permute-start.16 = (bf16[24,64,128]{2,1,0:T(8,128)(2,1)S(1)}, bf16[24,64,128]{2,1,0:T(8,128)(2,1)S(1)}, u32[]{:S(2)}, u32[]{:S(2)}) collective-permute-start(bf16[24,64,128]{2,1,0:T(8,128)(2,1)S(1)} %collective-permute-done.15.refs_4_), channel_id=1, source_target_pairs={{0,14},{1,3},{2,0},{3,5},{4,2},{5,7},{6,4},{7,9},{8,6},{9,11},{10,... | collective-permute-start | bytes 1179656 | tf_op jit(solution)/shard_map/ppermute | solution.py:26
  153.0 5.7 %collective-permute-done.13.refs_1_ = bf16[24,64,128]{2,1,0:T(8,128)(2,1)S(1)} collective-permute-done((bf16[24,64,128]{2,1,0:T(8,128)(2,1)S(1)}, bf16[24,64,128]{2,1,0:T(8,128)(2,1)S(1)}, u32[]{:S(2)}, u32[]{:S(2)}) %collective-permute-start.13) | collective-permute-done | bytes 393248 | tf_op jit(solution)/shard_map/ppermute | solution.py:26
  160.2 4.2 %couple.5 = (f32[6,64,128]{2,1,0:T(8,128)S(1)}, f32[6,64,128]{2,1,0:T(8,128)S(1)}) custom-call(s32[1]{0:T(128)} %bitcast.side, s32[192]{0:T(256)S(1)} %reshape.76.slots, f32[192]{0:T(256)S(1)} %reshape.77.weights, bf16[6,32,128,128]{3,2,1,0:T(8,128)(2,1)S(1)} %get-tuple-element.12.across, bf16[6,128,2048]{2,1,0:T(8,128)(2,1)S(1)} %get-tuple-element.13.halves, ...), custom_call_target="tpu_custom_call" | custom-call | tf_op jit(solution)/shard_map/couple/pallas_call | solution.py:156
  164.4 2.0 collective-permute-start.17
  168.1 51.3 %all_to_all.28 = f32[32,1,128]{2,1,0:T(1,128)S(1)} all-to-all(f32[32,1,128]{2,1,0:T(1,128)S(1)} %get-tuple-element.20), channel_id=1, replica_groups=mesh['job'=2,'chain'=16,'pair'=8,'pno'=2] {'chain','pno'}, dimensions={0} | all-to-all | bytes 32768 | tf_op jit(solution)/shard_map/all_to_all | solution.py:283
  219.5 10.9 %all_to_all.29.copies = f32[8,1,128]{2,1,0:T(1,128)S(1)} all-to-all(f32[8,1,128]{2,1,0:T(1,128)S(1)} %broadcast_in_dim.11), channel_id=1, replica_groups=mesh['job'=2,'chain'=16,'pair'=8,'pno'=2] {'pair'}, dimensions={0} | all-to-all | bytes 8192 | tf_op jit(solution)/shard_map/all_to_all | solution.py:285
  (43 shorter events, 18.2 us)
Async XLA Ops:
  0.6 0.9 copy-start
  1.5 0.7 copy-start.1
  23.6 15.0 %collective-permute-start = (bf16[24,64,128]{2,1,0:T(8,128)(2,1)S(1)}, bf16[24,64,128]{2,1,0:T(8,128)(2,1)S(1)}, u32[]{:S(2)}, u32[]{:S(2)}) collective-permute-start(bf16[24,64,128]{2,1,0:T(8,128)(2,1)S(1)} %bitcast.4), channel_id=1, source_target_pairs={{0,16},{16,32},{17,1},{32,48},{33,17},{48,64},{49,33},{64,80},{65,... | collective-permute-start | bytes 1179656 | tf_op jit(solution)/shard_map/ppermute | solution.py:26
  29.6 11.8 %collective-permute-start.3 = (bf16[24,64,128]{2,1,0:T(8,128)(2,1)S(1)}, bf16[24,64,128]{2,1,0:T(8,128)(2,1)S(1)}, u32[]{:S(2)}, u32[]{:S(2)}) collective-permute-start(bf16[24,64,128]{2,1,0:T(8,128)(2,1)S(1)} %bitcast.5), channel_id=1, source_target_pairs={{1,17},{16,0},{17,33},{32,16},{33,49},{48,32},{49,65},{64,48},{65,... | collective-permute-start | bytes 1179656 | tf_op jit(solution)/shard_map/ppermute | solution.py:26
  33.3 18.9 %collective-permute-start.2 = (bf16[24,64,128]{2,1,0:T(8,128)(2,1)S(1)}, bf16[24,64,128]{2,1,0:T(8,128)(2,1)S(1)}, u32[]{:S(2)}, u32[]{:S(2)}) collective-permute-start(bf16[24,64,128]{2,1,0:T(8,128)(2,1)S(1)} %bitcast.6), channel_id=1, source_target_pairs={{0,2},{1,15},{2,4},{3,1},{4,6},{5,3},{6,8},{7,5},{8,10},{9,7},{10,... | collective-permute-start | bytes 1179656 | tf_op jit(solution)/shard_map/ppermute | solution.py:26
  38.6 14.0 %collective-permute-start.1 = (bf16[24,64,128]{2,1,0:T(8,128)(2,1)S(1)}, bf16[24,64,128]{2,1,0:T(8,128)(2,1)S(1)}, u32[]{:S(2)}, u32[]{:S(2)}) collective-permute-start(bf16[24,64,128]{2,1,0:T(8,128)(2,1)S(1)} %collective-permute-done.refs_0_), channel_id=1, source_target_pairs={{0,2},{1,15},{2,4},{3,1},{4,6},{5,3},{6,8},{7,5},{8,10},{9,7},{10,... | collective-permute-start | bytes 1179656 | tf_op jit(solution)/shard_map/ppermute | solution.py:26
  41.4 11.2 %collective-permute-start.4 = (bf16[24,64,128]{2,1,0:T(8,128)(2,1)S(1)}, bf16[24,64,128]{2,1,0:T(8,128)(2,1)S(1)}, u32[]{:S(2)}, u32[]{:S(2)}) collective-permute-start(bf16[24,64,128]{2,1,0:T(8,128)(2,1)S(1)} %collective-permute-done.3.refs_4_), channel_id=1, source_target_pairs={{0,14},{1,3},{2,0},{3,5},{4,2},{5,7},{6,4},{7,9},{8,6},{9,11},{10,... | collective-permute-start | bytes 1179656 | tf_op jit(solution)/shard_map/ppermute | solution.py:26
  52.1 6.6 %copy-start.2 = (s32[6]{0:T(128)S(1)}, s32[6]{0:T(128)}, u32[]{:S(2)}) copy-start(s32[6]{0:T(128)} %ranks.1) | copy-start | bytes 76
  52.1 8.0 %copy-start.3 = (bf16[6,64,128]{2,1,0:T(8,128)(2,1)S(1)}, bf16[6,64,128]{2,1,0:T(8,128)(2,1)}, u32[]{:S(2)}) copy-start(bf16[6,64,128]{2,1,0:T(8,128)(2,1)} %param.9) | copy-start | bytes 294916
  52.2 8.0 %copy-start.4 = (f32[6,128]{1,0:T(8,128)S(1)}, f32[6,128]{1,0:T(8,128)}, u32[]{:S(2)}) copy-start(f32[6,128]{1,0:T(8,128)} %param.12) | copy-start | bytes 9220
  52.2 8.0 %copy-start.5 = (f32[6]{0:T(128)S(1)}, f32[6]{0:T(128)}, u32[]{:S(2)}) copy-start(f32[6]{0:T(128)} %param.13) | copy-start | bytes 76
  56.8 3.4 %collective-permute-start.5 = (f32[6,64,128]{2,1,0:T(8,128)S(1)}, f32[6,64,128]{2,1,0:T(8,128)S(1)}, u32[]{:S(2)}, u32[]{:S(2)}) collective-permute-start(f32[6,64,128]{2,1,0:T(8,128)S(1)} %get-tuple-element.15), channel_id=1, source_target_pairs={{0,1},{1,0},{2,3},{3,2},{4,5},{5,4},{6,7},{7,6},{8,9},{9,8},{10,11... | collective-permute-start | bytes 589832 | tf_op jit(solution)/shard_map/ppermute | solution.py:15
  78.1 13.2 %collective-permute-start.9 = (bf16[24,64,128]{2,1,0:T(8,128)(2,1)S(1)}, bf16[24,64,128]{2,1,0:T(8,128)(2,1)S(1)}, u32[]{:S(2)}, u32[]{:S(2)}) collective-permute-start(bf16[24,64,128]{2,1,0:T(8,128)(2,1)S(1)} %bitcast.13), channel_id=1, source_target_pairs={{1,17},{16,0},{17,33},{32,16},{33,49},{48,32},{49,65},{64,48},{65,... | collective-permute-start | bytes 1179656 | tf_op jit(solution)/shard_map/ppermute | solution.py:26
  79.4 16.1 %collective-permute-start.6 = (bf16[24,64,128]{2,1,0:T(8,128)(2,1)S(1)}, bf16[24,64,128]{2,1,0:T(8,128)(2,1)S(1)}, u32[]{:S(2)}, u32[]{:S(2)}) collective-permute-start(bf16[24,64,128]{2,1,0:T(8,128)(2,1)S(1)} %bitcast.14), channel_id=1, source_target_pairs={{0,16},{16,32},{17,1},{32,48},{33,17},{48,64},{49,33},{64,80},{65,... | collective-permute-start | bytes 1179656 | tf_op jit(solution)/shard_map/ppermute | solution.py:26
  86.6 14.2 %collective-permute-start.8 = (bf16[24,64,128]{2,1,0:T(8,128)(2,1)S(1)}, bf16[24,64,128]{2,1,0:T(8,128)(2,1)S(1)}, u32[]{:S(2)}, u32[]{:S(2)}) collective-permute-start(bf16[24,64,128]{2,1,0:T(8,128)(2,1)S(1)} %bitcast.15), channel_id=1, source_target_pairs={{0,2},{1,15},{2,4},{3,1},{4,6},{5,3},{6,8},{7,5},{8,10},{9,7},{10,... | collective-permute-start | bytes 1179656 | tf_op jit(solution)/shard_map/ppermute | solution.py:26
  91.3 13.0 %collective-permute-start.10 = (bf16[24,64,128]{2,1,0:T(8,128)(2,1)S(1)}, bf16[24,64,128]{2,1,0:T(8,128)(2,1)S(1)}, u32[]{:S(2)}, u32[]{:S(2)}) collective-permute-start(bf16[24,64,128]{2,1,0:T(8,128)(2,1)S(1)} %collective-permute-done.9.refs_4_), channel_id=1, source_target_pairs={{0,14},{1,3},{2,0},{3,5},{4,2},{5,7},{6,4},{7,9},{8,6},{9,11},{10,... | collective-permute-start | bytes 1179656 | tf_op jit(solution)/shard_map/ppermute | solution.py:26
  95.5 10.9 %collective-permute-start.7 = (bf16[24,64,128]{2,1,0:T(8,128)(2,1)S(1)}, bf16[24,64,128]{2,1,0:T(8,128)(2,1)S(1)}, u32[]{:S(2)}, u32[]{:S(2)}) collective-permute-start(bf16[24,64,128]{2,1,0:T(8,128)(2,1)S(1)} %collective-permute-done.6.refs_0_), channel_id=1, source_target_pairs={{0,2},{1,15},{2,4},{3,1},{4,6},{5,3},{6,8},{7,5},{8,10},{9,7},{10,... | collective-permute-start | bytes 1179656 | tf_op jit(solution)/shard_map/ppermute | solution.py:26
  110.6 3.4 %collective-permute-start.11 = (f32[6,64,128]{2,1,0:T(8,128)S(1)}, f32[6,64,128]{2,1,0:T(8,128)S(1)}, u32[]{:S(2)}, u32[]{:S(2)}) collective-permute-start(f32[6,64,128]{2,1,0:T(8,128)S(1)} %get-tuple-element.17), channel_id=1, source_target_pairs={{0,1},{1,0},{2,3},{3,2},{4,5},{5,4},{6,7},{7,6},{8,9},{9,8},{10,11... | collective-permute-start | bytes 589832 | tf_op jit(solution)/shard_map/ppermute | solution.py:15
  131.6 13.3 %collective-permute-start.12 = (bf16[24,64,128]{2,1,0:T(8,128)(2,1)S(1)}, bf16[24,64,128]{2,1,0:T(8,128)(2,1)S(1)}, u32[]{:S(2)}, u32[]{:S(2)}) collective-permute-start(bf16[24,64,128]{2,1,0:T(8,128)(2,1)S(1)} %bitcast.9), channel_id=1, source_target_pairs={{0,16},{16,32},{17,1},{32,48},{33,17},{48,64},{49,33},{64,80},{65,... | collective-permute-start | bytes 1179656 | tf_op jit(solution)/shard_map/ppermute | solution.py:26
  135.9 14.6 %collective-permute-start.15 = (bf16[24,64,128]{2,1,0:T(8,128)(2,1)S(1)}, bf16[24,64,128]{2,1,0:T(8,128)(2,1)S(1)}, u32[]{:S(2)}, u32[]{:S(2)}) collective-permute-start(bf16[24,64,128]{2,1,0:T(8,128)(2,1)S(1)} %bitcast.10), channel_id=1, source_target_pairs={{1,17},{16,0},{17,33},{32,16},{33,49},{48,32},{49,65},{64,48},{65,... | collective-permute-start | bytes 1179656 | tf_op jit(solution)/shard_map/ppermute | solution.py:26
  137.2 15.8 %collective-permute-start.14 = (bf16[24,64,128]{2,1,0:T(8,128)(2,1)S(1)}, bf16[24,64,128]{2,1,0:T(8,128)(2,1)S(1)}, u32[]{:S(2)}, u32[]{:S(2)}) collective-permute-start(bf16[24,64,128]{2,1,0:T(8,128)(2,1)S(1)} %bitcast.11), channel_id=1, source_target_pairs={{0,2},{1,15},{2,4},{3,1},{4,6},{5,3},{6,8},{7,5},{8,10},{9,7},{10,... | collective-permute-start | bytes 1179656 | tf_op jit(solution)/shard_map/ppermute | solution.py:26
  144.9 13.8 %collective-permute-start.13 = (bf16[24,64,128]{2,1,0:T(8,128)(2,1)S(1)}, bf16[24,64,128]{2,1,0:T(8,128)(2,1)S(1)}, u32[]{:S(2)}, u32[]{:S(2)}) collective-permute-start(bf16[24,64,128]{2,1,0:T(8,128)(2,1)S(1)} %collective-permute-done.12.refs_0_), channel_id=1, source_target_pairs={{0,2},{1,15},{2,4},{3,1},{4,6},{5,3},{6,8},{7,5},{8,10},{9,7},{10,... | collective-permute-start | bytes 1179656 | tf_op jit(solution)/shard_map/ppermute | solution.py:26
  150.6 9.7 %collective-permute-start.16 = (bf16[24,64,128]{2,1,0:T(8,128)(2,1)S(1)}, bf16[24,64,128]{2,1,0:T(8,128)(2,1)S(1)}, u32[]{:S(2)}, u32[]{:S(2)}) collective-permute-start(bf16[24,64,128]{2,1,0:T(8,128)(2,1)S(1)} %collective-permute-done.15.refs_4_), channel_id=1, source_target_pairs={{0,14},{1,3},{2,0},{3,5},{4,2},{5,7},{6,4},{7,9},{8,6},{9,11},{10,... | collective-permute-start | bytes 1179656 | tf_op jit(solution)/shard_map/ppermute | solution.py:26
  164.4 3.4 %collective-permute-start.17 = (f32[6,64,128]{2,1,0:T(8,128)S(1)}, f32[6,64,128]{2,1,0:T(8,128)S(1)}, u32[]{:S(2)}, u32[]{:S(2)}) collective-permute-start(f32[6,64,128]{2,1,0:T(8,128)S(1)} %get-tuple-element.19), channel_id=1, source_target_pairs={{0,1},{1,0},{2,3},{3,2},{4,5},{5,4},{6,7},{7,6},{8,9},{9,8},{10,11... | collective-permute-start | bytes 589832 | tf_op jit(solution)/shard_map/ppermute | solution.py:15

commit v7 on v6

--- a/solution.py
+++ b/solution.py
@@ -29,9 +29,7 @@
 def spread(piece):
     count = lax.axis_size("pair")
     groups = [list(range(first, count, 2)) for first in range(2)]
-    copies = jnp.broadcast_to(piece, (len(groups[0]), *piece.shape))
-    near = lax.all_to_all(copies, "pair", 0, 0, tiled=True, axis_index_groups=groups)
-    near = near.reshape(-1, *piece.shape[1:])
+    near = lax.all_gather(piece, "pair", axis=0, tiled=True, axis_index_groups=groups)
     fore, back = crossed(near, "chain", 1, False), crossed(near, "chain", -1, False)
     other = crossed(near, "pair", 1, True)
     fore_other = crossed(fore, "pair", 1, True)

time: 232 us -> 224 us (0.966)
  blocking collectives: 118 us -> 111 us
  starting transfers between devices: 50.8 us -> 53.7 us
  waiting for transfers between devices: 36.2 us -> 33.5 us
    all_to_all x3 -> x0, blocking collectives: 55.7 us -> none  [spread(): lax.all_to_all(copies, 'pair', 0, 0, tiled=True, axis_index_groups=groups)]
    all_gather x0 -> x3, blocking collectives: none -> 50.9 us  [spread(): lax.all_gather(piece, 'pair', axis=0, tiled=True, axis_index_groups=groups)]
    all_to_all x1, blocking collectives: 51.3 us -> 48.7 us  [per_device(): sums = lax.all_to_all(sums, ('chain', 'pno'), 0, 0, tiled=True)]
  transfers between devices with their start and end apart: 18 -> 18, of which waited for: 14 -> 15; matrix products, arithmetic and copies ran while one was open for 1% -> 1% of each run, Pallas kernels for 2% -> 3%
where the time goes in v7:
time: 224 us
  blocking collectives  111 us (50%)
  starting transfers between devices  53.7 us (24%)
  waiting for transfers between devices  33.5 us (15%)
  Pallas kernels  20.3 us (9%)
  local copies, waits for them, and re-layouts  2.5 us (1%)
    all_gather x3, blocking collectives, spread(): lax.all_gather(piece, 'pair', axis=0, tiled=True, axis_index_groups=groups)  50.9 us
    all_to_all x1, blocking collectives, per_device(): sums = lax.all_to_all(sums, ('chain', 'pno'), 0, 0, tiled=True)  48.7 us
    ppermute x15, starting transfers between devices, crossed(): return lax.ppermute(value, (axis, 'pno'), pairs)  47 us
    ppermute x15, waiting for transfers between devices, crossed(): return lax.ppermute(value, (axis, 'pno'), pairs)  29.9 us
    pallas_call x3, Pallas kernels, couple(): pl.pallas_call(couple_kernel, in_specs=[scalars] * 3 + [inside] * (2 + le...  12.6 us
    all_to_all x1, blocking collectives, per_device(): sums = lax.all_to_all(sums, 'pair', 0, 0, tiled=True)  11.6 us
    ppermute x3, starting transfers between devices, shifted(): return lax.ppermute(value, axis, pairs)  6.69 us
    pallas_call x1, Pallas kernels, arrange(): pl.pallas_call(arrange_kernel, grid_spec=pltpu.PrefetchScalarGridSpec(num...  5.68 us
  transfers between devices with their start and end apart: 18, of which 15 were waited for; matrix products, arithmetic and copies ran while one was open for 1% of the time, Pallas kernels for 3%

profile of v7, /device:TPU:80, one launch (start us, length us, event | category | flops | bytes accessed | tf_op | source)
XLA Modules:
  0.0 223.6 jit_solution(10586585940148035739)
XLA Ops:
  2.8 18.6 %all_gather.9.after.refs_2_ = bf16[24,64,128]{2,1,0:T(8,128)(2,1)S(1)} all-gather(bf16[6,64,128]{2,1,0:T(8,128)(2,1)S(1)} %masked.1.own), channel_id=1, replica_groups={{0,4,8,12},{2,6,10,14},{1,5,9,13},{3,7,11,15},{16,20,24,28},{18,22,26,3..., dimensions={0}, use_global_device_ids=true | all-gather | bytes 491520 | tf_op jit(solution)/shard_map/all_gather | solution.py:32
  21.4 6.0 %collective-permute-start = (bf16[24,64,128]{2,1,0:T(8,128)(2,1)S(1)}, bf16[24,64,128]{2,1,0:T(8,128)(2,1)S(1)}, u32[]{:S(2)}, u32[]{:S(2)}) collective-permute-start(bf16[24,64,128]{2,1,0:T(8,128)(2,1)S(1)} %all_gather.9.after.refs_2_), channel_id=1, source_target_pairs={{0,16},{16,32},{17,1},{32,48},{33,17},{48,64},{49,33},{64,80},{65,... | collective-permute-start | bytes 1179656 | tf_op jit(solution)/shard_map/ppermute | solution.py:26
  28.8 2.2 collective-permute-start.2
  32.6 1.6 collective-permute-done.refs_0_
  34.2 2.4 %collective-permute-start.1 = (bf16[24,64,128]{2,1,0:T(8,128)(2,1)S(1)}, bf16[24,64,128]{2,1,0:T(8,128)(2,1)S(1)}, u32[]{:S(2)}, u32[]{:S(2)}) collective-permute-start(bf16[24,64,128]{2,1,0:T(8,128)(2,1)S(1)} %collective-permute-done.refs_0_), channel_id=1, source_target_pairs={{0,2},{1,15},{2,4},{3,1},{4,6},{5,3},{6,8},{7,5},{8,10},{9,7},{10,... | collective-permute-start | bytes 1179656 | tf_op jit(solution)/shard_map/ppermute | solution.py:26
  36.6 2.6 %collective-permute-done.3.refs_4_ = bf16[24,64,128]{2,1,0:T(8,128)(2,1)S(1)} collective-permute-done((bf16[24,64,128]{2,1,0:T(8,128)(2,1)S(1)}, bf16[24,64,128]{2,1,0:T(8,128)(2,1)S(1)}, u32[]{:S(2)}, u32[]{:S(2)}) %collective-permute-start.3) | collective-permute-done | bytes 393248 | tf_op jit(solution)/shard_map/ppermute | solution.py:26
  39.2 2.1 collective-permute-start.4
  41.3 5.7 %arrange.1 = (bf16[6,32,128,128]{3,2,1,0:T(8,128)(2,1)S(1)}, bf16[6,128,2048]{2,1,0:T(8,128)(2,1)S(1)}) custom-call(s32[1]{0:T(128)} %bitcast.side, bf16[24,64,128]{2,1,0:T(8,128)(2,1)S(1)} %all_gather.9.after.refs_2_, bf16[6,32,128,128]{3,2,1,0:T(8,128)(2,1)} %over.1), custom_call_target="tpu_custom_call" | custom-call | flops 1000000000 | bytes 9437184 | tf_op jit(solution)/shard_map/arrange/pallas_call | solution.py:91
  48.9 4.2 %couple.3 = (f32[6,64,128]{2,1,0:T(8,128)S(1)}, f32[6,64,128]{2,1,0:T(8,128)S(1)}) custom-call(s32[1]{0:T(128)} %bitcast.side, s32[192]{0:T(256)S(1)} %reshape.67.slots, f32[192]{0:T(256)S(1)} %reshape.68.weights, bf16[6,32,128,128]{3,2,1,0:T(8,128)(2,1)S(1)} %get-tuple-element.12.across, bf16[6,128,2048]{2,1,0:T(8,128)(2,1)S(1)} %get-tuple-element.13.halves, ...), custom_call_target="tpu_custom_call" | custom-call | tf_op jit(solution)/shard_map/couple/pallas_call | solution.py:154
  53.1 2.0 collective-permute-start.5
  55.2 1.3 collective-permute-done.5
  56.7 16.4 %all_gather.10.refs_2_ = bf16[24,64,128]{2,1,0:T(8,128)(2,1)S(1)} all-gather(bf16[6,64,128]{2,1,0:T(8,128)(2,1)S(1)} %get-tuple-element.24), channel_id=1, replica_groups={{0,4,8,12},{2,6,10,14},{1,5,9,13},{3,7,11,15},{16,20,24,28},{18,22,26,3..., dimensions={0}, use_global_device_ids=true | all-gather | bytes 491520 | tf_op jit(solution)/shard_map/all_gather | solution.py:32
  74.4 6.7 %collective-permute-start.6 = (bf16[24,64,128]{2,1,0:T(8,128)(2,1)S(1)}, bf16[24,64,128]{2,1,0:T(8,128)(2,1)S(1)}, u32[]{:S(2)}, u32[]{:S(2)}) collective-permute-start(bf16[24,64,128]{2,1,0:T(8,128)(2,1)S(1)} %all_gather.10.refs_2_), channel_id=1, source_target_pairs={{0,16},{16,32},{17,1},{32,48},{33,17},{48,64},{49,33},{64,80},{65,... | collective-permute-start | bytes 1179656 | tf_op jit(solution)/shard_map/ppermute | solution.py:26
  81.1 2.0 collective-permute-start.8
  83.1 3.9 %collective-permute-done.9.refs_4_ = bf16[24,64,128]{2,1,0:T(8,128)(2,1)S(1)} collective-permute-done((bf16[24,64,128]{2,1,0:T(8,128)(2,1)S(1)}, bf16[24,64,128]{2,1,0:T(8,128)(2,1)S(1)}, u32[]{:S(2)}, u32[]{:S(2)}) %collective-permute-start.9) | collective-permute-done | bytes 393248 | tf_op jit(solution)/shard_map/ppermute | solution.py:26
  87.0 1.9 collective-permute-start.10
  88.9 4.0 %collective-permute-start.7 = (bf16[24,64,128]{2,1,0:T(8,128)(2,1)S(1)}, bf16[24,64,128]{2,1,0:T(8,128)(2,1)S(1)}, u32[]{:S(2)}, u32[]{:S(2)}) collective-permute-start(bf16[24,64,128]{2,1,0:T(8,128)(2,1)S(1)} %collective-permute-done.6.refs_0_), channel_id=1, source_target_pairs={{0,2},{1,15},{2,4},{3,1},{4,6},{5,3},{6,8},{7,5},{8,10},{9,7},{10,... | collective-permute-start | bytes 1179656 | tf_op jit(solution)/shard_map/ppermute | solution.py:26
  93.6 6.0 %collective-permute-done.10.refs_5_ = bf16[24,64,128]{2,1,0:T(8,128)(2,1)S(1)} collective-permute-done((bf16[24,64,128]{2,1,0:T(8,128)(2,1)S(1)}, bf16[24,64,128]{2,1,0:T(8,128)(2,1)S(1)}, u32[]{:S(2)}, u32[]{:S(2)}) %collective-permute-start.10) | collective-permute-done | bytes 393248 | tf_op jit(solution)/shard_map/ppermute | solution.py:26
  99.8 4.2 %couple.4 = (f32[6,64,128]{2,1,0:T(8,128)S(1)}, f32[6,64,128]{2,1,0:T(8,128)S(1)}) custom-call(s32[1]{0:T(128)} %bitcast.side, s32[192]{0:T(256)S(1)} %reshape.67.slots, f32[192]{0:T(256)S(1)} %reshape.68.weights, bf16[6,32,128,128]{3,2,1,0:T(8,128)(2,1)S(1)} %get-tuple-element.12.across, bf16[6,128,2048]{2,1,0:T(8,128)(2,1)S(1)} %get-tuple-element.13.halves, ...), custom_call_target="tpu_custom_call" | custom-call | tf_op jit(solution)/shard_map/couple/pallas_call | solution.py:154
  104.1 2.8 %collective-permute-start.11 = (f32[6,64,128]{2,1,0:T(8,128)S(1)}, f32[6,64,128]{2,1,0:T(8,128)S(1)}, u32[]{:S(2)}, u32[]{:S(2)}) collective-permute-start(f32[6,64,128]{2,1,0:T(8,128)S(1)} %get-tuple-element.17), channel_id=1, source_target_pairs={{0,1},{1,0},{2,3},{3,2},{4,5},{5,4},{6,7},{7,6},{8,9},{9,8},{10,11... | collective-permute-start | bytes 589832 | tf_op jit(solution)/shard_map/ppermute | solution.py:15
  108.1 15.8 %all_gather.11.refs_2_ = bf16[24,64,128]{2,1,0:T(8,128)(2,1)S(1)} all-gather(bf16[6,64,128]{2,1,0:T(8,128)(2,1)S(1)} %get-tuple-element.22), channel_id=1, replica_groups={{0,4,8,12},{2,6,10,14},{1,5,9,13},{3,7,11,15},{16,20,24,28},{18,22,26,3..., dimensions={0}, use_global_device_ids=true | all-gather | bytes 491520 | tf_op jit(solution)/shard_map/all_gather | solution.py:32
  123.9 8.9 %collective-permute-start.12 = (bf16[24,64,128]{2,1,0:T(8,128)(2,1)S(1)}, bf16[24,64,128]{2,1,0:T(8,128)(2,1)S(1)}, u32[]{:S(2)}, u32[]{:S(2)}) collective-permute-start(bf16[24,64,128]{2,1,0:T(8,128)(2,1)S(1)} %all_gather.11.refs_2_), channel_id=1, source_target_pairs={{0,16},{16,32},{17,1},{32,48},{33,17},{48,64},{49,33},{64,80},{65,... | collective-permute-start | bytes 1179656 | tf_op jit(solution)/shard_map/ppermute | solution.py:26
  134.2 2.0 collective-permute-start.14
  136.1 4.2 %collective-permute-done.12.refs_0_ = bf16[24,64,128]{2,1,0:T(8,128)(2,1)S(1)} collective-permute-done((bf16[24,64,128]{2,1,0:T(8,128)(2,1)S(1)}, bf16[24,64,128]{2,1,0:T(8,128)(2,1)S(1)}, u32[]{:S(2)}, u32[]{:S(2)}) %collective-permute-start.12) | collective-permute-done | bytes 393248 | tf_op jit(solution)/shard_map/ppermute | solution.py:26
  140.3 1.9 collective-permute-start.13
  142.3 2.2 collective-permute-done.15.refs_4_
  144.5 3.0 %collective-permute-start.16 = (bf16[24,64,128]{2,1,0:T(8,128)(2,1)S(1)}, bf16[24,64,128]{2,1,0:T(8,128)(2,1)S(1)}, u32[]{:S(2)}, u32[]{:S(2)}) collective-permute-start(bf16[24,64,128]{2,1,0:T(8,128)(2,1)S(1)} %collective-permute-done.15.refs_4_), channel_id=1, source_target_pairs={{0,14},{1,3},{2,0},{3,5},{4,2},{5,7},{6,4},{7,9},{8,6},{9,11},{10,... | collective-permute-start | bytes 1179656 | tf_op jit(solution)/shard_map/ppermute | solution.py:26
  147.5 6.0 %collective-permute-done.13.refs_1_ = bf16[24,64,128]{2,1,0:T(8,128)(2,1)S(1)} collective-permute-done((bf16[24,64,128]{2,1,0:T(8,128)(2,1)S(1)}, bf16[24,64,128]{2,1,0:T(8,128)(2,1)S(1)}, u32[]{:S(2)}, u32[]{:S(2)}) %collective-permute-start.13) | collective-permute-done | bytes 393248 | tf_op jit(solution)/shard_map/ppermute | solution.py:26
  154.2 4.2 %couple.5 = (f32[6,64,128]{2,1,0:T(8,128)S(1)}, f32[6,64,128]{2,1,0:T(8,128)S(1)}) custom-call(s32[1]{0:T(128)} %bitcast.side, s32[192]{0:T(256)S(1)} %reshape.67.slots, f32[192]{0:T(256)S(1)} %reshape.68.weights, bf16[6,32,128,128]{3,2,1,0:T(8,128)(2,1)S(1)} %get-tuple-element.12.across, bf16[6,128,2048]{2,1,0:T(8,128)(2,1)S(1)} %get-tuple-element.13.halves, ...), custom_call_target="tpu_custom_call" | custom-call | tf_op jit(solution)/shard_map/couple/pallas_call | solution.py:154
  158.4 2.0 collective-permute-start.17
  162.1 48.7 %all_to_all.10 = f32[32,1,128]{2,1,0:T(1,128)S(1)} all-to-all(f32[32,1,128]{2,1,0:T(1,128)S(1)} %get-tuple-element.20), channel_id=1, replica_groups=mesh['job'=2,'chain'=16,'pair'=8,'pno'=2] {'chain','pno'}, dimensions={0} | all-to-all | bytes 32768 | tf_op jit(solution)/shard_map/all_to_all | solution.py:281
  210.9 11.6 %all_to_all.11.copies = f32[8,1,128]{2,1,0:T(1,128)S(1)} all-to-all(f32[8,1,128]{2,1,0:T(1,128)S(1)} %broadcast_in_dim.2), channel_id=1, replica_groups=mesh['job'=2,'chain'=16,'pair'=8,'pno'=2] {'pair'}, dimensions={0} | all-to-all | bytes 8192 | tf_op jit(solution)/shard_map/all_to_all | solution.py:283
  (40 shorter events, 15.5 us)
Async XLA Ops:
  0.6 46.5 %copy-start.2 = (s32[6]{0:T(128)S(1)}, s32[6]{0:T(128)}, u32[]{:S(2)}) copy-start(s32[6]{0:T(128)} %ranks.1) | copy-start | bytes 76
  0.6 46.4 %copy-start.4 = (f32[6,128]{1,0:T(8,128)S(1)}, f32[6,128]{1,0:T(8,128)}, u32[]{:S(2)}) copy-start(f32[6,128]{1,0:T(8,128)} %param.12) | copy-start | bytes 9220
  0.7 0.9 copy-start
  1.6 0.7 copy-start.1
  21.4 12.8 %collective-permute-start = (bf16[24,64,128]{2,1,0:T(8,128)(2,1)S(1)}, bf16[24,64,128]{2,1,0:T(8,128)(2,1)S(1)}, u32[]{:S(2)}, u32[]{:S(2)}) collective-permute-start(bf16[24,64,128]{2,1,0:T(8,128)(2,1)S(1)} %all_gather.9.after.refs_2_), channel_id=1, source_target_pairs={{0,16},{16,32},{17,1},{32,48},{33,17},{48,64},{49,33},{64,80},{65,... | collective-permute-start | bytes 1179656 | tf_op jit(solution)/shard_map/ppermute | solution.py:26
  27.5 11.8 %collective-permute-start.3 = (bf16[24,64,128]{2,1,0:T(8,128)(2,1)S(1)}, bf16[24,64,128]{2,1,0:T(8,128)(2,1)S(1)}, u32[]{:S(2)}, u32[]{:S(2)}) collective-permute-start(bf16[24,64,128]{2,1,0:T(8,128)(2,1)S(1)} %all_gather.9.after.refs_2_), channel_id=1, source_target_pairs={{1,17},{16,0},{17,33},{32,16},{33,49},{48,32},{49,65},{64,48},{65,... | collective-permute-start | bytes 1179656 | tf_op jit(solution)/shard_map/ppermute | solution.py:26
  28.8 18.4 %collective-permute-start.2 = (bf16[24,64,128]{2,1,0:T(8,128)(2,1)S(1)}, bf16[24,64,128]{2,1,0:T(8,128)(2,1)S(1)}, u32[]{:S(2)}, u32[]{:S(2)}) collective-permute-start(bf16[24,64,128]{2,1,0:T(8,128)(2,1)S(1)} %all_gather.9.after.refs_2_), channel_id=1, source_target_pairs={{0,2},{1,15},{2,4},{3,1},{4,6},{5,3},{6,8},{7,5},{8,10},{9,7},{10,... | collective-permute-start | bytes 1179656 | tf_op jit(solution)/shard_map/ppermute | solution.py:26
  34.2 13.9 %collective-permute-start.1 = (bf16[24,64,128]{2,1,0:T(8,128)(2,1)S(1)}, bf16[24,64,128]{2,1,0:T(8,128)(2,1)S(1)}, u32[]{:S(2)}, u32[]{:S(2)}) collective-permute-start(bf16[24,64,128]{2,1,0:T(8,128)(2,1)S(1)} %collective-permute-done.refs_0_), channel_id=1, source_target_pairs={{0,2},{1,15},{2,4},{3,1},{4,6},{5,3},{6,8},{7,5},{8,10},{9,7},{10,... | collective-permute-start | bytes 1179656 | tf_op jit(solution)/shard_map/ppermute | solution.py:26
  39.2 9.7 %collective-permute-start.4 = (bf16[24,64,128]{2,1,0:T(8,128)(2,1)S(1)}, bf16[24,64,128]{2,1,0:T(8,128)(2,1)S(1)}, u32[]{:S(2)}, u32[]{:S(2)}) collective-permute-start(bf16[24,64,128]{2,1,0:T(8,128)(2,1)S(1)} %collective-permute-done.3.refs_4_), channel_id=1, source_target_pairs={{0,14},{1,3},{2,0},{3,5},{4,2},{5,7},{6,4},{7,9},{8,6},{9,11},{10,... | collective-permute-start | bytes 1179656 | tf_op jit(solution)/shard_map/ppermute | solution.py:26
  47.0 9.5 %copy-start.3 = (bf16[6,64,128]{2,1,0:T(8,128)(2,1)S(1)}, bf16[6,64,128]{2,1,0:T(8,128)(2,1)}, u32[]{:S(2)}) copy-start(bf16[6,64,128]{2,1,0:T(8,128)(2,1)} %param.9) | copy-start | bytes 294916
  47.0 9.4 %copy-start.5 = (f32[6]{0:T(128)S(1)}, f32[6]{0:T(128)}, u32[]{:S(2)}) copy-start(f32[6]{0:T(128)} %param.13) | copy-start | bytes 76
  53.1 3.4 %collective-permute-start.5 = (f32[6,64,128]{2,1,0:T(8,128)S(1)}, f32[6,64,128]{2,1,0:T(8,128)S(1)}, u32[]{:S(2)}, u32[]{:S(2)}) collective-permute-start(f32[6,64,128]{2,1,0:T(8,128)S(1)} %get-tuple-element.15), channel_id=1, source_target_pairs={{0,1},{1,0},{2,3},{3,2},{4,5},{5,4},{6,7},{7,6},{8,9},{9,8},{10,11... | collective-permute-start | bytes 589832 | tf_op jit(solution)/shard_map/ppermute | solution.py:15
  73.1 13.8 %collective-permute-start.9 = (bf16[24,64,128]{2,1,0:T(8,128)(2,1)S(1)}, bf16[24,64,128]{2,1,0:T(8,128)(2,1)S(1)}, u32[]{:S(2)}, u32[]{:S(2)}) collective-permute-start(bf16[24,64,128]{2,1,0:T(8,128)(2,1)S(1)} %all_gather.10.refs_2_), channel_id=1, source_target_pairs={{1,17},{16,0},{17,33},{32,16},{33,49},{48,32},{49,65},{64,48},{65,... | collective-permute-start | bytes 1179656 | tf_op jit(solution)/shard_map/ppermute | solution.py:26
  74.4 14.5 %collective-permute-start.6 = (bf16[24,64,128]{2,1,0:T(8,128)(2,1)S(1)}, bf16[24,64,128]{2,1,0:T(8,128)(2,1)S(1)}, u32[]{:S(2)}, u32[]{:S(2)}) collective-permute-start(bf16[24,64,128]{2,1,0:T(8,128)(2,1)S(1)} %all_gather.10.refs_2_), channel_id=1, source_target_pairs={{0,16},{16,32},{17,1},{32,48},{33,17},{48,64},{49,33},{64,80},{65,... | collective-permute-start | bytes 1179656 | tf_op jit(solution)/shard_map/ppermute | solution.py:26
  81.1 12.5 %collective-permute-start.8 = (bf16[24,64,128]{2,1,0:T(8,128)(2,1)S(1)}, bf16[24,64,128]{2,1,0:T(8,128)(2,1)S(1)}, u32[]{:S(2)}, u32[]{:S(2)}) collective-permute-start(bf16[24,64,128]{2,1,0:T(8,128)(2,1)S(1)} %all_gather.10.refs_2_), channel_id=1, source_target_pairs={{0,2},{1,15},{2,4},{3,1},{4,6},{5,3},{6,8},{7,5},{8,10},{9,7},{10,... | collective-permute-start | bytes 1179656 | tf_op jit(solution)/shard_map/ppermute | solution.py:26
  87.0 12.6 %collective-permute-start.10 = (bf16[24,64,128]{2,1,0:T(8,128)(2,1)S(1)}, bf16[24,64,128]{2,1,0:T(8,128)(2,1)S(1)}, u32[]{:S(2)}, u32[]{:S(2)}) collective-permute-start(bf16[24,64,128]{2,1,0:T(8,128)(2,1)S(1)} %collective-permute-done.9.refs_4_), channel_id=1, source_target_pairs={{0,14},{1,3},{2,0},{3,5},{4,2},{5,7},{6,4},{7,9},{8,6},{9,11},{10,... | collective-permute-start | bytes 1179656 | tf_op jit(solution)/shard_map/ppermute | solution.py:26
  88.9 10.9 %collective-permute-start.7 = (bf16[24,64,128]{2,1,0:T(8,128)(2,1)S(1)}, bf16[24,64,128]{2,1,0:T(8,128)(2,1)S(1)}, u32[]{:S(2)}, u32[]{:S(2)}) collective-permute-start(bf16[24,64,128]{2,1,0:T(8,128)(2,1)S(1)} %collective-permute-done.6.refs_0_), channel_id=1, source_target_pairs={{0,2},{1,15},{2,4},{3,1},{4,6},{5,3},{6,8},{7,5},{8,10},{9,7},{10,... | collective-permute-start | bytes 1179656 | tf_op jit(solution)/shard_map/ppermute | solution.py:26
  104.1 3.8 %collective-permute-start.11 = (f32[6,64,128]{2,1,0:T(8,128)S(1)}, f32[6,64,128]{2,1,0:T(8,128)S(1)}, u32[]{:S(2)}, u32[]{:S(2)}) collective-permute-start(f32[6,64,128]{2,1,0:T(8,128)S(1)} %get-tuple-element.17), channel_id=1, source_target_pairs={{0,1},{1,0},{2,3},{3,2},{4,5},{5,4},{6,7},{7,6},{8,9},{9,8},{10,11... | collective-permute-start | bytes 589832 | tf_op jit(solution)/shard_map/ppermute | solution.py:15
  123.9 16.4 %collective-permute-start.12 = (bf16[24,64,128]{2,1,0:T(8,128)(2,1)S(1)}, bf16[24,64,128]{2,1,0:T(8,128)(2,1)S(1)}, u32[]{:S(2)}, u32[]{:S(2)}) collective-permute-start(bf16[24,64,128]{2,1,0:T(8,128)(2,1)S(1)} %all_gather.11.refs_2_), channel_id=1, source_target_pairs={{0,16},{16,32},{17,1},{32,48},{33,17},{48,64},{49,33},{64,80},{65,... | collective-permute-start | bytes 1179656 | tf_op jit(solution)/shard_map/ppermute | solution.py:26
  132.9 11.6 %collective-permute-start.15 = (bf16[24,64,128]{2,1,0:T(8,128)(2,1)S(1)}, bf16[24,64,128]{2,1,0:T(8,128)(2,1)S(1)}, u32[]{:S(2)}, u32[]{:S(2)}) collective-permute-start(bf16[24,64,128]{2,1,0:T(8,128)(2,1)S(1)} %all_gather.11.refs_2_), channel_id=1, source_target_pairs={{1,17},{16,0},{17,33},{32,16},{33,49},{48,32},{49,65},{64,48},{65,... | collective-permute-start | bytes 1179656 | tf_op jit(solution)/shard_map/ppermute | solution.py:26
  134.2 13.3 %collective-permute-start.14 = (bf16[24,64,128]{2,1,0:T(8,128)(2,1)S(1)}, bf16[24,64,128]{2,1,0:T(8,128)(2,1)S(1)}, u32[]{:S(2)}, u32[]{:S(2)}) collective-permute-start(bf16[24,64,128]{2,1,0:T(8,128)(2,1)S(1)} %all_gather.11.refs_2_), channel_id=1, source_target_pairs={{0,2},{1,15},{2,4},{3,1},{4,6},{5,3},{6,8},{7,5},{8,10},{9,7},{10,... | collective-permute-start | bytes 1179656 | tf_op jit(solution)/shard_map/ppermute | solution.py:26
  140.3 13.2 %collective-permute-start.13 = (bf16[24,64,128]{2,1,0:T(8,128)(2,1)S(1)}, bf16[24,64,128]{2,1,0:T(8,128)(2,1)S(1)}, u32[]{:S(2)}, u32[]{:S(2)}) collective-permute-start(bf16[24,64,128]{2,1,0:T(8,128)(2,1)S(1)} %collective-permute-done.12.refs_0_), channel_id=1, source_target_pairs={{0,2},{1,15},{2,4},{3,1},{4,6},{5,3},{6,8},{7,5},{8,10},{9,7},{10,... | collective-permute-start | bytes 1179656 | tf_op jit(solution)/shard_map/ppermute | solution.py:26
  144.5 9.7 %collective-permute-start.16 = (bf16[24,64,128]{2,1,0:T(8,128)(2,1)S(1)}, bf16[24,64,128]{2,1,0:T(8,128)(2,1)S(1)}, u32[]{:S(2)}, u32[]{:S(2)}) collective-permute-start(bf16[24,64,128]{2,1,0:T(8,128)(2,1)S(1)} %collective-permute-done.15.refs_4_), channel_id=1, source_target_pairs={{0,14},{1,3},{2,0},{3,5},{4,2},{5,7},{6,4},{7,9},{8,6},{9,11},{10,... | collective-permute-start | bytes 1179656 | tf_op jit(solution)/shard_map/ppermute | solution.py:26
  158.4 3.4 %collective-permute-start.17 = (f32[6,64,128]{2,1,0:T(8,128)S(1)}, f32[6,64,128]{2,1,0:T(8,128)S(1)}, u32[]{:S(2)}, u32[]{:S(2)}) collective-permute-start(f32[6,64,128]{2,1,0:T(8,128)S(1)} %get-tuple-element.19), channel_id=1, source_target_pairs={{0,1},{1,0},{2,3},{3,2},{4,5},{5,4},{6,7},{7,6},{8,9},{9,8},{10,11... | collective-permute-start | bytes 589832 | tf_op jit(solution)/shard_map/ppermute | solution.py:15
